TPU v7x, 8 devices: a whole 2x2x1 slice. The times are simulated.
8 devices in a mesh: dp: 1 (over z), tp: 2 (over y), sp: 4 (over x, core).
Axes of the slice: x: 2, y: 2, z: 1, core: 2. Of those that a mesh axis runs over, the one named last changes fastest.
Arguments:
- hidden: bfloat16 [128, 8192], P('dp')
- seq_lens: int32 [128], P('dp')
- rope_cos: float32 [128, 64], P('dp')
- rope_sin: float32 [128, 64], P('dp')
- k_cache: bfloat16 [128, 256, 8, 128], P('dp', 'sp', 'tp')
- v_cache: bfloat16 [128, 256, 8, 128], P('dp', 'sp', 'tp')
- norm_gain: bfloat16 [8192], replicated
- w_qkv: bfloat16 [8192, 8, 1280], P(None, 'tp')
- b_qkv: bfloat16 [8, 1280], P('tp')
- sink_logits: float32 [64], P('tp')
- w_o: bfloat16 [8192, 8192], P('tp')
- b_o: bfloat16 [8192], replicated
Outputs:
- output 1: bfloat16 [128, 8192], P('dp')
- output 2: bfloat16 [128, 256, 8, 128], P('dp', 'sp', 'tp')
- output 3: bfloat16 [128, 256, 8, 128], P('dp', 'sp', 'tp')
All inputs are finite; a program needn't handle non-finite values.
Results may differ from a plain program's by a relative error of at most 0.00537465.
Values sent between devices are 32-bit elements.
A program may use at most 1 GiB of HBM per device.

v0:
```python
import jax
import jax.numpy as jnp
from jax import lax
from jax.sharding import PartitionSpec as P

NORM_EPS = 1e-5


def rotate_half(heads_in, cos_part, sin_part):
    half_dim = heads_in.shape[-1] // 2
    first_half = heads_in[..., :half_dim]
    second_half = heads_in[..., half_dim:]
    return jnp.concatenate([first_half * cos_part - second_half * sin_part, second_half * cos_part + first_half * sin_part], axis=-1)


def local_partials(hidden, seq_lens, rope_cos, rope_sin, k_cache, v_cache, norm_gain, w_qkv, b_qkv, sink_logits):
    num_seqs, ctx_local, kv_local, head_dim = k_cache.shape
    group_size = w_qkv.shape[2] // head_dim - 2
    x_wide = hidden.astype(jnp.float32)
    inv_rms = lax.rsqrt(jnp.mean(x_wide * x_wide, axis=-1, keepdims=True) + NORM_EPS)
    normed = (x_wide * inv_rms * norm_gain.astype(jnp.float32)).astype(jnp.bfloat16)
    qkv_all = jnp.einsum("bd,dkc->bkc", normed, w_qkv, preferred_element_type=jnp.float32) + b_qkv.astype(jnp.float32)
    qkv_all = qkv_all.reshape(num_seqs, kv_local, group_size + 2, head_dim)
    q_rot = rotate_half(qkv_all[:, :, :group_size], rope_cos[:, None, None, :], rope_sin[:, None, None, :]).astype(jnp.bfloat16)
    k_new = rotate_half(qkv_all[:, :, group_size], rope_cos[:, None, :], rope_sin[:, None, :]).astype(jnp.bfloat16)
    v_new = qkv_all[:, :, group_size + 1].astype(jnp.bfloat16)
    positions = lax.axis_index("sp") * ctx_local + jnp.arange(ctx_local)
    is_new = (positions[None, :] == seq_lens[:, None])[:, :, None, None]
    k_out = jnp.where(is_new, k_new[:, None], k_cache)
    v_out = jnp.where(is_new, v_new[:, None], v_cache)
    logits = jnp.einsum("bkgd,blkd->bkgl", q_rot, k_out, preferred_element_type=jnp.float32) * head_dim ** -0.5
    logits = jnp.where((positions[None, :] <= seq_lens[:, None])[:, None, None, :], logits, -jnp.inf)
    row_max = jnp.maximum(jnp.max(logits, axis=-1), sink_logits.reshape(kv_local, group_size))
    weights = jnp.exp(logits - row_max[..., None])
    row_sum = jnp.sum(weights, axis=-1)
    weighted = jnp.einsum("bkgl,blkd->bkgd", weights.astype(jnp.bfloat16), v_out, preferred_element_type=jnp.float32)
    packed = jnp.concatenate([row_max[..., None], row_sum[..., None], weighted], axis=-1)
    return packed.reshape(num_seqs, kv_local * group_size, head_dim + 2), k_out, v_out


def combine_shards(parts_in, sinks_here):
    shard_max = parts_in[..., 0]
    shard_sum = parts_in[..., 1]
    top_max = jnp.max(shard_max, axis=1)
    rescale = jnp.exp(shard_max - top_max[:, None])
    denominator = jnp.sum(shard_sum * rescale, axis=1) + jnp.exp(sinks_here[None, :] - top_max)
    combined = jnp.sum(parts_in[..., 2:] * rescale[..., None], axis=1)
    return combined / denominator[..., None]


def solution(mesh):
    sp_size = mesh.shape["sp"]
    cache_spec = P("dp", "sp", "tp", None)

    def block_step(hidden, seq_lens, rope_cos, rope_sin, k_cache, v_cache, norm_gain, w_qkv, b_qkv, sink_logits, w_o, b_o):
        packed, k_out, v_out = local_partials(hidden, seq_lens, rope_cos, rope_sin, k_cache, v_cache, norm_gain, w_qkv, b_qkv, sink_logits)
        num_seqs, local_heads, width = packed.shape
        head_dim = width - 2
        head_share = local_heads // sp_size
        received = lax.all_to_all(packed.reshape(num_seqs, sp_size, head_share, width), "sp", 1, 1, tiled=True)
        sp_index = lax.axis_index("sp")
        sinks_here = sink_logits.reshape(sp_size, head_share)[sp_index]
        combined = combine_shards(received, sinks_here)
        w_rows = w_o.reshape(sp_size, head_share * head_dim, w_o.shape[1])[sp_index]
        partial_out = jnp.dot(combined.astype(jnp.bfloat16).reshape(num_seqs, head_share * head_dim), w_rows, preferred_element_type=jnp.float32)
        summed = lax.psum(partial_out, ("tp", "sp"))
        out_hidden = (hidden.astype(jnp.float32) + summed + b_o.astype(jnp.float32)).astype(jnp.bfloat16)
        return out_hidden, k_out, v_out

    return jax.shard_map(block_step, mesh=mesh, in_specs=(P("dp", None), P("dp"), P("dp", None), P("dp", None), cache_spec, cache_spec, P(None), P(None, "tp", None), P("tp", None), P("tp"), P("tp", None), P(None)), out_specs=(P("dp", None), cache_spec, cache_spec), check_vma=False)
```

profile of v0, /device:TPU:0, one launch (start us, length us, event | category | flops | bytes accessed | tf_op | source)
XLA Modules:
  0.0 241.8 jit_solution(5349184670628195311)
XLA Ops:
  7.2 0.9 convert_element_type.50
  8.8 2.1 fusion.9
  10.9 45.6 %fusion.14 = f32[128,4,1280]{2,0,1:T(8,128)} fusion(bf16[8192,4,1280]{2,1,0:T(4,128)(2,1)} %param.19, bf16[128,8192]{1,0:T(8,128)(2,1)S(1)} %copy-done.1, f32[8192]{0:T(1024)S(1)} %convert_element_type.50, f32[128]{0:T(128)S(1)} %add_rsqrt_fusion, f32[4,1280]{1,0:T(4,128)S(1)} %convert_element_type.52), kind=kOutput, calls=%fused_computation.20 | convolution fusion | flops 10742267904 | bytes 88658432 | tf_op jit(solution)/shard_map/bd,dkc->bkc/dot_general | solution.py:22
  56.4 2.1 copy.96
  58.7 1.5 fusion.41
  61.6 0.9 subtract_convert_fusion.1
  63.3 3.1 %copy.118 = f32[128,4,8,64]{3,2,1,0:T(8,128)S(1)} copy(f32[128,4,8,64]{0,3,2,1:T(8,128)} %get-tuple-element.6) | data formatting | bytes 2097152
  66.4 2.8 %copy.119 = f32[128,4,8,64]{3,2,1,0:T(8,128)} copy(f32[128,4,8,64]{0,3,2,1:T(8,128)S(1)} %copy-done.4) | data formatting | bytes 2097152
  69.9 0.7 broadcast_compare_fusion.1
  70.7 3.5 %subtract_convert_fusion = (bf16[128,4,8,64]{3,2,1,0:T(8,128)(2,1)}, bf16[128,4,8,64]{3,2,1,0:T(8,128)(2,1)}) fusion(f32[128,4,8,64]{3,2,1,0:T(8,128)} %copy.119, f32[128,4,8,64]{3,2,1,0:T(8,128)S(1)} %copy.118, f32[128,64]{1,0:T(8,128)S(1)} %copy-done.6, f32[128,64]{1,0:T(8,128)S(1)} %copy-done.7), kind=kLoop, calls=%fused_computation.27 | loop fusion | flops 2097152 | bytes 3211264 | tf_op jit(solution)/shard_map/convert.3
  74.2 13.5 %broadcast_select_fusion.1 = (bf16[128,64,4,128]{3,2,1,0:T(4,128)(2,1)S(1)}, bf16[128,64,4,128]{3,2,1,0:T(4,128)(2,1)S(1)}) fusion(bf16[128,64,4,128]{3,2,1,0:T(4,128)(2,1)} %param.16, pred[128,64]{1,0:T(8,128)(4,1)S(1)} %get-tuple-element.12, bf16[128,4,128]{2,1,0:T(4,128)(2,1)S(1)} %copy.101, bf16[128,64,4,128]{3,2,1,0:T(4,128)(2,1)} %param.17, ...), kind=kLoop, calls=%fused_computation.10 | loop fusion | flops 8388608 | bytes 33824768 | tf_op jit(solution)/shard_map/jit(_where)/select_n | solution.py:29
  87.8 7.9 %fusion.22 = (f32[128,4,8]{2,1,0:T(4,128)S(1)}, f32[128,4,8,64]{3,2,1,0:T(8,128)S(1)}) fusion(pred[128,64]{1,0:T(8,128)(4,1)S(1)} %get-tuple-element.11, bf16[128,64,4,128]{3,2,1,0:T(4,128)(2,1)S(1)} %get-tuple-element.9, bf16[128,4,8,64]{3,2,1,0:T(8,128)(2,1)} %get-tuple-element.4, bf16[128,4,8,64]{3,2,1,0:T(8,128)(2,1)} %get-tuple-element.3), kind=kOutput, calls=%fused_computation.30 | convolution fusion | flops 69988352 | bytes 10510336 | tf_op jit(solution)/shard_map/bkgd,blkd->bkgl/dot_general | solution.py:31
  95.7 1.4 fusion.24
  97.1 3.7 %fusion.5 = f32[128,4,8,128]{3,2,1,0:T(8,128)} fusion(bf16[128,64,4,128]{3,2,1,0:T(4,128)(2,1)S(1)} %get-tuple-element.10, f32[128,4,8,64]{3,2,1,0:T(8,128)S(1)} %get-tuple-element.14, f32[128,4,8]{2,1,0:T(4,128)S(1)} %bitcast.43, pred[128,64]{1,0:T(8,128)(4,1)S(1)} %get-tuple-element.11), kind=kOutput, calls=%fused_computation.5 | convolution fusion | flops 68157440 | bytes 11558912 | tf_op jit(solution)/shard_map/bkgl,blkd->bkgd/dot_general | solution.py:36
  100.8 3.1 %copy.109 = f32[128,4,8,1]{3,2,1,0:T(8,128)S(1)} copy(f32[128,4,8,1]{2,1,0,3:T(4,128)S(1)} %bitcast.41) | data formatting | bytes 32768 | tf_op jit(solution)/shard_map/broadcast_in_dim | solution.py:37
  103.9 4.4 %copy.104 = f32[128,4,8,1]{3,2,1,0:T(8,128)} copy(f32[128,4,8,1]{2,1,0,3:T(4,128)S(1)} %bitcast.39) | data formatting | bytes 32768 | tf_op jit(solution)/shard_map/reduce_max | solution.py:33
  108.3 2.0 broadcast_maximum_fusion
  110.5 4.2 %pad_maximum_fusion = f32[128,4,8,130]{3,2,1,0:T(8,128)} fusion(f32[128,4,8,128]{3,2,1,0:T(8,128)S(1)} %copy-done.5, f32[128,4,8,1]{3,2,1,0:T(8,128)S(1)} %copy.109, f32[128,4,8,1]{3,2,1,0:T(8,128)S(1)} %broadcast_maximum_fusion), kind=kLoop, calls=%fused_computation.19 | loop fusion | flops 1064960 | bytes 4259840 | tf_op jit(solution)/shard_map/concatenate | solution.py:37
  114.7 4.9 %copy.110 = f32[128,4,8,130]{0,2,3,1:T(8,128)} copy(f32[128,4,8,130]{3,2,1,0:T(8,128)} %pad_maximum_fusion) | data formatting | bytes 4259840 | tf_op jit(solution)/shard_map/concatenate | solution.py:37
  119.6 4.6 %all-to-all-start = ((f32[128,4,8,130]{0,2,3,1:T(8,128)}), f32[128,4,8,130]{0,2,3,1:T(8,128)S(1)}, u32[]{:S(2)}, u32[]{:S(2)}) async-start(f32[128,4,8,130]{0,2,3,1:T(8,128)} %copy.110), calls=%async_computation | async-start | bytes 4259840 | tf_op jit(solution)/shard_map/all_to_all | solution.py:60
  124.2 25.8 %all-to-all-done = f32[128,4,8,130]{0,2,3,1:T(8,128)S(1)} async-done(((f32[128,4,8,130]{0,2,3,1:T(8,128)}), f32[128,4,8,130]{0,2,3,1:T(8,128)S(1)}, u32[]{:S(2)}, u32[]{:S(2)}) %all-to-all-start) | async-done | bytes 2129952 | tf_op jit(solution)/shard_map/all_to_all | solution.py:60
  150.4 10.2 %fusion.2 = f32[128,8192]{1,0:T(8,128)} fusion(bf16[128,1024]{0,1:T(8,128)(2,1)S(1)} %bitcast.40, bf16[4,1024,8192]{2,1,0:T(8,128)(2,1)} %bitcast.11, s32[]{:T(128)S(6)} %select_n.18), kind=kOutput, calls=%fused_computation.2 | convolution fusion | flops 2147483648 | bytes 21233668 | tf_op jit(solution)/shard_map/dot_general | solution.py:65
  161.4 69.6 %all-reduce.2.cloned.1.call-done = f32[128,8192]{1,0:T(8,128)} async-done(((f32[128,8192]{1,0:T(8,128)}), f32[128,8192]{1,0:T(8,128)}) %all-reduce.2.cloned.1.call-update) | async-done | bytes 4194320 | tf_op jit(solution)/shard_map/psum | solution.py:66
  231.0 4.0 %fusion.13 = bf16[128,8192]{1,0:T(8,128)(2,1)} fusion(f32[128,8192]{1,0:T(8,128)} %all-reduce.2.cloned.1.call-done, bf16[128,8192]{1,0:T(8,128)(2,1)S(1)} %copy-done.2, f32[8192]{0:T(1024)S(1)} %convert_element_type.57), kind=kLoop, calls=%fused_computation.18 | loop fusion | flops 4194304 | bytes 8421376 | tf_op jit(solution)/shard_map/convert_element_type | solution.py:67
  (50 shorter events, 5.0 us)
Async XLA Ops:
  7.2 3.7 %copy-start.1 = (bf16[128,8192]{1,0:T(8,128)(2,1)S(1)}, bf16[128,8192]{1,0:T(8,128)(2,1)}, u32[]{:S(2)}) copy-start(bf16[128,8192]{1,0:T(8,128)(2,1)} %param.12) | copy-start | bytes 6291460
  58.6 1.5 copy-start.8
  58.7 2.2 copy-start.9
  61.6 4.8 %copy-start.4 = (f32[128,4,8,64]{0,3,2,1:T(8,128)S(1)}, f32[128,4,8,64]{0,3,2,1:T(8,128)}, u32[]{:S(2)}) copy-start(f32[128,4,8,64]{0,3,2,1:T(8,128)} %get-tuple-element.5) | copy-start | bytes 3145732
  66.4 2.9 %copy-start.12 = (f32[32]{0:T(128)S(1)}, f32[32]{0:T(128)}, u32[]{:S(2)}) copy-start(f32[32]{0:T(128)} %param.21) | copy-start | bytes 388
  66.4 4.3 %copy-start.6 = (f32[128,64]{1,0:T(8,128)S(1)}, f32[128,64]{1,0:T(8,128)}, u32[]{:S(2)}) copy-start(f32[128,64]{1,0:T(8,128)} %copy.100) | copy-start | bytes 98308
  66.4 4.3 %copy-start.7 = (f32[128,64]{1,0:T(8,128)S(1)}, f32[128,64]{1,0:T(8,128)}, u32[]{:S(2)}) copy-start(f32[128,64]{1,0:T(8,128)} %copy.98) | copy-start | bytes 98308
  87.7 8.0 %copy-start = (bf16[128,64,4,128]{3,2,1,0:T(4,128)(2,1)}, bf16[128,64,4,128]{3,2,1,0:T(4,128)(2,1)S(1)}, u32[]{:S(2)}) copy-start(bf16[128,64,4,128]{3,2,1,0:T(4,128)(2,1)S(1)} %get-tuple-element.9) | copy-start | bytes 25165828
  87.7 9.4 %copy-start.3 = (bf16[128,64,4,128]{3,2,1,0:T(4,128)(2,1)}, bf16[128,64,4,128]{3,2,1,0:T(4,128)(2,1)S(1)}, u32[]{:S(2)}) copy-start(bf16[128,64,4,128]{3,2,1,0:T(4,128)(2,1)S(1)} %get-tuple-element.10) | copy-start | bytes 25165828
  87.8 7.9 %copy-start.10 = (f32[4,8]{1,0:T(4,128)S(1)}, f32[4,8]{1,0:T(4,128)}, u32[]{:S(2)}) copy-start(f32[4,8]{1,0:T(4,128)} %max.22) | copy-start | bytes 388
  108.3 2.2 copy-start.5
  119.6 30.4 %all-to-all-start = ((f32[128,4,8,130]{0,2,3,1:T(8,128)}), f32[128,4,8,130]{0,2,3,1:T(8,128)S(1)}, u32[]{:S(2)}, u32[]{:S(2)}) async-start(f32[128,4,8,130]{0,2,3,1:T(8,128)} %copy.110), calls=%async_computation | async-start | bytes 4259840 | tf_op jit(solution)/shard_map/all_to_all | solution.py:60
  124.2 106.7 %all-reduce.2.cloned.1.call-start = ((), (), s32[]{:S(2)}) async-start(), calls=%async_computation.1 | async-start | bytes 8388608 | tf_op jit(solution)/shard_map/psum | solution.py:66
  160.6 0.7 copy-start.11
  160.6 70.3 %copy-start.2 = (bf16[128,8192]{1,0:T(8,128)(2,1)S(1)}, bf16[128,8192]{1,0:T(8,128)(2,1)}, u32[]{:S(2)}) copy-start(bf16[128,8192]{1,0:T(8,128)(2,1)} %param.12) | copy-start | bytes 6291460
Sparse Core Ops, SparseCore 0:
  160.8 70.1 all-reduce.1
where the time goes:
time: 242 us
  waiting for transfers between devices  95.4 us (39%)
  matrix products  67.4 us (28%)
  other arithmetic  34.8 us (14%)
  local copies, waits for them, and re-layouts  25.2 us (10%)
  between operations  14.3 us (6%)
  starting transfers between devices  4.62 us (2%)
    psum x1, waiting for transfers between devices, block_step(): summed = lax.psum(partial_out, ('tp', 'sp'))  69.6 us
    dot_general x1, matrix products, local_partials(): jnp.einsum('bd,dkc->bkc', normed, w_qkv, preferred_element_type=jnp.float32)  45.6 us
    all_to_all x1, waiting for transfers between devices, block_step(): lax.all_to_all(packed.reshape(num_seqs, sp_size, head_share, width), 'sp'...  25.8 us
    select_n x1, other arithmetic, local_partials(): k_out = jnp.where(is_new, k_new[:, None], k_cache)  13.5 us
    dot_general x1, matrix products, block_step(): jnp.dot(combined.astype(jnp.bfloat16).reshape(num_seqs, head_share * head...  10.2 us
    unnamed x31, local copies, waits for them, and re-layouts  8.24 us
    dot_general x1, matrix products, local_partials(): jnp.einsum('bkgd,blkd->bkgl', q_rot, k_out, preferred_element_type=jnp.fl...  7.91 us
    concatenate x1, local copies, waits for them, and re-layouts, local_partials(): jnp.concatenate([row_max[..., None], row_sum[..., None], weighted], axis=-1)  4.93 us
  transfers between devices with their start and end apart: 2, of which 2 were waited for; matrix products, arithmetic and copies ran while one was open for 0% of the time, Pallas kernels for 0%

commit v1 on v0

v1 whole, which is shorter than its diff:
```python
import functools

import jax
import jax.numpy as jnp
from jax import lax
from jax.experimental import pallas as pl
from jax.experimental.pallas import tpu as pltpu
from jax.sharding import PartitionSpec as P

NORM_EPS = 1e-5
F32 = jnp.float32
BF16 = jnp.bfloat16
MESH = pl.DeviceIdType.MESH


def sp_place():
    sp = lax.axis_index("sp")
    return lax.div(sp, 2), lax.rem(sp, 2)


def remote(src, dst, send_sem, recv_sem, where):
    return pltpu.make_async_remote_copy(src_ref=src, dst_ref=dst, send_sem=send_sem, recv_sem=recv_sem, device_id=where, device_id_type=MESH)


QKV_ROWS = 512
QKV_SLOTS = 3


def qkv_kernel(x_ref, gain_ref, cos_ref, sin_ref, bias_ref, w_ref, out_ref, normed, heads, acc_q, acc_e, wq_buf, we_buf, wq_sem, we_sem, send_sem, recv_sem, out_sem):
    chip, core = sp_place()
    partner = {"sp": 2 * chip + (1 - core)}
    num_seqs, depth = x_ref.shape
    head_dim = acc_e.shape[2]
    q_cols = acc_q.shape[2]
    kv_local = acc_q.shape[0]
    per_core = q_cols // head_dim
    group = 2 * per_core
    steps = depth // QKV_ROWS

    def fetch(step, slot):
        rows = pl.ds(step * QKV_ROWS, QKV_ROWS)
        cq = pltpu.make_async_copy(w_ref.at[rows, :, pl.ds(pl.multiple_of(core * q_cols, 128), q_cols)], wq_buf.at[slot], wq_sem.at[slot])
        ce = pltpu.make_async_copy(w_ref.at[rows, :, pl.ds(pl.multiple_of((group + core) * head_dim, 128), head_dim)], we_buf.at[slot], we_sem.at[slot])
        return cq, ce

    for s in range(QKV_SLOTS - 1):
        for c in fetch(s, s):
            c.start()

    barrier = pltpu.get_barrier_semaphore()
    pl.semaphore_signal(barrier, inc=1, device_id=partner, device_id_type=MESH)

    def norm_rows(r, _):
        rows = pl.ds(pl.multiple_of(r * 16, 16), 16)
        xw = x_ref[rows, :].astype(F32)
        inv = lax.rsqrt(jnp.mean(xw * xw, axis=-1, keepdims=True) + NORM_EPS)
        normed[rows, :] = (xw * inv * gain_ref[...].astype(F32)).astype(BF16)
        return 0

    lax.fori_loop(0, num_seqs // 16, norm_rows, 0)
    acc_q[...] = jnp.zeros_like(acc_q)
    acc_e[...] = jnp.zeros_like(acc_e)

    def step_fn(step, _):
        slot = lax.rem(step, QKV_SLOTS)
        for c in fetch(step, slot):
            c.wait()

        @pl.when(step + QKV_SLOTS - 1 < steps)
        def _():
            for c in fetch(step + QKV_SLOTS - 1, lax.rem(step + QKV_SLOTS - 1, QKV_SLOTS)):
                c.start()

        h = normed[:, pl.ds(pl.multiple_of(step * QKV_ROWS, 128), QKV_ROWS)]
        wq = jnp.swapaxes(wq_buf[slot], 0, 1)
        we = jnp.swapaxes(we_buf[slot], 0, 1)
        for k in range(kv_local):
            acc_q[k] += jnp.dot(h, wq[k], preferred_element_type=F32)
            acc_e[k] += jnp.dot(h, we[k], preferred_element_type=F32)
        return 0

    lax.fori_loop(0, steps, step_fn, 0)

    cos_t = cos_ref[...].T
    sin_t = sin_ref[...].T
    cos2 = jnp.concatenate([cos_t, cos_t], axis=1)
    sin2 = jnp.concatenate([-sin_t, sin_t], axis=1)
    is_key = core == 0
    cos_e = jnp.where(is_key, cos2, jnp.ones_like(cos2))
    sin_e = jnp.where(is_key, sin2, jnp.zeros_like(sin2))

    def rotate(v, c, s):
        r = v * c + pltpu.roll(v, head_dim // 2, 1) * s
        return r.astype(BF16).astype(F32)

    pl.semaphore_wait(barrier, 1)
    copies = []
    for k in range(kv_local):
        bias_q = bias_ref[k : k + 1, pl.ds(pl.multiple_of(core * q_cols, 128), q_cols)].astype(F32)
        for g in range(per_core):
            cols = slice(g * head_dim, (g + 1) * head_dim)
            heads[k * group + per_core * core + g] = rotate(acc_q[k, :, cols] + bias_q[:, cols], cos2, sin2)
        part = heads.at[pl.ds(k * group + per_core * core, per_core)]
        copies.append(remote(part, part, send_sem.at[k], recv_sem.at[k], partner))
        copies[-1].start()
    for k in range(kv_local):
        bias_e = bias_ref[k : k + 1, pl.ds(pl.multiple_of((group + core) * head_dim, 128), head_dim)].astype(F32)
        heads[kv_local * group + kv_local * core + k] = rotate(acc_e[k] + bias_e, cos_e, sin_e)
    part = heads.at[pl.ds(kv_local * group + kv_local * core, kv_local)]
    copies.append(remote(part, part, send_sem.at[kv_local], recv_sem.at[kv_local], partner))
    copies[-1].start()
    for c in copies:
        c.wait()
    done = pltpu.make_async_copy(heads, out_ref, out_sem)
    done.start()
    done.wait()


def qkv_heads(hidden, rope_cos, rope_sin, norm_gain, w_qkv, b_qkv, head_dim):
    num_seqs, depth = hidden.shape
    kv_local = w_qkv.shape[1]
    per_core = (w_qkv.shape[2] // head_dim - 2) // 2
    rows = kv_local * (2 * per_core + 2)
    vmem = pl.BlockSpec(memory_space=pltpu.VMEM)
    anyspace = pl.BlockSpec(memory_space=pl.ANY)
    return pl.pallas_call(
        qkv_kernel,
        out_shape=jax.ShapeDtypeStruct((rows, num_seqs, head_dim), F32),
        in_specs=[vmem] * 5 + [anyspace],
        out_specs=anyspace,
        scratch_shapes=[
            pltpu.VMEM((num_seqs, depth), BF16),
            pltpu.VMEM((rows, num_seqs, head_dim), F32),
            pltpu.VMEM((kv_local, num_seqs, per_core * head_dim), F32),
            pltpu.VMEM((kv_local, num_seqs, head_dim), F32),
            pltpu.VMEM((QKV_SLOTS, QKV_ROWS, kv_local, per_core * head_dim), BF16),
            pltpu.VMEM((QKV_SLOTS, QKV_ROWS, kv_local, head_dim), BF16),
            pltpu.SemaphoreType.DMA((QKV_SLOTS,)),
            pltpu.SemaphoreType.DMA((QKV_SLOTS,)),
            pltpu.SemaphoreType.DMA((kv_local + 1,)),
            pltpu.SemaphoreType.DMA((kv_local + 1,)),
            pltpu.SemaphoreType.DMA,
        ],
        compiler_params=pltpu.CompilerParams(collective_id=0, has_side_effects=True, vmem_limit_bytes=56 << 20),
        name="qkv_heads",
    )(hidden, norm_gain.reshape(1, depth), rope_cos.T, rope_sin.T, b_qkv, w_qkv)


ATT_SEQS = 8


def attend_kernel(lens_ref, heads_ref, sink_ref, k_ref, v_ref, k_out, v_out, num_ref, ml_ref):
    step = pl.program_id(0)
    q_rows = num_ref.shape[0]
    kv_local = (heads_ref.shape[0] - q_rows) // 2
    group = q_rows // kv_local
    rows, head_dim = k_ref.shape[1:]
    ctx_local = rows // kv_local
    base = lax.axis_index("sp") * ctx_local
    scale = head_dim**-0.5
    col = lax.broadcasted_iota(jnp.int32, (q_rows, rows), 1)
    kv_row = lax.div(lax.broadcasted_iota(jnp.int32, (q_rows, rows), 0), group)
    col_pos = jnp.where(lax.rem(col, kv_local) == kv_row, lax.div(col, kv_local), ctx_local * 1024)
    sub_pos = lax.div(lax.broadcasted_iota(jnp.int32, (16, head_dim), 0), kv_local)
    lane = lax.broadcasted_iota(jnp.int32, (q_rows, head_dim), 1)
    sink = sink_ref[...]

    @pl.when(step == 0)
    def _():
        ml_ref[...] = jnp.zeros_like(ml_ref)

    m_all = ml_ref[0:q_rows]
    l_all = ml_ref[q_rows : 2 * q_rows]
    for s in range(ATT_SEQS):
        seq = step * ATT_SEQS + s
        n = lens_ref[seq] - base
        inside = jnp.logical_and(n >= 0, n < ctx_local)
        at = jnp.where(inside, n, 0)
        start = pl.multiple_of(lax.div(at * kv_local, 16) * 16, 16)
        hit = jnp.logical_and(sub_pos == lax.rem(at, 16 // kv_local), inside)
        for cache, out, lo in ((k_ref, k_out, q_rows), (v_ref, v_out, q_rows + kv_local)):
            out[s] = cache[s]
            new = heads_ref[lo : lo + kv_local, s, :]
            new = jnp.concatenate([new] * (16 // kv_local), axis=0)
            old = cache[s, pl.ds(start, 16), :].astype(F32)
            out[s, pl.ds(start, 16), :] = jnp.where(hit, new, old).astype(BF16)
        q = heads_ref[0:q_rows, s, :].astype(BF16)
        logits = lax.dot_general(q, k_out[s], (((1,), (1,)), ((), ())), preferred_element_type=F32) * scale
        logits = jnp.where(col_pos <= n, logits, -jnp.inf)
        m = jnp.maximum(jnp.max(logits, axis=1, keepdims=True), sink)
        e = jnp.exp(logits - m[:, 0:1])
        total = jnp.sum(e, axis=1, keepdims=True)
        num_ref[:, s, :] = jnp.dot(e.astype(BF16), v_out[s], preferred_element_type=F32)
        here = lane == seq
        m_all = jnp.where(here, m, m_all)
        l_all = jnp.where(here, total, l_all)
    ml_ref[0:q_rows] = m_all
    ml_ref[q_rows : 2 * q_rows] = l_all


def attend(seq_lens, heads, sink_wide, k_rows, v_rows):
    num_seqs, rows, head_dim = k_rows.shape
    q_rows = sink_wide.shape[0]
    cache = pl.BlockSpec((ATT_SEQS, rows, head_dim), lambda i, lens: (i, 0, 0))
    return pl.pallas_call(
        attend_kernel,
        grid_spec=pltpu.PrefetchScalarGridSpec(
            num_scalar_prefetch=1,
            grid=(num_seqs // ATT_SEQS,),
            in_specs=[
                pl.BlockSpec((heads.shape[0], ATT_SEQS, head_dim), lambda i, lens: (0, i, 0)),
                pl.BlockSpec((q_rows, head_dim), lambda i, lens: (0, 0)),
                cache,
                cache,
            ],
            out_specs=[
                cache,
                cache,
                pl.BlockSpec((q_rows, ATT_SEQS, head_dim), lambda i, lens: (0, i, 0)),
                pl.BlockSpec((2 * q_rows, num_seqs), lambda i, lens: (0, 0)),
            ],
        ),
        out_shape=[
            jax.ShapeDtypeStruct(k_rows.shape, BF16),
            jax.ShapeDtypeStruct(v_rows.shape, BF16),
            jax.ShapeDtypeStruct((q_rows, num_seqs, head_dim), F32),
            jax.ShapeDtypeStruct((2 * q_rows, num_seqs), F32),
        ],
        compiler_params=pltpu.CompilerParams(dimension_semantics=("arbitrary",), vmem_limit_bytes=40 << 20),
        name="attend",
    )(seq_lens, heads, sink_wide, k_rows, v_rows)


OUT_COLS = 256
HEAD_GROUPS = 4
LAG_Y = 4
LAG_X = 3


def finish_kernel(num_ref, ml_ref, sink_ref, hid_ref, bo_ref, wo_ref, y_ref,
                  w_buf, x_buf, r1, r1ml, own, away, away_ml, r2, r2ml, fac, o_buf, r3, o_all,
                  y_send, y_recv, z_buf, x_recv, p1, p2,
                  w_sem, h_sem, s1_send, s1_recv, s2_send, s2_recv, s3_send, s3_recv,
                  y_ss, y_rs, x_ss, x_rs, p1_ss, p1_rs, p2_ss, p2_rs):
    chip, core = sp_place()
    tp = lax.axis_index("tp")
    partner = {"sp": 2 * chip + (1 - core)}
    across_x = {"sp": 2 * (1 - chip) + core}
    across_y = {"tp": 1 - tp}
    q_rows, num_seqs, head_dim = num_ref.shape
    half_h = q_rows // 2
    half_s = num_seqs // 2
    cols = w_buf.shape[1]
    chunks = cols // OUT_COLS
    per_group = half_h // HEAD_GROUPS
    mine = pl.multiple_of(core * half_h, half_h)
    theirs = pl.multiple_of((1 - core) * half_h, half_h)
    here = pl.ds(pl.multiple_of(chip * half_s, half_s), half_s)
    there = pl.ds(pl.multiple_of((1 - chip) * half_s, half_s), half_s)

    barrier = pltpu.get_barrier_semaphore()
    for peer in (partner, across_x, across_y):
        pl.semaphore_signal(barrier, inc=1, device_id=peer, device_id_type=MESH)

    parts = w_sem.shape[0]
    w_rows = w_buf.shape[0] // parts
    w_copies = []
    my_cols = pl.ds(pl.multiple_of(core * cols, 128), cols)
    for p in range(parts):
        rows = pl.ds(p * w_rows, w_rows)
        w_copies.append(pltpu.make_async_copy(wo_ref.at[rows, my_cols], w_buf.at[rows], w_sem.at[p]))
        w_copies[-1].start()
    h_copy = pltpu.make_async_copy(hid_ref.at[here, my_cols], x_buf, h_sem)
    h_copy.start()

    pl.semaphore_wait(barrier, 3)

    c_ml = remote(ml_ref, r1ml, s1_send.at[0], s1_recv.at[0], partner)
    c_there = remote(num_ref.at[pl.ds(theirs, half_h), there], r1.at[:, there], s1_send.at[1], s1_recv.at[1], partner)
    c_here = remote(num_ref.at[pl.ds(theirs, half_h), here], r1.at[:, here], s1_send.at[2], s1_recv.at[2], partner)
    for c in (c_ml, c_there, c_here):
        c.start()

    c_ml.wait_recv()
    m_a, l_a = ml_ref[pl.ds(mine, half_h)], ml_ref[pl.ds(q_rows + mine, half_h)]
    m_b, l_b = r1ml[pl.ds(mine, half_h)], r1ml[pl.ds(q_rows + mine, half_h)]
    m_chip = jnp.maximum(m_a, m_b)
    f_a = jnp.exp(m_a - m_chip)
    f_b = jnp.exp(m_b - m_chip)
    l_chip = l_a * f_a + l_b * f_b
    fac[0] = f_a.T
    fac[1] = f_b.T
    away_ml[0:half_h] = m_chip
    away_ml[half_h : 2 * half_h] = l_chip
    c2_ml = remote(away_ml, r2ml, s2_send.at[HEAD_GROUPS], s2_recv.at[HEAD_GROUPS], across_x)
    c2_ml.start()

    c_there.wait_recv()
    fa, fb = fac[0, there, :], fac[1, there, :]
    c2 = []
    for g in range(HEAD_GROUPS):
        for h in range(g * per_group, (g + 1) * per_group):
            away[h] = num_ref[mine + h, there, :] * fa[:, h : h + 1] + r1[h, there, :] * fb[:, h : h + 1]
        part = pl.ds(g * per_group, per_group)
        c2.append(remote(away.at[part], r2.at[part], s2_send.at[g], s2_recv.at[g], across_x))
        c2[-1].start()
    c_here.wait_recv()
    fa, fb = fac[0, here, :], fac[1, here, :]
    for h in range(half_h):
        own[h] = num_ref[mine + h, here, :] * fa[:, h : h + 1] + r1[h, here, :] * fb[:, h : h + 1]

    c2_ml.wait_recv()
    m_o, l_o = r2ml[0:half_h], r2ml[half_h : 2 * half_h]
    m_top = jnp.maximum(m_chip, m_o)
    f_a = jnp.exp(m_chip - m_top)
    f_b = jnp.exp(m_o - m_top)
    den = l_chip * f_a + l_o * f_b + jnp.exp(sink_ref[pl.ds(mine, half_h)] - m_top)
    fac[2] = (f_a / den).T
    fac[3] = (f_b / den).T
    fa, fb = fac[2, here, :], fac[3, here, :]
    c3 = []
    width = per_group * head_dim
    for g in range(HEAD_GROUPS):
        c2[g].wait_recv()
        for i in range(per_group):
            h = g * per_group + i
            o_buf[g, :, i * head_dim : (i + 1) * head_dim] = own[h] * fa[:, h : h + 1] + r2[h] * fb[:, h : h + 1]
        c3.append(remote(o_buf.at[g], r3.at[g], s3_send.at[g], s3_recv.at[g], partner))
        c3[-1].start()
        o_all[:, pl.ds(pl.multiple_of(core * half_h * head_dim + g * width, 128), width)] = o_buf[g].astype(BF16)
    for g in range(HEAD_GROUPS):
        c3[g].wait_recv()
        o_all[:, pl.ds(pl.multiple_of((1 - core) * half_h * head_dim + g * width, 128), width)] = r3[g].astype(BF16)
    for c in w_copies:
        c.wait()
    h_copy.wait()

    def y_copy(j):
        return remote(y_send.at[j], y_recv.at[j], y_ss.at[j], y_rs.at[j], across_y)

    def x_copy(j):
        return remote(z_buf.at[j], x_recv.at[j], x_ss.at[j], x_rs.at[j], across_x)

    def p1_copy(j):
        return remote(z_buf.at[j], p1.at[j], p1_ss.at[j], p1_rs.at[j], partner)

    def p2_copy(j):
        return remote(x_recv.at[j], p2.at[j], p2_ss.at[j], p2_rs.at[j], partner)

    def at_col(which, j):
        return pl.ds(pl.multiple_of(which * cols + j * OUT_COLS, 128), OUT_COLS)

    def body(t, _):
        @pl.when(t < chunks)
        def _():
            j = t
            w = w_buf[:, pl.ds(pl.multiple_of(j * OUT_COLS, 128), OUT_COLS)]
            y_send[j] = jnp.dot(o_all[...], w, preferred_element_type=F32)
            y_copy(j).start()

        @pl.when(jnp.logical_and(t >= LAG_Y, t < chunks + LAG_Y))
        def _():
            j = t - LAG_Y
            y_copy(j).wait_recv()
            x_part = x_buf[:, pl.ds(pl.multiple_of(j * OUT_COLS, 128), OUT_COLS)].astype(F32)
            z = (x_part + (y_send[j] + y_recv[j]) + bo_ref[:, at_col(core, j)].astype(F32)).astype(BF16)
            z_buf[j] = z.astype(F32)
            x_copy(j).start()
            p1_copy(j).start()
            y_ref[here, at_col(core, j)] = z

        @pl.when(t >= LAG_Y + LAG_X)
        def _():
            j = t - (LAG_Y + LAG_X)
            x_copy(j).wait_recv()
            p2_copy(j).start()
            y_ref[there, at_col(core, j)] = x_recv[j].astype(BF16)
            p1_copy(j).wait_recv()
            y_ref[here, at_col(1 - core, j)] = p1[j].astype(BF16)

        return 0

    lax.fori_loop(0, chunks + LAG_Y + LAG_X, body, 0)

    def tail(j, _):
        p2_copy(j).wait_recv()
        y_ref[there, at_col(1 - core, j)] = p2[j].astype(BF16)
        y_copy(j).wait_send()
        x_copy(j).wait_send()
        p1_copy(j).wait_send()
        p2_copy(j).wait_send()
        return 0

    lax.fori_loop(0, chunks, tail, 0)
    for c in (c_ml, c_there, c_here, c2_ml, *c2, *c3):
        c.wait_send()


def finish(num, ml, sink_wide, hidden, b_o, w_o):
    q_rows, num_seqs, head_dim = num.shape
    half_h, half_s = q_rows // 2, num_seqs // 2
    width = w_o.shape[1]
    cols = width // 2
    chunks = cols // OUT_COLS
    group_cols = half_h // HEAD_GROUPS * head_dim
    vmem = pl.BlockSpec(memory_space=pltpu.VMEM)
    anyspace = pl.BlockSpec(memory_space=pl.ANY)
    chunked = pltpu.VMEM((chunks, half_s, OUT_COLS), F32)
    dma = pltpu.SemaphoreType.DMA
    return pl.pallas_call(
        finish_kernel,
        out_shape=jax.ShapeDtypeStruct((num_seqs, width), BF16),
        in_specs=[vmem, vmem, vmem, anyspace, vmem, anyspace],
        out_specs=vmem,
        scratch_shapes=[
            pltpu.VMEM((w_o.shape[0], cols), BF16),
            pltpu.VMEM((half_s, cols), BF16),
            pltpu.VMEM((half_h, num_seqs, head_dim), F32),
            pltpu.VMEM((2 * q_rows, num_seqs), F32),
            pltpu.VMEM((half_h, half_s, head_dim), F32),
            pltpu.VMEM((half_h, half_s, head_dim), F32),
            pltpu.VMEM((2 * half_h, num_seqs), F32),
            pltpu.VMEM((half_h, half_s, head_dim), F32),
            pltpu.VMEM((2 * half_h, num_seqs), F32),
            pltpu.VMEM((4, num_seqs, half_h), F32),
            pltpu.VMEM((HEAD_GROUPS, half_s, group_cols), F32),
            pltpu.VMEM((HEAD_GROUPS, half_s, group_cols), F32),
            pltpu.VMEM((half_s, q_rows * head_dim), BF16),
            chunked, chunked, chunked, chunked, chunked, chunked,
            dma((4,)), dma,
            dma((3,)), dma((3,)),
            dma((HEAD_GROUPS + 1,)), dma((HEAD_GROUPS + 1,)),
            dma((HEAD_GROUPS,)), dma((HEAD_GROUPS,)),
            *[dma((chunks,))] * 8,
        ],
        compiler_params=pltpu.CompilerParams(collective_id=1, has_side_effects=True, vmem_limit_bytes=60 << 20),
        name="finish",
    )(num, ml, sink_wide, hidden, b_o.reshape(1, width), w_o)


def solution(mesh):
    cache_spec = P("dp", "sp", "tp", None)

    def block_step(hidden, seq_lens, rope_cos, rope_sin, k_cache, v_cache, norm_gain, w_qkv, b_qkv, sink_logits, w_o, b_o):
        num_seqs, ctx_local, kv_local, head_dim = k_cache.shape
        heads = qkv_heads(hidden, rope_cos, rope_sin, norm_gain, w_qkv, b_qkv, head_dim)
        sink_wide = jnp.broadcast_to(sink_logits[:, None], (sink_logits.shape[0], num_seqs))
        rows = (num_seqs, ctx_local * kv_local, head_dim)
        k_out, v_out, num, ml = attend(seq_lens, heads, sink_wide, k_cache.reshape(rows), v_cache.reshape(rows))
        out_hidden = finish(num, ml, sink_wide, hidden, b_o, w_o)
        return out_hidden, k_out.reshape(k_cache.shape), v_out.reshape(v_cache.shape)

    return jax.shard_map(block_step, mesh=mesh, in_specs=(P("dp", None), P("dp"), P("dp", None), P("dp", None), cache_spec, cache_spec, P(None), P(None, "tp", None), P("tp", None), P("tp"), P("tp", None), P(None)), out_specs=(P("dp", None), cache_spec, cache_spec), check_vma=False)
```

time: 242 us -> 142 us (0.59)
  Pallas kernels: 0 us -> 128 us
  waiting for transfers between devices: 95.4 us -> 0 us
  matrix products: 67.4 us -> 0 us
  other arithmetic: 34.8 us -> 0 us
  between operations: 14.3 us -> 0.68 us
  local copies, waits for them, and re-layouts: 25.2 us -> 12.8 us
  starting transfers between devices: 4.62 us -> 0 us
    pallas_call x0 -> x3, Pallas kernels: none -> 128 us  [the longest x1 53.3 us: finish(): pl.pallas_call(finish_kernel, out_shape=jax.ShapeDtypeStruct((num_seqs, w...]
    psum x1 -> x0, waiting for transfers between devices: 69.6 us -> none  [block_step(): summed = lax.psum(partial_out, ('tp', 'sp'))]
    dot_general x4 -> x0, matrix products: 67.4 us -> none  [the longest x1 45.6 us: local_partials(): jnp.einsum('bd,dkc->bkc', normed, w_qkv, preferred_element_type=jnp.float32)]
    all_to_all x1 -> x0, waiting for transfers between devices: 25.8 us -> none  [block_step(): lax.all_to_all(packed.reshape(num_seqs, sp_size, head_share, width), 'sp'...]
    select_n x1 -> x0, other arithmetic: 13.5 us -> none  [local_partials(): k_out = jnp.where(is_new, k_new[:, None], k_cache)]
    convert_element_type x5 -> x0, other arithmetic: 5.67 us -> none  [the longest x1 4.04 us: block_step(): (hidden.astype(jnp.float32) + summed + b_o.astype(jnp.float32)).astype(jn...]
    concatenate x2 -> x0, local copies, waits for them, and re-layouts: 5.07 us -> none  [the longest x1 4.93 us: local_partials(): jnp.concatenate([row_max[..., None], row_sum[..., None], weighted], axis=-1)]
    all_to_all x1 -> x0, starting transfers between devices: 4.61 us -> none  [block_step(): lax.all_to_all(packed.reshape(num_seqs, sp_size, head_share, width), 'sp'...]
  transfers between devices with their start and end apart: 2 -> 0, of which waited for: 2 -> 0; matrix products, arithmetic and copies ran while one was open for 0% -> 0% of each run, Pallas kernels for 0% -> 0%
where the time goes in v1:
time: 142 us; the launch traced here: 141 us
  Pallas kernels  128 us (90%)
  local copies, waits for them, and re-layouts  12.8 us (9%)
    pallas_call x1, Pallas kernels, finish(): pl.pallas_call(finish_kernel, out_shape=jax.ShapeDtypeStruct((num_seqs, w...  53.3 us
    pallas_call x1, Pallas kernels, attend(): pl.pallas_call(attend_kernel, grid_spec=pltpu.PrefetchScalarGridSpec(num_...  44.9 us
    pallas_call x1, Pallas kernels, qkv_heads(): pl.pallas_call(qkv_kernel, out_shape=jax.ShapeDtypeStruct((rows, num_seqs...  29.5 us
    unnamed x15, local copies, waits for them, and re-layouts  10.1 us

profile of v1, /device:TPU:0, one launch (start us, length us, event | category | flops | bytes accessed | tf_op | source)
XLA Modules:
  0.0 141.2 jit_solution(9324224801774531540)
XLA Ops:
  0.6 0.7 broadcast_in_dim.2.sink_ref
  1.4 0.0 copy-start.3
  1.4 1.4 reshape.25.gain_ref
  2.7 0.0 copy-start.5
  2.7 29.5 %qkv_heads.1.heads_ref = f32[40,128,128]{2,1,0:T(8,128)} custom-call(bf16[128,8192]{1,0:T(8,128)(2,1)} %hid_ref.1, bf16[1,8192]{1,0:T(2,128)(2,1)} %reshape.25.gain_ref, f32[64,128]{1,0:T(8,128)} %bitcast.8, f32[64,128]{1,0:T(8,128)} %bitcast.9, bf16[4,1280]{1,0:T(4,128)(2,1)} %bias_ref.1, bf16[8192,4,1280]{2,1,0:T(4,128)(2,1)} %w_ref.1), custom_call_target="tpu_custom_call" | custom-call | tf_op jit(solution)/shard_map/qkv_heads/pallas_call | solution.py:126
  32.2 0.0 copy-done.3
  32.2 0.0 copy-done.5
  32.2 0.0 copy-start
  32.2 1.7 %copy-done = f32[40,128,128]{2,1,0:T(8,128)S(1)} copy-done((f32[40,128,128]{2,1,0:T(8,128)S(1)}, f32[40,128,128]{2,1,0:T(8,128)}, u32[]{:S(2)}) %copy-start) | copy-done | bytes 2621464
  34.0 0.0 copy-start.1
  34.0 3.4 %copy-done.1 = bf16[128,64,4,128]{3,2,1,0:T(4,128)(2,1)S(1)} copy-done((bf16[128,64,4,128]{3,2,1,0:T(4,128)(2,1)S(1)}, bf16[128,64,4,128]{3,2,1,0:T(4,128)(2,1)}, u32[]{:S(2)}) %copy-start.1) | copy-done | bytes 8388632
  37.4 0.0 copy-start.6
  37.4 44.9 %attend.1 = (bf16[128,256,128]{2,1,0:T(8,128)(2,1)}, bf16[128,256,128]{2,1,0:T(8,128)(2,1)}, f32[32,128,128]{2,1,0:T(8,128)S(1)}, f32[64,128]{1,0:T(8,128)S(1)}) custom-call(s32[128]{0:T(128)S(1)} %copy-done.5, f32[40,128,128]{2,1,0:T(8,128)S(1)} %copy-done, f32[32,128]{1,0:T(8,128)S(1)} %broadcast_in_dim.2.sink_ref, bf16[128,256,128]{2,1,0:T(8,128)(2,1)S(1)} %bitcast.6, ...), custom_call_target="tpu_custom_call" | custom-call | tf_op jit(solution)/shard_map/attend/pallas_call | solution.py:205
  82.3 0.0 copy-start.2
  82.3 1.3 copy-done.2
  83.6 0.0 copy-start.4
  83.6 0.6 copy-done.4
  84.2 0.0 copy-done.6
  84.2 0.6 reshape.28.bo_ref
  84.8 53.3 %finish.1 = bf16[128,8192]{1,0:T(8,128)(2,1)} custom-call(f32[32,128,128]{2,1,0:T(8,128)} %copy-done.2, f32[64,128]{1,0:T(8,128)} %copy-done.4, f32[32,128]{1,0:T(8,128)} %copy-done.3, bf16[128,8192]{1,0:T(8,128)(2,1)} %hid_ref.1, bf16[1,8192]{1,0:T(2,128)(2,1)} %reshape.28.bo_ref, bf16[4096,8192]{1,0:T(8,128)(2,1)} %wo_ref.1), custom_call_target="tpu_custom_call" | custom-call | tf_op jit(solution)/shard_map/finish/pallas_call | solution.py:410
  138.1 3.1 %copy.16 = bf16[128,8192]{1,0:T(8,128)(2,1)} copy(bf16[128,8192]{1,0:T(8,128)(2,1)} %finish.1) | data formatting | bytes 4194304
Async XLA Ops:
  1.4 30.9 %copy-start.3 = (f32[32,128]{1,0:T(8,128)}, f32[32,128]{1,0:T(8,128)S(1)}, u32[]{:S(2)}) copy-start(f32[32,128]{1,0:T(8,128)S(1)} %broadcast_in_dim.2.sink_ref) | copy-start | bytes 49156
  2.7 29.5 %copy-start.5 = (s32[128]{0:T(128)S(1)}, s32[128]{0:T(128)}, u32[]{:S(2)}) copy-start(s32[128]{0:T(128)} %lens_ref.1) | copy-start | bytes 1540
  32.2 1.7 %copy-start = (f32[40,128,128]{2,1,0:T(8,128)S(1)}, f32[40,128,128]{2,1,0:T(8,128)}, u32[]{:S(2)}) copy-start(f32[40,128,128]{2,1,0:T(8,128)} %qkv_heads.1.heads_ref) | copy-start | bytes 7864324
  34.0 3.4 %copy-start.1 = (bf16[128,64,4,128]{3,2,1,0:T(4,128)(2,1)S(1)}, bf16[128,64,4,128]{3,2,1,0:T(4,128)(2,1)}, u32[]{:S(2)}) copy-start(bf16[128,64,4,128]{3,2,1,0:T(4,128)(2,1)} %param.16) | copy-start | bytes 25165828
  37.4 46.8 %copy-start.6 = (bf16[8192]{0:T(1024)(128)(2,1)S(1)}, bf16[8192]{0:T(1024)(128)(2,1)}, u32[]{:S(2)}) copy-start(bf16[8192]{0:T(1024)(128)(2,1)} %param.23) | copy-start | bytes 49156
  82.3 1.3 copy-start.2
  83.6 0.6 copy-start.4

commit v2 on v1

--- a/solution.py
+++ b/solution.py
@@ -22,11 +22,17 @@
     return pltpu.make_async_remote_copy(src_ref=src, dst_ref=dst, send_sem=send_sem, recv_sem=recv_sem, device_id=where, device_id_type=MESH)
 
 
+def column(row_ref, count):
+    wide = jnp.broadcast_to(row_ref[...], (count, count))
+    same = lax.broadcasted_iota(jnp.int32, (count, count), 0) == lax.broadcasted_iota(jnp.int32, (count, count), 1)
+    return jnp.sum(jnp.where(same, wide, 0.0), axis=1, keepdims=True)
+
+
 QKV_ROWS = 512
 QKV_SLOTS = 3
 
 
-def qkv_kernel(x_ref, gain_ref, cos_ref, sin_ref, bias_ref, w_ref, out_ref, normed, heads, acc_q, acc_e, wq_buf, we_buf, wq_sem, we_sem, send_sem, recv_sem, out_sem):
+def qkv_kernel(x_ref, gain_ref, cos_ref, sin_ref, bias_ref, w_ref, out_ref, normed, gain, heads, acc_q, acc_e, wq_buf, we_buf, wq_sem, we_sem, send_sem, recv_sem, out_sem):
     chip, core = sp_place()
     partner = {"sp": 2 * chip + (1 - core)}
     num_seqs, depth = x_ref.shape
@@ -50,11 +56,15 @@
     barrier = pltpu.get_barrier_semaphore()
     pl.semaphore_signal(barrier, inc=1, device_id=partner, device_id_type=MESH)
 
+    gain[...] = gain_ref[...].astype(F32)
+
     def norm_rows(r, _):
         rows = pl.ds(pl.multiple_of(r * 16, 16), 16)
         xw = x_ref[rows, :].astype(F32)
         inv = lax.rsqrt(jnp.mean(xw * xw, axis=-1, keepdims=True) + NORM_EPS)
-        normed[rows, :] = (xw * inv * gain_ref[...].astype(F32)).astype(BF16)
+        for t in range(depth // head_dim):
+            cols = slice(t * head_dim, (t + 1) * head_dim)
+            normed[rows, cols] = (xw[:, cols] * inv * gain[t : t + 1, :]).astype(BF16)
         return 0
 
     lax.fori_loop(0, num_seqs // 16, norm_rows, 0)
@@ -130,6 +140,7 @@
         out_specs=anyspace,
         scratch_shapes=[
             pltpu.VMEM((num_seqs, depth), BF16),
+            pltpu.VMEM((depth // head_dim, head_dim), F32),
             pltpu.VMEM((rows, num_seqs, head_dim), F32),
             pltpu.VMEM((kv_local, num_seqs, per_core * head_dim), F32),
             pltpu.VMEM((kv_local, num_seqs, head_dim), F32),
@@ -143,7 +154,7 @@
         ],
         compiler_params=pltpu.CompilerParams(collective_id=0, has_side_effects=True, vmem_limit_bytes=56 << 20),
         name="qkv_heads",
-    )(hidden, norm_gain.reshape(1, depth), rope_cos.T, rope_sin.T, b_qkv, w_qkv)
+    )(hidden, norm_gain.reshape(depth // head_dim, head_dim), rope_cos.T, rope_sin.T, b_qkv, w_qkv)
 
 
 ATT_SEQS = 8
@@ -162,45 +173,51 @@
     kv_row = lax.div(lax.broadcasted_iota(jnp.int32, (q_rows, rows), 0), group)
     col_pos = jnp.where(lax.rem(col, kv_local) == kv_row, lax.div(col, kv_local), ctx_local * 1024)
     sub_pos = lax.div(lax.broadcasted_iota(jnp.int32, (16, head_dim), 0), kv_local)
-    lane = lax.broadcasted_iota(jnp.int32, (q_rows, head_dim), 1)
-    sink = sink_ref[...]
+    lane = lax.broadcasted_iota(jnp.int32, (q_rows, ml_ref.shape[1]), 1)
 
     @pl.when(step == 0)
     def _():
         ml_ref[...] = jnp.zeros_like(ml_ref)
 
-    m_all = ml_ref[0:q_rows]
-    l_all = ml_ref[q_rows : 2 * q_rows]
-    for s in range(ATT_SEQS):
-        seq = step * ATT_SEQS + s
-        n = lens_ref[seq] - base
+    seqs = range(ATT_SEQS)
+    rel = []
+    for s in seqs:
+        k_out[s] = k_ref[s]
+        v_out[s] = v_ref[s]
+    for s in seqs:
+        n = lens_ref[step * ATT_SEQS + s] - base
+        rel.append(n)
         inside = jnp.logical_and(n >= 0, n < ctx_local)
         at = jnp.where(inside, n, 0)
         start = pl.multiple_of(lax.div(at * kv_local, 16) * 16, 16)
         hit = jnp.logical_and(sub_pos == lax.rem(at, 16 // kv_local), inside)
         for cache, out, lo in ((k_ref, k_out, q_rows), (v_ref, v_out, q_rows + kv_local)):
-            out[s] = cache[s]
             new = heads_ref[lo : lo + kv_local, s, :]
             new = jnp.concatenate([new] * (16 // kv_local), axis=0)
             old = cache[s, pl.ds(start, 16), :].astype(F32)
             out[s, pl.ds(start, 16), :] = jnp.where(hit, new, old).astype(BF16)
-        q = heads_ref[0:q_rows, s, :].astype(BF16)
-        logits = lax.dot_general(q, k_out[s], (((1,), (1,)), ((), ())), preferred_element_type=F32) * scale
-        logits = jnp.where(col_pos <= n, logits, -jnp.inf)
-        m = jnp.maximum(jnp.max(logits, axis=1, keepdims=True), sink)
-        e = jnp.exp(logits - m[:, 0:1])
-        total = jnp.sum(e, axis=1, keepdims=True)
-        num_ref[:, s, :] = jnp.dot(e.astype(BF16), v_out[s], preferred_element_type=F32)
-        here = lane == seq
-        m_all = jnp.where(here, m, m_all)
-        l_all = jnp.where(here, total, l_all)
+    sink = column(sink_ref, q_rows)
+    queries = [heads_ref[0:q_rows, s, :].astype(BF16) for s in seqs]
+    logits = [lax.dot_general(queries[s], k_out[s], (((1,), (1,)), ((), ())), preferred_element_type=F32) for s in seqs]
+    logits = [jnp.where(col_pos <= rel[s], logits[s] * scale, -jnp.inf) for s in seqs]
+    tops = [jnp.maximum(jnp.max(logits[s], axis=1, keepdims=True), sink) for s in seqs]
+    weights = [jnp.exp(logits[s] - tops[s]) for s in seqs]
+    totals = [jnp.sum(weights[s], axis=1, keepdims=True) for s in seqs]
+    sums = [jnp.dot(weights[s].astype(BF16), v_out[s], preferred_element_type=F32) for s in seqs]
+    m_all = ml_ref[0:q_rows]
+    l_all = ml_ref[q_rows : 2 * q_rows]
+    for s in seqs:
+        num_ref[:, s, :] = sums[s]
+        here = lane == step * ATT_SEQS + s
+        m_all = jnp.where(here, tops[s], m_all)
+        l_all = jnp.where(here, totals[s], l_all)
     ml_ref[0:q_rows] = m_all
     ml_ref[q_rows : 2 * q_rows] = l_all
 
 
-def attend(seq_lens, heads, sink_wide, k_rows, v_rows):
+def attend(seq_lens, heads, sinks, k_rows, v_rows):
     num_seqs, rows, head_dim = k_rows.shape
-    q_rows = sink_wide.shape[0]
+    q_rows = sinks.shape[1]
     cache = pl.BlockSpec((ATT_SEQS, rows, head_dim), lambda i, lens: (i, 0, 0))
     return pl.pallas_call(
         attend_kernel,
@@ -209,7 +226,7 @@
             grid=(num_seqs // ATT_SEQS,),
             in_specs=[
                 pl.BlockSpec((heads.shape[0], ATT_SEQS, head_dim), lambda i, lens: (0, i, 0)),
-                pl.BlockSpec((q_rows, head_dim), lambda i, lens: (0, 0)),
+                pl.BlockSpec((1, q_rows), lambda i, lens: (0, 0)),
                 cache,
                 cache,
             ],
@@ -226,9 +243,9 @@
             jax.ShapeDtypeStruct((q_rows, num_seqs, head_dim), F32),
             jax.ShapeDtypeStruct((2 * q_rows, num_seqs), F32),
         ],
-        compiler_params=pltpu.CompilerParams(dimension_semantics=("arbitrary",), vmem_limit_bytes=40 << 20),
+        compiler_params=pltpu.CompilerParams(dimension_semantics=("arbitrary",), vmem_limit_bytes=60 << 20),
         name="attend",
-    )(seq_lens, heads, sink_wide, k_rows, v_rows)
+    )(seq_lens, heads, sinks, k_rows, v_rows)
 
 
 OUT_COLS = 256
@@ -238,7 +255,7 @@
 
 
 def finish_kernel(num_ref, ml_ref, sink_ref, hid_ref, bo_ref, wo_ref, y_ref,
-                  w_buf, x_buf, r1, r1ml, own, away, away_ml, r2, r2ml, fac, o_buf, r3, o_all,
+                  w_buf, x_buf, sink_col, bo_f32, r1, r1ml, own, away, away_ml, r2, r2ml, fac, o_buf, r3, o_all,
                   y_send, y_recv, z_buf, x_recv, p1, p2,
                   w_sem, h_sem, s1_send, s1_recv, s2_send, s2_recv, s3_send, s3_recv,
                   y_ss, y_rs, x_ss, x_rs, p1_ss, p1_rs, p2_ss, p2_rs):
@@ -273,6 +290,8 @@
     h_copy = pltpu.make_async_copy(hid_ref.at[here, my_cols], x_buf, h_sem)
     h_copy.start()
 
+    sink_col[...] = jnp.broadcast_to(column(sink_ref, q_rows), sink_col.shape)
+    bo_f32[...] = bo_ref[...].astype(F32)
     pl.semaphore_wait(barrier, 3)
 
     c_ml = remote(ml_ref, r1ml, s1_send.at[0], s1_recv.at[0], partner)
@@ -314,7 +333,7 @@
     m_top = jnp.maximum(m_chip, m_o)
     f_a = jnp.exp(m_chip - m_top)
     f_b = jnp.exp(m_o - m_top)
-    den = l_chip * f_a + l_o * f_b + jnp.exp(sink_ref[pl.ds(mine, half_h)] - m_top)
+    den = l_chip * f_a + l_o * f_b + jnp.exp(sink_col[pl.ds(mine, half_h)] - m_top)
     fac[2] = (f_a / den).T
     fac[3] = (f_b / den).T
     fa, fb = fac[2, here, :], fac[3, here, :]
@@ -363,7 +382,9 @@
             j = t - LAG_Y
             y_copy(j).wait_recv()
             x_part = x_buf[:, pl.ds(pl.multiple_of(j * OUT_COLS, 128), OUT_COLS)].astype(F32)
-            z = (x_part + (y_send[j] + y_recv[j]) + bo_ref[:, at_col(core, j)].astype(F32)).astype(BF16)
+            row = (core * cols + j * OUT_COLS) // head_dim
+            bias = jnp.concatenate([bo_f32[pl.ds(row + i, 1), :] for i in range(OUT_COLS // head_dim)], axis=1)
+            z = (x_part + (y_send[j] + y_recv[j]) + bias).astype(BF16)
             z_buf[j] = z.astype(F32)
             x_copy(j).start()
             p1_copy(j).start()
@@ -396,7 +417,7 @@
         c.wait_send()
 
 
-def finish(num, ml, sink_wide, hidden, b_o, w_o):
+def finish(num, ml, sinks, hidden, b_o, w_o):
     q_rows, num_seqs, head_dim = num.shape
     half_h, half_s = q_rows // 2, num_seqs // 2
     width = w_o.shape[1]
@@ -415,6 +436,8 @@
         scratch_shapes=[
             pltpu.VMEM((w_o.shape[0], cols), BF16),
             pltpu.VMEM((half_s, cols), BF16),
+            pltpu.VMEM((q_rows, num_seqs), F32),
+            pltpu.VMEM((width // head_dim, head_dim), F32),
             pltpu.VMEM((half_h, num_seqs, head_dim), F32),
             pltpu.VMEM((2 * q_rows, num_seqs), F32),
             pltpu.VMEM((half_h, half_s, head_dim), F32),
@@ -435,7 +458,7 @@
         ],
         compiler_params=pltpu.CompilerParams(collective_id=1, has_side_effects=True, vmem_limit_bytes=60 << 20),
         name="finish",
-    )(num, ml, sink_wide, hidden, b_o.reshape(1, width), w_o)
+    )(num, ml, sinks, hidden, b_o.reshape(width // head_dim, head_dim), w_o)
 
 
 def solution(mesh):
@@ -444,10 +467,10 @@
     def block_step(hidden, seq_lens, rope_cos, rope_sin, k_cache, v_cache, norm_gain, w_qkv, b_qkv, sink_logits, w_o, b_o):
         num_seqs, ctx_local, kv_local, head_dim = k_cache.shape
         heads = qkv_heads(hidden, rope_cos, rope_sin, norm_gain, w_qkv, b_qkv, head_dim)
-        sink_wide = jnp.broadcast_to(sink_logits[:, None], (sink_logits.shape[0], num_seqs))
+        sinks = sink_logits.reshape(1, sink_logits.shape[0])
         rows = (num_seqs, ctx_local * kv_local, head_dim)
-        k_out, v_out, num, ml = attend(seq_lens, heads, sink_wide, k_cache.reshape(rows), v_cache.reshape(rows))
-        out_hidden = finish(num, ml, sink_wide, hidden, b_o, w_o)
+        k_out, v_out, num, ml = attend(seq_lens, heads, sinks, k_cache.reshape(rows), v_cache.reshape(rows))
+        out_hidden = finish(num, ml, sinks, hidden, b_o, w_o)
         return out_hidden, k_out.reshape(k_cache.shape), v_out.reshape(v_cache.shape)
 
     return jax.shard_map(block_step, mesh=mesh, in_specs=(P("dp", None), P("dp"), P("dp", None), P("dp", None), cache_spec, cache_spec, P(None), P(None, "tp", None), P("tp", None), P("tp"), P("tp", None), P(None)), out_specs=(P("dp", None), cache_spec, cache_spec), check_vma=False)

time: 142 us -> 106 us (0.75)
  Pallas kernels: 128 us -> 102 us
  local copies, waits for them, and re-layouts: 12.8 us -> 3.1 us
    pallas_call x1, Pallas kernels: 44.9 us -> 19.3 us  [attend(): pl.pallas_call(attend_kernel, grid_spec=pltpu.PrefetchScalarGridSpec(num_...]
    unnamed x15 -> x1, local copies, waits for them, and re-layouts: 10.1 us -> 3.1 us
    reshape x2 -> x0, local copies, waits for them, and re-layouts: 1.98 us -> none  [the longest x1 1.36 us: qkv_heads(): norm_gain.reshape(1, depth)]
where the time goes in v2:
time: 106 us
  Pallas kernels  102 us (96%)
  local copies, waits for them, and re-layouts  3.1 us (3%)
    pallas_call x1, Pallas kernels, finish(): pl.pallas_call(finish_kernel, out_shape=jax.ShapeDtypeStruct((num_seqs, w...  53.3 us
    pallas_call x1, Pallas kernels, qkv_heads(): pl.pallas_call(qkv_kernel, out_shape=jax.ShapeDtypeStruct((rows, num_seqs...  29.3 us
    pallas_call x1, Pallas kernels, attend(): pl.pallas_call(attend_kernel, grid_spec=pltpu.PrefetchScalarGridSpec(num_...  19.3 us
    unnamed x1, local copies, waits for them, and re-layouts  3.1 us

profile of v2, /device:TPU:0, one launch (start us, length us, event | category | flops | bytes accessed | tf_op | source)
XLA Modules:
  0.0 105.7 jit_solution(13050713277175894219)
XLA Ops:
  0.6 29.3 %qkv_heads.1.heads_ref = f32[40,128,128]{2,1,0:T(8,128)} custom-call(bf16[128,8192]{1,0:T(8,128)(2,1)} %hid_ref.1, bf16[64,128]{1,0:T(8,128)(2,1)} %bitcast.13, f32[64,128]{1,0:T(8,128)} %bitcast.11, f32[64,128]{1,0:T(8,128)} %bitcast.12, bf16[4,1280]{1,0:T(4,128)(2,1)} %bias_ref.1, bf16[8192,4,1280]{2,1,0:T(4,128)(2,1)} %w_ref.1), custom_call_target="tpu_custom_call" | custom-call | tf_op jit(solution)/shard_map/qkv_heads/pallas_call | solution.py:136
  30.0 19.3 %attend.1 = (bf16[128,256,128]{2,1,0:T(8,128)(2,1)}, bf16[128,256,128]{2,1,0:T(8,128)(2,1)}, f32[32,128,128]{2,1,0:T(8,128)}, f32[64,128]{1,0:T(8,128)}) custom-call(s32[128]{0:T(128)} %lens_ref.1, f32[40,128,128]{2,1,0:T(8,128)} %qkv_heads.1.heads_ref, f32[1,32]{1,0:T(1,128)} %bitcast.15, bf16[128,256,128]{2,1,0:T(8,128)(2,1)} %bitcast.9, ...), custom_call_target="tpu_custom_call" | custom-call | tf_op jit(solution)/shard_map/attend/pallas_call | solution.py:222
  49.3 53.3 %finish.1 = bf16[128,8192]{1,0:T(8,128)(2,1)} custom-call(f32[32,128,128]{2,1,0:T(8,128)} %get-tuple-element.7.num_ref, f32[64,128]{1,0:T(8,128)} %get-tuple-element.8.ml_ref, f32[1,32]{1,0:T(1,128)} %bitcast.16, bf16[128,8192]{1,0:T(8,128)(2,1)} %hid_ref.1, bf16[64,128]{1,0:T(8,128)(2,1)} %bitcast.14, bf16[4096,8192]{1,0:T(8,128)(2,1)} %wo_ref.1), custom_call_target="tpu_custom_call" | custom-call | tf_op jit(solution)/shard_map/finish/pallas_call | solution.py:431
  102.6 3.1 %copy.16 = bf16[128,8192]{1,0:T(8,128)(2,1)} copy(bf16[128,8192]{1,0:T(8,128)(2,1)} %finish.1) | data formatting | bytes 4194304

commit v3 on v2

v3 whole, which is shorter than its diff:
```python
import functools

import jax
import jax.numpy as jnp
from jax import lax
from jax.experimental import pallas as pl
from jax.experimental.pallas import tpu as pltpu
from jax.sharding import PartitionSpec as P

NORM_EPS = 1e-5
F32 = jnp.float32
BF16 = jnp.bfloat16
MESH = pl.DeviceIdType.MESH


def sp_place():
    sp = lax.axis_index("sp")
    return lax.div(sp, 2), lax.rem(sp, 2)


def remote(src, dst, send_sem, recv_sem, where):
    return pltpu.make_async_remote_copy(src_ref=src, dst_ref=dst, send_sem=send_sem, recv_sem=recv_sem, device_id=where, device_id_type=MESH)


def column(row_ref, count):
    wide = jnp.broadcast_to(row_ref[...], (count, count))
    same = lax.broadcasted_iota(jnp.int32, (count, count), 0) == lax.broadcasted_iota(jnp.int32, (count, count), 1)
    return jnp.sum(jnp.where(same, wide, 0.0), axis=1, keepdims=True)


QKV_ROWS = 512
QKV_SLOTS = 3


def qkv_kernel(x_ref, gain_ref, cos_ref, sin_ref, bias_ref, w_ref, out_ref, normed, gain, heads, acc_q, acc_e, wq_buf, we_buf, wq_sem, we_sem, send_sem, recv_sem, out_sem):
    chip, core = sp_place()
    partner = {"sp": 2 * chip + (1 - core)}
    num_seqs, depth = x_ref.shape
    head_dim = acc_e.shape[2]
    q_cols = acc_q.shape[2]
    kv_local = acc_q.shape[0]
    per_core = q_cols // head_dim
    group = 2 * per_core
    steps = depth // QKV_ROWS

    def fetch(step, slot):
        rows = pl.ds(step * QKV_ROWS, QKV_ROWS)
        cq = pltpu.make_async_copy(w_ref.at[rows, :, pl.ds(pl.multiple_of(core * q_cols, 128), q_cols)], wq_buf.at[slot], wq_sem.at[slot])
        ce = pltpu.make_async_copy(w_ref.at[rows, :, pl.ds(pl.multiple_of((group + core) * head_dim, 128), head_dim)], we_buf.at[slot], we_sem.at[slot])
        return cq, ce

    for s in range(QKV_SLOTS - 1):
        for c in fetch(s, s):
            c.start()

    barrier = pltpu.get_barrier_semaphore()
    pl.semaphore_signal(barrier, inc=1, device_id=partner, device_id_type=MESH)

    gain[...] = gain_ref[...].astype(F32)

    def norm_rows(r, _):
        rows = pl.ds(pl.multiple_of(r * 16, 16), 16)
        xw = x_ref[rows, :].astype(F32)
        inv = lax.rsqrt(jnp.mean(xw * xw, axis=-1, keepdims=True) + NORM_EPS)
        for t in range(depth // head_dim):
            cols = slice(t * head_dim, (t + 1) * head_dim)
            normed[rows, cols] = (xw[:, cols] * inv * gain[t : t + 1, :]).astype(BF16)
        return 0

    lax.fori_loop(0, num_seqs // 16, norm_rows, 0)
    acc_q[...] = jnp.zeros_like(acc_q)
    acc_e[...] = jnp.zeros_like(acc_e)

    def step_fn(step, _):
        slot = lax.rem(step, QKV_SLOTS)
        for c in fetch(step, slot):
            c.wait()

        @pl.when(step + QKV_SLOTS - 1 < steps)
        def _():
            for c in fetch(step + QKV_SLOTS - 1, lax.rem(step + QKV_SLOTS - 1, QKV_SLOTS)):
                c.start()

        h = normed[:, pl.ds(pl.multiple_of(step * QKV_ROWS, 128), QKV_ROWS)]
        wq = jnp.swapaxes(wq_buf[slot], 0, 1)
        we = jnp.swapaxes(we_buf[slot], 0, 1)
        for k in range(kv_local):
            acc_q[k] += jnp.dot(h, wq[k], preferred_element_type=F32)
            acc_e[k] += jnp.dot(h, we[k], preferred_element_type=F32)
        return 0

    lax.fori_loop(0, steps, step_fn, 0)

    cos_t = cos_ref[...].T
    sin_t = sin_ref[...].T
    cos2 = jnp.concatenate([cos_t, cos_t], axis=1)
    sin2 = jnp.concatenate([-sin_t, sin_t], axis=1)
    is_key = core == 0
    cos_e = jnp.where(is_key, cos2, jnp.ones_like(cos2))
    sin_e = jnp.where(is_key, sin2, jnp.zeros_like(sin2))

    def rotate(v, c, s):
        r = v * c + pltpu.roll(v, head_dim // 2, 1) * s
        return r.astype(BF16).astype(F32)

    pl.semaphore_wait(barrier, 1)
    copies = []
    for k in range(kv_local):
        bias_q = bias_ref[k : k + 1, pl.ds(pl.multiple_of(core * q_cols, 128), q_cols)].astype(F32)
        for g in range(per_core):
            cols = slice(g * head_dim, (g + 1) * head_dim)
            heads[k * group + per_core * core + g] = rotate(acc_q[k, :, cols] + bias_q[:, cols], cos2, sin2)
        part = heads.at[pl.ds(k * group + per_core * core, per_core)]
        copies.append(remote(part, part, send_sem.at[k], recv_sem.at[k], partner))
        copies[-1].start()
    for k in range(kv_local):
        bias_e = bias_ref[k : k + 1, pl.ds(pl.multiple_of((group + core) * head_dim, 128), head_dim)].astype(F32)
        heads[kv_local * group + kv_local * core + k] = rotate(acc_e[k] + bias_e, cos_e, sin_e)
    part = heads.at[pl.ds(kv_local * group + kv_local * core, kv_local)]
    copies.append(remote(part, part, send_sem.at[kv_local], recv_sem.at[kv_local], partner))
    copies[-1].start()
    for c in copies:
        c.wait()
    done = pltpu.make_async_copy(heads, out_ref, out_sem)
    done.start()
    done.wait()


def qkv_heads(hidden, rope_cos, rope_sin, norm_gain, w_qkv, b_qkv, head_dim):
    num_seqs, depth = hidden.shape
    kv_local = w_qkv.shape[1]
    per_core = (w_qkv.shape[2] // head_dim - 2) // 2
    rows = kv_local * (2 * per_core + 2)
    vmem = pl.BlockSpec(memory_space=pltpu.VMEM)
    anyspace = pl.BlockSpec(memory_space=pl.ANY)
    return pl.pallas_call(
        qkv_kernel,
        out_shape=jax.ShapeDtypeStruct((rows, num_seqs, head_dim), F32),
        in_specs=[vmem] * 5 + [anyspace],
        out_specs=anyspace,
        scratch_shapes=[
            pltpu.VMEM((num_seqs, depth), BF16),
            pltpu.VMEM((depth // head_dim, head_dim), F32),
            pltpu.VMEM((rows, num_seqs, head_dim), F32),
            pltpu.VMEM((kv_local, num_seqs, per_core * head_dim), F32),
            pltpu.VMEM((kv_local, num_seqs, head_dim), F32),
            pltpu.VMEM((QKV_SLOTS, QKV_ROWS, kv_local, per_core * head_dim), BF16),
            pltpu.VMEM((QKV_SLOTS, QKV_ROWS, kv_local, head_dim), BF16),
            pltpu.SemaphoreType.DMA((QKV_SLOTS,)),
            pltpu.SemaphoreType.DMA((QKV_SLOTS,)),
            pltpu.SemaphoreType.DMA((kv_local + 1,)),
            pltpu.SemaphoreType.DMA((kv_local + 1,)),
            pltpu.SemaphoreType.DMA,
        ],
        compiler_params=pltpu.CompilerParams(collective_id=0, has_side_effects=True, vmem_limit_bytes=56 << 20),
        name="qkv_heads",
    )(hidden, norm_gain.reshape(depth // head_dim, head_dim), rope_cos.T, rope_sin.T, b_qkv, w_qkv)


ATT_SEQS = 8


def attend_kernel(lens_ref, heads_ref, sink_ref, k_ref, v_ref, k_out, v_out, num_ref, ml_ref, k_buf, v_buf, h_buf, n_buf, k_in, v_in, h_in, k_back, v_back, n_back):
    num_seqs, rows, head_dim = k_buf.shape
    q_rows = n_buf.shape[0]
    kv_local = (h_buf.shape[0] - q_rows) // 2
    group = q_rows // kv_local
    ctx_local = rows // kv_local
    steps = num_seqs // ATT_SEQS
    base = lax.axis_index("sp") * ctx_local
    scale = head_dim**-0.5

    def block(step):
        return pl.ds(pl.multiple_of(step * ATT_SEQS, ATT_SEQS), ATT_SEQS)

    def loads(step):
        at = block(step)
        return (
            pltpu.make_async_copy(heads_ref.at[:, at], h_buf.at[:, at], h_in.at[step]),
            pltpu.make_async_copy(k_ref.at[at], k_buf.at[at], k_in.at[step]),
            pltpu.make_async_copy(v_ref.at[at], v_buf.at[at], v_in.at[step]),
        )

    def stores(step):
        at = block(step)
        return (
            pltpu.make_async_copy(k_buf.at[at], k_out.at[at], k_back.at[step]),
            pltpu.make_async_copy(v_buf.at[at], v_out.at[at], v_back.at[step]),
            pltpu.make_async_copy(n_buf.at[:, at], num_ref.at[:, at], n_back.at[step]),
        )

    for step in range(steps):
        for c in loads(step):
            c.start()

    col = lax.broadcasted_iota(jnp.int32, (q_rows, rows), 1)
    kv_row = lax.div(lax.broadcasted_iota(jnp.int32, (q_rows, rows), 0), group)
    col_pos = jnp.where(lax.rem(col, kv_local) == kv_row, lax.div(col, kv_local), ctx_local * 1024)
    sub_pos = lax.div(lax.broadcasted_iota(jnp.int32, (16, head_dim), 0), kv_local)
    lane = lax.broadcasted_iota(jnp.int32, (q_rows, num_seqs), 1)
    sink = column(sink_ref, q_rows)
    seqs = range(ATT_SEQS)

    def step_fn(step, carry):
        m_all, l_all = carry
        for c in loads(step):
            c.wait()
        first = step * ATT_SEQS
        heads = h_buf.at[:, block(step)]
        rel = []
        for s in seqs:
            n = lens_ref[first + s] - base
            rel.append(n)
            inside = jnp.logical_and(n >= 0, n < ctx_local)
            at = jnp.where(inside, n, 0)
            start = pl.multiple_of(lax.div(at * kv_local, 16) * 16, 16)
            hit = jnp.logical_and(sub_pos == lax.rem(at, 16 // kv_local), inside)
            for cache, lo in ((k_buf, q_rows), (v_buf, q_rows + kv_local)):
                new = heads[lo : lo + kv_local, s, :]
                new = jnp.concatenate([new] * (16 // kv_local), axis=0)
                old = cache[first + s, pl.ds(start, 16), :].astype(F32)
                cache[first + s, pl.ds(start, 16), :] = jnp.where(hit, new, old).astype(BF16)
        queries = [heads[0:q_rows, s, :].astype(BF16) for s in seqs]
        logits = [lax.dot_general(queries[s], k_buf[first + s], (((1,), (1,)), ((), ())), preferred_element_type=F32) for s in seqs]
        logits = [jnp.where(col_pos <= rel[s], logits[s] * scale, -jnp.inf) for s in seqs]
        tops = [jnp.maximum(jnp.max(logits[s], axis=1, keepdims=True), sink) for s in seqs]
        weights = [jnp.exp(logits[s] - tops[s]) for s in seqs]
        totals = [jnp.sum(weights[s], axis=1, keepdims=True) for s in seqs]
        sums = [jnp.dot(weights[s].astype(BF16), v_buf[first + s], preferred_element_type=F32) for s in seqs]
        for s in seqs:
            here = lane == first + s
            m_all = jnp.where(here, tops[s], m_all)
            l_all = jnp.where(here, totals[s], l_all)
        out = n_buf.at[:, block(step)]
        for s in seqs:
            out[:, s, :] = sums[s]
        for c in stores(step):
            c.start()
        return m_all, l_all

    zero = jnp.zeros((q_rows, num_seqs), F32)
    m_all, l_all = lax.fori_loop(0, steps, step_fn, (zero, zero))
    ml_ref[0:q_rows] = m_all
    ml_ref[q_rows : 2 * q_rows] = l_all
    for step in range(steps):
        for c in stores(step):
            c.wait()


def attend(seq_lens, heads, sinks, k_rows, v_rows):
    num_seqs, rows, head_dim = k_rows.shape
    q_rows = sinks.shape[1]
    vmem = pl.BlockSpec(memory_space=pltpu.VMEM)
    anyspace = pl.BlockSpec(memory_space=pl.ANY)
    dma = pltpu.SemaphoreType.DMA((num_seqs // ATT_SEQS,))
    return pl.pallas_call(
        attend_kernel,
        in_specs=[pl.BlockSpec(memory_space=pltpu.SMEM), anyspace, vmem, anyspace, anyspace],
        out_specs=[anyspace, anyspace, anyspace, vmem],
        out_shape=[
            jax.ShapeDtypeStruct(k_rows.shape, BF16),
            jax.ShapeDtypeStruct(v_rows.shape, BF16),
            jax.ShapeDtypeStruct((q_rows, num_seqs, head_dim), F32),
            jax.ShapeDtypeStruct((2 * q_rows, num_seqs), F32),
        ],
        scratch_shapes=[
            pltpu.VMEM((num_seqs, rows, head_dim), BF16),
            pltpu.VMEM((num_seqs, rows, head_dim), BF16),
            pltpu.VMEM(heads.shape, F32),
            pltpu.VMEM((q_rows, num_seqs, head_dim), F32),
        ] + [dma] * 6,
        compiler_params=pltpu.CompilerParams(vmem_limit_bytes=60 << 20),
        name="attend",
    )(seq_lens, heads, sinks, k_rows, v_rows)


OUT_COLS = 256
SEQ_GROUPS = 2
W_PARTS = 4
LAG_Y = 6
LAG_X = 5


def finish_kernel(num_hbm, ml_ref, sink_ref, hid_ref, bo_ref, wo_ref, y_ref,
                  w_buf, x_buf, num, sink_col, bo_f32, r1, r1ml, own, away, away_ml, r2, r2ml, fac, o_buf, r3, o_all,
                  y_send, y_recv, z_buf, x_recv, p1, p2,
                  w_sem, h_sem, n_sem, s1_send, s1_recv, s2_send, s2_recv, s3_send, s3_recv, ml_send, ml_recv,
                  y_ss, y_rs, x_ss, x_rs, p1_ss, p1_rs, p2_ss, p2_rs):
    chip, core = sp_place()
    tp = lax.axis_index("tp")
    partner = {"sp": 2 * chip + (1 - core)}
    across_x = {"sp": 2 * (1 - chip) + core}
    across_y = {"tp": 1 - tp}
    q_rows, num_seqs, head_dim = num.shape
    half_h = q_rows // 2
    half_s = num_seqs // 2
    some = half_s // SEQ_GROUPS
    cols = w_buf.shape[1]
    chunks = cols // OUT_COLS
    total = SEQ_GROUPS * chunks
    mine = pl.multiple_of(core * half_h, half_h)
    theirs = pl.multiple_of((1 - core) * half_h, half_h)

    def seqs(which, g):
        return pl.ds(pl.multiple_of(which * half_s + g * some, some), some)

    barrier = pltpu.get_barrier_semaphore()
    for peer in (partner, across_x, across_y):
        pl.semaphore_signal(barrier, inc=1, device_id=peer, device_id_type=MESH)

    n_copies = []
    for i, h in enumerate((theirs, mine)):
        part = pl.ds(h, half_h)
        n_copies.append(pltpu.make_async_copy(num_hbm.at[part], num.at[part], n_sem.at[i]))
        n_copies[-1].start()
    my_cols = pl.ds(pl.multiple_of(core * cols, 128), cols)
    h_copy = pltpu.make_async_copy(hid_ref.at[pl.ds(pl.multiple_of(chip * half_s, half_s), half_s), my_cols], x_buf, h_sem)
    h_copy.start()
    w_cols = cols // W_PARTS
    w_chunks = w_cols // OUT_COLS

    def w_copy(p):
        return pltpu.make_async_copy(wo_ref.at[:, pl.ds(pl.multiple_of(core * cols + p * w_cols, 128), w_cols)], w_buf.at[:, pl.ds(pl.multiple_of(p * w_cols, 128), w_cols)], w_sem.at[p])

    sink_col[...] = jnp.broadcast_to(column(sink_ref, q_rows), sink_col.shape)
    bo_f32[...] = bo_ref[...].astype(F32)
    n_copies[0].wait()
    for p in range(W_PARTS):
        w_copy(p).start()
    pl.semaphore_wait(barrier, 3)

    c_ml = remote(ml_ref, r1ml, ml_send.at[0], ml_recv.at[0], partner)
    c_ml.start()
    c1 = []
    for g in range(SEQ_GROUPS):
        for i, which in enumerate((1 - chip, chip)):
            c1.append(remote(num.at[pl.ds(theirs, half_h), seqs(which, g)], r1.at[:, seqs(which, g)], s1_send.at[2 * g + i], s1_recv.at[2 * g + i], partner))
            c1[-1].start()

    c_ml.wait_recv()
    m_a, l_a = ml_ref[pl.ds(mine, half_h)], ml_ref[pl.ds(q_rows + mine, half_h)]
    m_b, l_b = r1ml[pl.ds(mine, half_h)], r1ml[pl.ds(q_rows + mine, half_h)]
    m_chip = jnp.maximum(m_a, m_b)
    f_a = jnp.exp(m_a - m_chip)
    f_b = jnp.exp(m_b - m_chip)
    l_chip = l_a * f_a + l_b * f_b
    fac[0] = f_a.T
    fac[1] = f_b.T
    away_ml[0:half_h] = m_chip
    away_ml[half_h : 2 * half_h] = l_chip
    n_copies[1].wait()

    c2_ml = remote(away_ml, r2ml, ml_send.at[1], ml_recv.at[1], across_x)
    c2 = []
    for g in range(SEQ_GROUPS):
        c1[2 * g].wait_recv()
        at = seqs(1 - chip, g)
        fa, fb = fac[0, at, :], fac[1, at, :]
        for h in range(half_h):
            away[g, h] = num[mine + h, at, :] * fa[:, h : h + 1] + r1[h, at, :] * fb[:, h : h + 1]
        if g == 0:
            c2_ml.start()
        c2.append(remote(away.at[g], r2.at[g], s2_send.at[g], s2_recv.at[g], across_x))
        c2[-1].start()
    for g in range(SEQ_GROUPS):
        c1[2 * g + 1].wait_recv()
        at = seqs(chip, g)
        fa, fb = fac[0, at, :], fac[1, at, :]
        for h in range(half_h):
            own[g, h] = num[mine + h, at, :] * fa[:, h : h + 1] + r1[h, at, :] * fb[:, h : h + 1]

    c2_ml.wait_recv()
    m_o, l_o = r2ml[0:half_h], r2ml[half_h : 2 * half_h]
    m_top = jnp.maximum(m_chip, m_o)
    f_a = jnp.exp(m_chip - m_top)
    f_b = jnp.exp(m_o - m_top)
    den = l_chip * f_a + l_o * f_b + jnp.exp(sink_col[pl.ds(mine, half_h)] - m_top)
    fac[2] = (f_a / den).T
    fac[3] = (f_b / den).T
    width = half_h * head_dim

    def heads_start(g):
        at = seqs(chip, g)
        fa, fb = fac[2, at, :], fac[3, at, :]
        c2[g].wait_recv()
        for h in range(half_h):
            o_buf[g, :, h * head_dim : (h + 1) * head_dim] = own[g, h] * fa[:, h : h + 1] + r2[g, h] * fb[:, h : h + 1]
        c = remote(o_buf.at[g], r3.at[g], s3_send.at[g], s3_recv.at[g], partner)
        c.start()
        o_all[g, :, pl.ds(pl.multiple_of(core * width, 128), width)] = o_buf[g].astype(BF16)
        return c

    def heads_end(g, c):
        c.wait_recv()
        o_all[g, :, pl.ds(pl.multiple_of((1 - core) * width, 128), width)] = r3[g].astype(BF16)

    def y_copy(t):
        return remote(y_send.at[t], y_recv.at[t], y_ss.at[t], y_rs.at[t], across_y)

    def x_copy(t):
        return remote(z_buf.at[t], x_recv.at[t], x_ss.at[t], x_rs.at[t], across_x)

    def p1_copy(t):
        return remote(z_buf.at[t], p1.at[t], p1_ss.at[t], p1_rs.at[t], partner)

    def p2_copy(t):
        return remote(x_recv.at[t], p2.at[t], p2_ss.at[t], p2_rs.at[t], partner)

    def place(which_seqs, which_cols, t):
        g, j = lax.div(t, chunks), lax.rem(t, chunks)
        return seqs(which_seqs, g), pl.ds(pl.multiple_of(which_cols * cols + j * OUT_COLS, 128), OUT_COLS)

    def body(t, _):
        @pl.when(t < total)
        def _():
            g, j = lax.div(t, chunks), lax.rem(t, chunks)

            @pl.when(jnp.logical_and(g == 0, lax.rem(j, w_chunks) == 0))
            def _():
                w_copy(lax.div(j, w_chunks)).wait()

            w = w_buf[:, pl.ds(pl.multiple_of(j * OUT_COLS, 128), OUT_COLS)]
            y_send[t] = jnp.dot(o_all[g], w, preferred_element_type=F32)
            y_copy(t).start()

        @pl.when(jnp.logical_and(t >= LAG_Y, t < total + LAG_Y))
        def _():
            u = t - LAG_Y
            g, j = lax.div(u, chunks), lax.rem(u, chunks)
            y_copy(u).wait_recv()
            x_part = x_buf[pl.ds(pl.multiple_of(g * some, some), some), pl.ds(pl.multiple_of(j * OUT_COLS, 128), OUT_COLS)].astype(F32)
            row = (core * cols + j * OUT_COLS) // head_dim
            bias = jnp.concatenate([bo_f32[pl.ds(row + i, 1), :] for i in range(OUT_COLS // head_dim)], axis=1)
            z = (x_part + (y_send[u] + y_recv[u]) + bias).astype(BF16)
            z_buf[u] = z.astype(F32)
            x_copy(u).start()
            p1_copy(u).start()
            rows_at, cols_at = place(chip, core, u)
            y_ref[rows_at, cols_at] = z

        @pl.when(t >= LAG_Y + LAG_X)
        def _():
            u = t - (LAG_Y + LAG_X)
            x_copy(u).wait_recv()
            p2_copy(u).start()
            rows_at, cols_at = place(1 - chip, core, u)
            y_ref[rows_at, cols_at] = x_recv[u].astype(BF16)
            p1_copy(u).wait_recv()
            rows_at, cols_at = place(chip, 1 - core, u)
            y_ref[rows_at, cols_at] = p1[u].astype(BF16)

        return 0

    c3 = [heads_start(0)]
    heads_end(0, c3[0])
    h_copy.wait()
    lax.fori_loop(0, 8, body, 0)
    c3.append(heads_start(1))
    lax.fori_loop(8, 12, body, 0)
    heads_end(1, c3[1])
    lax.fori_loop(12, total + LAG_Y + LAG_X, body, 0)

    def tail(t, _):
        p2_copy(t).wait_recv()
        rows_at, cols_at = place(1 - chip, 1 - core, t)
        y_ref[rows_at, cols_at] = p2[t].astype(BF16)
        y_copy(t).wait_send()
        x_copy(t).wait_send()
        p1_copy(t).wait_send()
        p2_copy(t).wait_send()
        return 0

    lax.fori_loop(0, total, tail, 0)
    for c in (c_ml, c2_ml, *c1, *c2, *c3):
        c.wait_send()


def finish(num, ml, sinks, hidden, b_o, w_o):
    q_rows, num_seqs, head_dim = num.shape
    half_h, half_s = q_rows // 2, num_seqs // 2
    some = half_s // SEQ_GROUPS
    width = w_o.shape[1]
    cols = width // 2
    total = SEQ_GROUPS * (cols // OUT_COLS)
    vmem = pl.BlockSpec(memory_space=pltpu.VMEM)
    anyspace = pl.BlockSpec(memory_space=pl.ANY)
    chunked = pltpu.VMEM((total, some, OUT_COLS), F32)
    dma = pltpu.SemaphoreType.DMA
    return pl.pallas_call(
        finish_kernel,
        out_shape=jax.ShapeDtypeStruct((num_seqs, width), BF16),
        in_specs=[anyspace, vmem, vmem, anyspace, vmem, anyspace],
        out_specs=vmem,
        scratch_shapes=[
            pltpu.VMEM((w_o.shape[0], cols), BF16),
            pltpu.VMEM((half_s, cols), BF16),
            pltpu.VMEM(num.shape, F32),
            pltpu.VMEM((q_rows, num_seqs), F32),
            pltpu.VMEM((width // head_dim, head_dim), F32),
            pltpu.VMEM((half_h, num_seqs, head_dim), F32),
            pltpu.VMEM((2 * q_rows, num_seqs), F32),
            pltpu.VMEM((SEQ_GROUPS, half_h, some, head_dim), F32),
            pltpu.VMEM((SEQ_GROUPS, half_h, some, head_dim), F32),
            pltpu.VMEM((2 * half_h, num_seqs), F32),
            pltpu.VMEM((SEQ_GROUPS, half_h, some, head_dim), F32),
            pltpu.VMEM((2 * half_h, num_seqs), F32),
            pltpu.VMEM((4, num_seqs, half_h), F32),
            pltpu.VMEM((SEQ_GROUPS, some, half_h * head_dim), F32),
            pltpu.VMEM((SEQ_GROUPS, some, half_h * head_dim), F32),
            pltpu.VMEM((SEQ_GROUPS, some, q_rows * head_dim), BF16),
            chunked, chunked, chunked, chunked, chunked, chunked,
            dma((W_PARTS,)), dma, dma((2,)),
            dma((2 * SEQ_GROUPS,)), dma((2 * SEQ_GROUPS,)),
            dma((SEQ_GROUPS,)), dma((SEQ_GROUPS,)),
            dma((SEQ_GROUPS,)), dma((SEQ_GROUPS,)),
            dma((2,)), dma((2,)),
            *[dma((total,))] * 8,
        ],
        compiler_params=pltpu.CompilerParams(collective_id=1, has_side_effects=True, vmem_limit_bytes=56 << 20),
        name="finish",
    )(num, ml, sinks, hidden, b_o.reshape(width // head_dim, head_dim), w_o)


def solution(mesh):
    cache_spec = P("dp", "sp", "tp", None)

    def block_step(hidden, seq_lens, rope_cos, rope_sin, k_cache, v_cache, norm_gain, w_qkv, b_qkv, sink_logits, w_o, b_o):
        num_seqs, ctx_local, kv_local, head_dim = k_cache.shape
        heads = qkv_heads(hidden, rope_cos, rope_sin, norm_gain, w_qkv, b_qkv, head_dim)
        sinks = sink_logits.reshape(1, sink_logits.shape[0])
        rows = (num_seqs, ctx_local * kv_local, head_dim)
        k_out, v_out, num, ml = attend(seq_lens, heads, sinks, k_cache.reshape(rows), v_cache.reshape(rows))
        out_hidden = finish(num, ml, sinks, hidden, b_o, w_o)
        return out_hidden, k_out.reshape(k_cache.shape), v_out.reshape(v_cache.shape)

    return jax.shard_map(block_step, mesh=mesh, in_specs=(P("dp", None), P("dp"), P("dp", None), P("dp", None), cache_spec, cache_spec, P(None), P(None, "tp", None), P("tp", None), P("tp"), P("tp", None), P(None)), out_specs=(P("dp", None), cache_spec, cache_spec), check_vma=False)
```

time: 106 us -> 96.7 us (0.912)
  Pallas kernels: 102 us -> 92.7 us
    pallas_call x1, Pallas kernels: 53.3 us -> 47.8 us  [finish(): pl.pallas_call(finish_kernel, out_shape=jax.ShapeDtypeStruct((num_seqs, w...]
    pallas_call x1, Pallas kernels: 19.3 us -> 15.5 us  [attend(): pl.pallas_call(attend_kernel, in_specs=[pl.BlockSpec(memory_space=pltpu.S...]
where the time goes in v3:
time: 96.7 us; the launch traced here: 96.4 us
  Pallas kernels  92.7 us (96%)
  local copies, waits for them, and re-layouts  3.1 us (3%)
    pallas_call x1, Pallas kernels, finish(): pl.pallas_call(finish_kernel, out_shape=jax.ShapeDtypeStruct((num_seqs, w...  47.8 us
    pallas_call x1, Pallas kernels, qkv_heads(): pl.pallas_call(qkv_kernel, out_shape=jax.ShapeDtypeStruct((rows, num_seqs...  29.3 us
    pallas_call x1, Pallas kernels, attend(): pl.pallas_call(attend_kernel, in_specs=[pl.BlockSpec(memory_space=pltpu.S...  15.5 us
    unnamed x1, local copies, waits for them, and re-layouts  3.1 us

profile of v3, /device:TPU:0, one launch (start us, length us, event | category | flops | bytes accessed | tf_op | source)
XLA Modules:
  0.0 96.4 jit_solution(6225718951614328026)
XLA Ops:
  0.6 29.3 %qkv_heads.1.heads_ref = f32[40,128,128]{2,1,0:T(8,128)} custom-call(bf16[128,8192]{1,0:T(8,128)(2,1)} %hid_ref.1, bf16[64,128]{1,0:T(8,128)(2,1)} %bitcast.13, f32[64,128]{1,0:T(8,128)} %bitcast.11, f32[64,128]{1,0:T(8,128)} %bitcast.12, bf16[4,1280]{1,0:T(4,128)(2,1)} %bias_ref.1, bf16[8192,4,1280]{2,1,0:T(4,128)(2,1)} %w_ref.1), custom_call_target="tpu_custom_call" | custom-call | tf_op jit(solution)/shard_map/qkv_heads/pallas_call | solution.py:136
  30.0 15.5 %attend.1 = (bf16[128,256,128]{2,1,0:T(8,128)(2,1)}, bf16[128,256,128]{2,1,0:T(8,128)(2,1)}, f32[32,128,128]{2,1,0:T(8,128)}, f32[64,128]{1,0:T(8,128)}) custom-call(s32[128]{0:T(128)} %lens_ref.1, f32[40,128,128]{2,1,0:T(8,128)} %qkv_heads.1.heads_ref, f32[1,32]{1,0:T(1,128)} %bitcast.15, bf16[128,256,128]{2,1,0:T(8,128)(2,1)} %bitcast.9, ...), custom_call_target="tpu_custom_call" | custom-call | tf_op jit(solution)/shard_map/attend/pallas_call | solution.py:256
  45.5 47.8 %finish.1 = bf16[128,8192]{1,0:T(8,128)(2,1)} custom-call(f32[32,128,128]{2,1,0:T(8,128)} %get-tuple-element.7.num_hbm, f32[64,128]{1,0:T(8,128)} %get-tuple-element.8.ml_ref, f32[1,32]{1,0:T(1,128)} %bitcast.16, bf16[128,8192]{1,0:T(8,128)(2,1)} %hid_ref.1, bf16[64,128]{1,0:T(8,128)(2,1)} %bitcast.14, bf16[4096,8192]{1,0:T(8,128)(2,1)} %wo_ref.1), custom_call_target="tpu_custom_call" | custom-call | tf_op jit(solution)/shard_map/finish/pallas_call | solution.py:489
  93.3 3.1 %copy.16 = bf16[128,8192]{1,0:T(8,128)(2,1)} copy(bf16[128,8192]{1,0:T(8,128)(2,1)} %finish.1) | data formatting | bytes 4194304

commit v4 on v3

v4 whole, which is shorter than its diff:
```python
import functools

import jax
import jax.numpy as jnp
from jax import lax
from jax.experimental import pallas as pl
from jax.experimental.pallas import tpu as pltpu
from jax.sharding import PartitionSpec as P

NORM_EPS = 1e-5
F32 = jnp.float32
BF16 = jnp.bfloat16
MESH = pl.DeviceIdType.MESH


def sp_place():
    sp = lax.axis_index("sp")
    return lax.div(sp, 2), lax.rem(sp, 2)


def remote(src, dst, send_sem, recv_sem, where):
    return pltpu.make_async_remote_copy(src_ref=src, dst_ref=dst, send_sem=send_sem, recv_sem=recv_sem, device_id=where, device_id_type=MESH)


def sink_column(row_ref, count, halves, group):
    row = lax.broadcasted_iota(jnp.int32, (count, count), 0)
    per_half = count // halves
    part = group // halves
    head = lax.div(lax.rem(row, per_half), part) * group + lax.div(row, per_half) * part + lax.rem(row, part)
    same = head == lax.broadcasted_iota(jnp.int32, (count, count), 1)
    return jnp.sum(jnp.where(same, jnp.broadcast_to(row_ref[...], (count, count)), 0.0), axis=1, keepdims=True)


QKV_ROWS = 512
QKV_SLOTS = 3
CACHE_SEQS = 8
CACHE_AHEAD = 4


def project_kernel(x_ref, gain_ref, cos_ref, sin_ref, bias_ref, w_ref, k_ref, v_ref, out_ref, k_out, v_out,
                   normed, gain, heads, acc_q, acc_e, wq_buf, we_buf, k_buf, v_buf, wq_sem, we_sem, out_sem, k_in, v_in, k_back, v_back):
    _, core = sp_place()
    num_seqs, depth = x_ref.shape
    head_dim = acc_e.shape[2]
    q_cols = acc_q.shape[2]
    kv_local = acc_q.shape[0]
    per_core = q_cols // head_dim
    group = 2 * per_core
    steps = depth // QKV_ROWS
    blocks = num_seqs // CACHE_SEQS

    def fetch(step, slot):
        rows = pl.ds(step * QKV_ROWS, QKV_ROWS)
        cq = pltpu.make_async_copy(w_ref.at[rows, :, pl.ds(pl.multiple_of(core * q_cols, 128), q_cols)], wq_buf.at[slot], wq_sem.at[slot])
        ce = pltpu.make_async_copy(w_ref.at[rows, :, pl.ds(pl.multiple_of((group + core) * head_dim, 128), head_dim)], we_buf.at[slot], we_sem.at[slot])
        return cq, ce

    def cache_in(i):
        at = pl.ds(i * CACHE_SEQS, CACHE_SEQS)
        return pltpu.make_async_copy(k_ref.at[at], k_buf.at[at], k_in.at[i]), pltpu.make_async_copy(v_ref.at[at], v_buf.at[at], v_in.at[i])

    def cache_back(i):
        at = pl.ds(i * CACHE_SEQS, CACHE_SEQS)
        return pltpu.make_async_copy(k_buf.at[at], k_out.at[at], k_back.at[i]), pltpu.make_async_copy(v_buf.at[at], v_out.at[at], v_back.at[i])

    for s in range(QKV_SLOTS - 1):
        for c in fetch(s, s):
            c.start()
    for i in range(CACHE_AHEAD):
        for c in cache_in(i):
            c.start()

    gain[...] = gain_ref[...].astype(F32)

    def norm_rows(r, _):
        rows = pl.ds(pl.multiple_of(r * 16, 16), 16)
        xw = x_ref[rows, :].astype(F32)
        inv = lax.rsqrt(jnp.mean(xw * xw, axis=-1, keepdims=True) + NORM_EPS)
        for t in range(depth // head_dim):
            cols = slice(t * head_dim, (t + 1) * head_dim)
            normed[rows, cols] = (xw[:, cols] * inv * gain[t : t + 1, :]).astype(BF16)
        return 0

    lax.fori_loop(0, num_seqs // 16, norm_rows, 0)
    acc_q[...] = jnp.zeros_like(acc_q)
    acc_e[...] = jnp.zeros_like(acc_e)

    def step_fn(step, _):
        slot = lax.rem(step, QKV_SLOTS)

        @pl.when(step + CACHE_AHEAD < blocks)
        def _():
            for c in cache_in(step + CACHE_AHEAD):
                c.start()

        for c in fetch(step, slot):
            c.wait()

        @pl.when(step + QKV_SLOTS - 1 < steps)
        def _():
            for c in fetch(step + QKV_SLOTS - 1, lax.rem(step + QKV_SLOTS - 1, QKV_SLOTS)):
                c.start()

        for c in cache_in(step):
            c.wait()
        for c in cache_back(step):
            c.start()

        h = normed[:, pl.ds(pl.multiple_of(step * QKV_ROWS, 128), QKV_ROWS)]
        wq = jnp.swapaxes(wq_buf[slot], 0, 1)
        we = jnp.swapaxes(we_buf[slot], 0, 1)
        for k in range(kv_local):
            acc_q[k] += jnp.dot(h, wq[k], preferred_element_type=F32)
            acc_e[k] += jnp.dot(h, we[k], preferred_element_type=F32)
        return 0

    lax.fori_loop(0, steps, step_fn, 0)

    cos_t = cos_ref[...].T
    sin_t = sin_ref[...].T
    cos2 = jnp.concatenate([cos_t, cos_t], axis=1)
    sin2 = jnp.concatenate([-sin_t, sin_t], axis=1)
    is_key = core == 0
    cos_e = jnp.where(is_key, cos2, jnp.ones_like(cos2))
    sin_e = jnp.where(is_key, sin2, jnp.zeros_like(sin2))

    def rotate(v, c, s):
        r = v * c + pltpu.roll(v, head_dim // 2, 1) * s
        return r.astype(BF16).astype(F32)

    for k in range(kv_local):
        bias_q = bias_ref[k : k + 1, pl.ds(pl.multiple_of(core * q_cols, 128), q_cols)].astype(F32)
        for g in range(per_core):
            cols = slice(g * head_dim, (g + 1) * head_dim)
            heads[k * per_core + g] = rotate(acc_q[k, :, cols] + bias_q[:, cols], cos2, sin2)
        bias_e = bias_ref[k : k + 1, pl.ds(pl.multiple_of((group + core) * head_dim, 128), head_dim)].astype(F32)
        heads[kv_local * per_core + k] = rotate(acc_e[k] + bias_e, cos_e, sin_e)
    done = pltpu.make_async_copy(heads, out_ref, out_sem)
    done.start()
    for i in range(blocks):
        for c in cache_back(i):
            c.wait()
    done.wait()


def project(hidden, rope_cos, rope_sin, norm_gain, w_qkv, b_qkv, k_rows, v_rows):
    num_seqs, depth = hidden.shape
    head_dim = k_rows.shape[2]
    kv_local = w_qkv.shape[1]
    per_core = (w_qkv.shape[2] // head_dim - 2) // 2
    rows = kv_local * (per_core + 1)
    blocks = num_seqs // CACHE_SEQS
    assert blocks == depth // QKV_ROWS
    vmem = pl.BlockSpec(memory_space=pltpu.VMEM)
    anyspace = pl.BlockSpec(memory_space=pl.ANY)
    dma = pltpu.SemaphoreType.DMA
    return pl.pallas_call(
        project_kernel,
        out_shape=[
            jax.ShapeDtypeStruct((rows, num_seqs, head_dim), F32),
            jax.ShapeDtypeStruct(k_rows.shape, BF16),
            jax.ShapeDtypeStruct(v_rows.shape, BF16),
        ],
        in_specs=[vmem] * 5 + [anyspace] * 3,
        out_specs=[anyspace] * 3,
        scratch_shapes=[
            pltpu.VMEM((num_seqs, depth), BF16),
            pltpu.VMEM((depth // head_dim, head_dim), F32),
            pltpu.VMEM((rows, num_seqs, head_dim), F32),
            pltpu.VMEM((kv_local, num_seqs, per_core * head_dim), F32),
            pltpu.VMEM((kv_local, num_seqs, head_dim), F32),
            pltpu.VMEM((QKV_SLOTS, QKV_ROWS, kv_local, per_core * head_dim), BF16),
            pltpu.VMEM((QKV_SLOTS, QKV_ROWS, kv_local, head_dim), BF16),
            pltpu.VMEM(k_rows.shape, BF16),
            pltpu.VMEM(v_rows.shape, BF16),
            dma((QKV_SLOTS,)), dma((QKV_SLOTS,)), dma,
            dma((blocks,)), dma((blocks,)), dma((blocks,)), dma((blocks,)),
        ],
        compiler_params=pltpu.CompilerParams(vmem_limit_bytes=60 << 20),
        name="project",
    )(hidden, norm_gain.reshape(depth // head_dim, head_dim), rope_cos.T, rope_sin.T, b_qkv, w_qkv, k_rows, v_rows)


ATT_SEQS = 8
ATT_SLOTS = 5
OUT_COLS = 256
SEQ_GROUPS = 2
W_PARTS = 4
LAG_Y = 6
LAG_X = 5


def finish_kernel(lens_ref, half_hbm, sink_ref, hid_ref, bo_ref, wo_ref, k_hbm, v_hbm, y_ref, new_ref,
                  w_buf, x_buf, h_buf, k_ring, v_ring, pos_ref, num, ml, sink_col, bo_f32, r1, r1ml, own, own_ml, away, away_ml, r2, r2ml, o_buf, r3, o_all,
                  y_send, y_recv, z_buf, x_recv, p1, p2,
                  w_sem, x_sem, k_sem, v_sem, h_in, h_send, h_recv, s1_send, s1_recv, s2_send, s2_recv, s3_send, s3_recv,
                  y_ss, y_rs, x_ss, x_rs, p1_ss, p1_rs, p2_ss, p2_rs):
    chip, core = sp_place()
    tp = lax.axis_index("tp")
    partner = {"sp": 2 * chip + (1 - core)}
    across_x = {"sp": 2 * (1 - chip) + core}
    across_y = {"tp": 1 - tp}
    groups, q_rows, some, head_dim = num.shape
    num_seqs = h_buf.shape[1]
    kv_local = (h_buf.shape[0] - q_rows) // 2
    rows = k_ring.shape[2]
    ctx_local = rows // kv_local
    half_h = q_rows // 2
    half_s = num_seqs // 2
    part_h = half_h // kv_local
    cols = w_buf.shape[1]
    chunks = cols // OUT_COLS
    total = SEQ_GROUPS * chunks
    mine = pl.multiple_of(core * half_h, half_h)
    theirs = pl.multiple_of((1 - core) * half_h, half_h)

    def seqs(which, g):
        return pl.ds(pl.multiple_of(which * half_s + g * some, some), some)

    barrier = pltpu.get_barrier_semaphore()
    for peer in (partner, across_x, across_y):
        pl.semaphore_signal(barrier, inc=1, device_id=peer, device_id_type=MESH)

    order = [(1 - chip, g) for g in range(SEQ_GROUPS)] + [(chip, g) for g in range(SEQ_GROUPS)]
    own_rows = (pl.ds(mine, half_h), pl.ds(pl.multiple_of(q_rows + kv_local * core, kv_local), kv_local))
    src_rows = (pl.ds(0, half_h), pl.ds(half_h, kv_local))
    h_local, h_remote = [], []
    for i, (which, g) in enumerate(order):
        at = seqs(which, g)
        for j in range(2):
            h_local.append(pltpu.make_async_copy(half_hbm.at[src_rows[j], at], h_buf.at[own_rows[j], at], h_in.at[2 * i + j]))
            h_local[-1].start()
            h_remote.append(remote(half_hbm.at[src_rows[j], at], h_buf.at[own_rows[j], at], h_send.at[2 * i + j], h_recv.at[2 * i + j], partner))

    steps = num_seqs // ATT_SEQS
    per_group = some // ATT_SEQS

    def block(p):
        return lax.rem(p + (1 - chip) * (steps // 2), steps) * ATT_SEQS

    def kv_load(p):
        at = pl.ds(pl.multiple_of(block(p), ATT_SEQS), ATT_SEQS)
        slot = lax.rem(p, ATT_SLOTS)
        return pltpu.make_async_copy(k_hbm.at[at], k_ring.at[slot], k_sem.at[slot]), pltpu.make_async_copy(v_hbm.at[at], v_ring.at[slot], v_sem.at[slot])

    for p in range(ATT_SLOTS):
        for c in kv_load(p):
            c.start()
    my_cols = pl.ds(pl.multiple_of(core * cols, 128), cols)
    x_copy_in = pltpu.make_async_copy(hid_ref.at[pl.ds(pl.multiple_of(chip * half_s, half_s), half_s), my_cols], x_buf, x_sem)
    w_cols = cols // W_PARTS
    w_chunks = w_cols // OUT_COLS

    def w_copy(p):
        return pltpu.make_async_copy(wo_ref.at[:, pl.ds(pl.multiple_of(core * cols + p * w_cols, 128), w_cols)], w_buf.at[:, pl.ds(pl.multiple_of(p * w_cols, 128), w_cols)], w_sem.at[p])

    sink = sink_column(sink_ref, q_rows, 2, 2 * part_h)
    sink_col[...] = jnp.broadcast_to(sink, sink_col.shape)
    bo_f32[...] = bo_ref[...].astype(F32)
    pos_ref[...] = lax.div(lax.broadcasted_iota(jnp.int32, pos_ref.shape, 0), kv_local).astype(F32).astype(BF16)
    pl.semaphore_wait(barrier, 3)
    for c in h_remote:
        c.start()

    base = lax.axis_index("sp") * ctx_local
    scale = head_dim**-0.5
    col = lax.broadcasted_iota(jnp.int32, (q_rows, rows), 1)
    kv_row = lax.div(lax.rem(lax.broadcasted_iota(jnp.int32, (q_rows, rows), 0), half_h), part_h)
    col_pos = jnp.where(lax.rem(col, kv_local) == kv_row, lax.div(col, kv_local), ctx_local * 1024)
    lane = lax.broadcasted_iota(jnp.int32, (q_rows, ml.shape[2]), 1)
    batch = range(ATT_SEQS)

    def attend(i, first, last, carry):
        def step_fn(t, carry):
            m_all, l_all = carry
            p = i * per_group + t
            slot = lax.rem(p, ATT_SLOTS)
            for c in kv_load(p):
                c.wait()
            start = block(p)
            heads = h_buf.at[:, pl.ds(pl.multiple_of(start, ATT_SEQS), ATT_SEQS)]
            rel = [lens_ref[start + s] - base for s in batch]
            keys, values = [], []
            for s in batch:
                n = jnp.full((16, head_dim), rel[s].astype(F32)).astype(BF16)
                hit = pos_ref[...].reshape(rows // 16, 16, head_dim) == n[None]
                for j, (ring, out) in enumerate(((k_ring, keys), (v_ring, values))):
                    new = heads[q_rows + j * kv_local : q_rows + (j + 1) * kv_local, s, :].astype(BF16)
                    new_ref[j, start + s] = new
                    new = jnp.concatenate([new] * (16 // kv_local), axis=0)
                    old = ring[slot, s].reshape(rows // 16, 16, head_dim)
                    out.append(jnp.where(hit, new[None], old).reshape(rows, head_dim))
            queries = [heads[0:q_rows, s, :].astype(BF16) for s in batch]
            logits = [lax.dot_general(queries[s], keys[s], (((1,), (1,)), ((), ())), preferred_element_type=F32) for s in batch]
            logits = [jnp.where(col_pos <= rel[s], logits[s] * scale, -jnp.inf) for s in batch]
            tops = [jnp.maximum(jnp.max(logits[s], axis=1, keepdims=True), sink) for s in batch]
            weights = [jnp.exp(logits[s] - tops[s]) for s in batch]
            totals = [jnp.sum(weights[s], axis=1, keepdims=True) for s in batch]
            sums = [jnp.dot(weights[s].astype(BF16), values[s], preferred_element_type=F32) for s in batch]
            out = num.at[i, :, pl.ds(pl.multiple_of(t * ATT_SEQS, ATT_SEQS), ATT_SEQS)]
            for s in batch:
                here = lane == t * ATT_SEQS + s
                m_all = jnp.where(here, tops[s], m_all)
                l_all = jnp.where(here, totals[s], l_all)
                out[:, s, :] = sums[s]

            @pl.when(p + ATT_SLOTS < steps)
            def _():
                for c in kv_load(p + ATT_SLOTS):
                    c.start()

            return m_all, l_all

        return lax.fori_loop(first, last, step_fn, carry)

    def heads_wait(i):
        for j in range(2):
            h_local[2 * i + j].wait()
            h_remote[2 * i + j].wait_recv()

    zero = jnp.zeros((q_rows, ml.shape[2]), F32)
    c1 = []

    def to_partner(i, carry):
        ml[i, 0:q_rows] = carry[0]
        ml[i, q_rows : 2 * q_rows] = carry[1]
        c1.append((
            remote(ml.at[i], r1ml.at[i], s1_send.at[2 * i], s1_recv.at[2 * i], partner),
            remote(num.at[i, pl.ds(theirs, half_h)], r1.at[i], s1_send.at[2 * i + 1], s1_recv.at[2 * i + 1], partner),
        ))
        for c in c1[-1]:
            c.start()

    def combine(i, dst, dst_ml):
        for c in c1[i]:
            c.wait_recv()
        m_a, l_a = ml[i, pl.ds(mine, half_h)], ml[i, pl.ds(q_rows + mine, half_h)]
        m_b, l_b = r1ml[i, pl.ds(mine, half_h)], r1ml[i, pl.ds(q_rows + mine, half_h)]
        m_chip = jnp.maximum(m_a, m_b)
        f_a = jnp.exp(m_a - m_chip)
        f_b = jnp.exp(m_b - m_chip)
        dst_ml[0:half_h] = m_chip
        dst_ml[half_h : 2 * half_h] = l_a * f_a + l_b * f_b
        f_a, f_b = f_a.T, f_b.T
        for h in range(half_h):
            dst[h] = num[i, mine + h] * f_a[0:some, h : h + 1] + r1[i, h] * f_b[0:some, h : h + 1]

    c2 = []

    def across(g):
        combine(g, away.at[g], away_ml.at[g])
        c2.append((
            remote(away_ml.at[g], r2ml.at[g], s2_send.at[2 * g], s2_recv.at[2 * g], across_x),
            remote(away.at[g], r2.at[g], s2_send.at[2 * g + 1], s2_recv.at[2 * g + 1], across_x),
        ))
        for c in c2[-1]:
            c.start()

    width = half_h * head_dim
    part_w = part_h * head_dim

    def o_place(which_half, k):
        return pl.ds(pl.multiple_of(2 * k * part_w + which_half * part_w, 128), part_w)

    def heads_start(g):
        for c in c2[g]:
            c.wait_recv()
        m_a, l_a = own_ml[g, 0:half_h], own_ml[g, half_h : 2 * half_h]
        m_b, l_b = r2ml[g, 0:half_h], r2ml[g, half_h : 2 * half_h]
        m_top = jnp.maximum(m_a, m_b)
        f_a = jnp.exp(m_a - m_top)
        f_b = jnp.exp(m_b - m_top)
        den = l_a * f_a + l_b * f_b + jnp.exp(sink_col[pl.ds(mine, half_h)] - m_top)
        f_a, f_b = (f_a / den).T, (f_b / den).T
        for h in range(half_h):
            o_buf[g, :, h * head_dim : (h + 1) * head_dim] = own[g, h] * f_a[0:some, h : h + 1] + r2[g, h] * f_b[0:some, h : h + 1]
        c = remote(o_buf.at[g], r3.at[g], s3_send.at[g], s3_recv.at[g], partner)
        c.start()
        for k in range(kv_local):
            o_all[g, :, o_place(core, k)] = o_buf[g, :, k * part_w : (k + 1) * part_w].astype(BF16)
        return c

    def heads_end(g, c):
        c.wait_recv()
        for k in range(kv_local):
            o_all[g, :, o_place(1 - core, k)] = r3[g, :, k * part_w : (k + 1) * part_w].astype(BF16)

    def y_copy(t):
        return remote(y_send.at[t], y_recv.at[t], y_ss.at[t], y_rs.at[t], across_y)

    def x_copy(t):
        return remote(z_buf.at[t], x_recv.at[t], x_ss.at[t], x_rs.at[t], across_x)

    def p1_copy(t):
        return remote(z_buf.at[t], p1.at[t], p1_ss.at[t], p1_rs.at[t], partner)

    def p2_copy(t):
        return remote(x_recv.at[t], p2.at[t], p2_ss.at[t], p2_rs.at[t], partner)

    def place(which_seqs, which_cols, t):
        g, j = lax.div(t, chunks), lax.rem(t, chunks)
        return seqs(which_seqs, g), pl.ds(pl.multiple_of(which_cols * cols + j * OUT_COLS, 128), OUT_COLS)

    def body(t, _):
        @pl.when(t < total)
        def _():
            g, j = lax.div(t, chunks), lax.rem(t, chunks)

            @pl.when(jnp.logical_and(g == 0, lax.rem(j, w_chunks) == 0))
            def _():
                w_copy(lax.div(j, w_chunks)).wait()

            w = w_buf[:, pl.ds(pl.multiple_of(j * OUT_COLS, 128), OUT_COLS)]
            y_send[t] = jnp.dot(o_all[g], w, preferred_element_type=F32)
            y_copy(t).start()

        @pl.when(jnp.logical_and(t >= LAG_Y, t < total + LAG_Y))
        def _():
            u = t - LAG_Y
            g, j = lax.div(u, chunks), lax.rem(u, chunks)
            y_copy(u).wait_recv()
            x_part = x_buf[pl.ds(pl.multiple_of(g * some, some), some), pl.ds(pl.multiple_of(j * OUT_COLS, 128), OUT_COLS)].astype(F32)
            row = (core * cols + j * OUT_COLS) // head_dim
            bias = jnp.concatenate([bo_f32[pl.ds(row + i, 1), :] for i in range(OUT_COLS // head_dim)], axis=1)
            z = (x_part + (y_send[u] + y_recv[u]) + bias).astype(BF16)
            z_buf[u] = z.astype(F32)
            x_copy(u).start()
            p1_copy(u).start()
            rows_at, cols_at = place(chip, core, u)
            y_ref[rows_at, cols_at] = z

        @pl.when(t >= LAG_Y + LAG_X)
        def _():
            u = t - (LAG_Y + LAG_X)
            x_copy(u).wait_recv()
            p2_copy(u).start()
            rows_at, cols_at = place(1 - chip, core, u)
            y_ref[rows_at, cols_at] = x_recv[u].astype(BF16)
            p1_copy(u).wait_recv()
            rows_at, cols_at = place(chip, 1 - core, u)
            y_ref[rows_at, cols_at] = p1[u].astype(BF16)

        return 0

    half_group = per_group // 2
    heads_wait(0)
    carry = attend(0, 0, per_group, (zero, zero))
    to_partner(0, carry)
    x_copy_in.start()
    for p in range(W_PARTS // 2):
        w_copy(p).start()
    heads_wait(1)
    carry = attend(1, 0, half_group, (zero, zero))
    across(0)
    carry = attend(1, half_group, per_group, carry)
    to_partner(1, carry)
    for p in range(W_PARTS // 2, W_PARTS):
        w_copy(p).start()
    heads_wait(2)
    carry = attend(2, 0, half_group, (zero, zero))
    across(1)
    carry = attend(2, half_group, per_group, carry)
    to_partner(2, carry)
    heads_wait(3)
    carry = attend(3, 0, per_group, (zero, zero))
    to_partner(3, carry)
    combine(2, own.at[0], own_ml.at[0])
    combine(3, own.at[1], own_ml.at[1])

    c3 = [heads_start(0)]
    heads_end(0, c3[0])
    x_copy_in.wait()
    lax.fori_loop(0, 8, body, 0)
    c3.append(heads_start(1))
    lax.fori_loop(8, 12, body, 0)
    heads_end(1, c3[1])
    lax.fori_loop(12, total + LAG_Y + LAG_X, body, 0)

    def tail(t, _):
        p2_copy(t).wait_recv()
        rows_at, cols_at = place(1 - chip, 1 - core, t)
        y_ref[rows_at, cols_at] = p2[t].astype(BF16)
        y_copy(t).wait_send()
        x_copy(t).wait_send()
        p1_copy(t).wait_send()
        p2_copy(t).wait_send()
        return 0

    lax.fori_loop(0, total, tail, 0)
    for c in (*h_remote, *(c for pair in c1 + c2 for c in pair), *c3):
        c.wait_send()


def finish(seq_lens, half, sinks, hidden, b_o, w_o, k_rows, v_rows):
    num_seqs, rows, head_dim = k_rows.shape
    q_rows = sinks.shape[1]
    half_h, half_s = q_rows // 2, num_seqs // 2
    kv_local = half.shape[0] - half_h
    some = half_s // SEQ_GROUPS
    groups = 2 * SEQ_GROUPS
    width = w_o.shape[1]
    cols = width // 2
    total = SEQ_GROUPS * (cols // OUT_COLS)
    vmem = pl.BlockSpec(memory_space=pltpu.VMEM)
    anyspace = pl.BlockSpec(memory_space=pl.ANY)
    chunked = pltpu.VMEM((total, some, OUT_COLS), F32)
    parts = pltpu.VMEM((SEQ_GROUPS, half_h, some, head_dim), F32)
    parts_ml = pltpu.VMEM((SEQ_GROUPS, 2 * half_h, 128), F32)
    ring = pltpu.VMEM((ATT_SLOTS, ATT_SEQS, rows, head_dim), BF16)
    dma = pltpu.SemaphoreType.DMA
    return pl.pallas_call(
        finish_kernel,
        out_shape=[
            jax.ShapeDtypeStruct((num_seqs, width), BF16),
            jax.ShapeDtypeStruct((2, num_seqs, kv_local, head_dim), BF16),
        ],
        in_specs=[pl.BlockSpec(memory_space=pltpu.SMEM), anyspace, vmem, anyspace, vmem, anyspace, anyspace, anyspace],
        out_specs=[vmem, vmem],
        scratch_shapes=[
            pltpu.VMEM((w_o.shape[0], cols), BF16),
            pltpu.VMEM((half_s, cols), BF16),
            pltpu.VMEM((q_rows + 2 * kv_local, num_seqs, head_dim), F32),
            ring, ring,
            pltpu.VMEM((rows, head_dim), BF16),
            pltpu.VMEM((groups, q_rows, some, head_dim), F32),
            pltpu.VMEM((groups, 2 * q_rows, 128), F32),
            pltpu.VMEM((q_rows, 128), F32),
            pltpu.VMEM((width // head_dim, head_dim), F32),
            pltpu.VMEM((groups, half_h, some, head_dim), F32),
            pltpu.VMEM((groups, 2 * q_rows, 128), F32),
            parts, parts_ml, parts, parts_ml, parts, parts_ml,
            pltpu.VMEM((SEQ_GROUPS, some, half_h * head_dim), F32),
            pltpu.VMEM((SEQ_GROUPS, some, half_h * head_dim), F32),
            pltpu.VMEM((SEQ_GROUPS, some, q_rows * head_dim), BF16),
            chunked, chunked, chunked, chunked, chunked, chunked,
            dma((W_PARTS,)), dma, dma((ATT_SLOTS,)), dma((ATT_SLOTS,)),
            dma((2 * groups,)), dma((2 * groups,)), dma((2 * groups,)),
            dma((2 * groups,)), dma((2 * groups,)),
            dma((groups,)), dma((groups,)),
            dma((SEQ_GROUPS,)), dma((SEQ_GROUPS,)),
            *[dma((total,))] * 8,
        ],
        compiler_params=pltpu.CompilerParams(collective_id=1, has_side_effects=True, vmem_limit_bytes=62 << 20),
        name="finish",
    )(seq_lens, half, sinks, hidden, b_o.reshape(width // head_dim, head_dim), w_o, k_rows, v_rows)


LAST_PARTS = 4


def last_kernel(lens_ref, y_hbm, new_ref, k_in, v_in, y_out, k_out, v_out, y_buf, in_sem, out_sem, k_sem, v_sem):
    num_seqs, ctx_local = k_out.shape[:2]
    base = lax.axis_index("sp") * ctx_local
    rows = y_hbm.shape[0] // LAST_PARTS
    loads, stores = [], []
    for p in range(LAST_PARTS):
        at = pl.ds(p * rows, rows)
        loads.append(pltpu.make_async_copy(y_hbm.at[at], y_buf.at[at], in_sem.at[p]))
        stores.append(pltpu.make_async_copy(y_buf.at[at], y_out.at[at], out_sem.at[p]))
        loads[-1].start()

    def copies(b, n):
        return pltpu.make_async_copy(new_ref.at[0, b], k_out.at[b, n], k_sem), pltpu.make_async_copy(new_ref.at[1, b], v_out.at[b, n], v_sem)

    def put(b, _):
        n = lens_ref[b] - base

        @pl.when(jnp.logical_and(n >= 0, n < ctx_local))
        def _():
            for c in copies(b, n):
                c.start()

        return 0

    lax.fori_loop(0, num_seqs, put, 0)
    for p in range(LAST_PARTS):
        loads[p].wait()
        stores[p].start()

    def settle(b, _):
        n = lens_ref[b] - base

        @pl.when(jnp.logical_and(n >= 0, n < ctx_local))
        def _():
            for c in copies(b, n):
                c.wait()

        return 0

    lax.fori_loop(0, num_seqs, settle, 0)
    for c in stores:
        c.wait()


def last(seq_lens, y, new, k_copy, v_copy):
    vmem = pl.BlockSpec(memory_space=pltpu.VMEM)
    anyspace = pl.BlockSpec(memory_space=pl.ANY)
    dma = pltpu.SemaphoreType.DMA
    return pl.pallas_call(
        last_kernel,
        out_shape=[jax.ShapeDtypeStruct(a.shape, a.dtype) for a in (y, k_copy, v_copy)],
        in_specs=[pl.BlockSpec(memory_space=pltpu.SMEM), anyspace, vmem, anyspace, anyspace],
        out_specs=[anyspace] * 3,
        scratch_shapes=[pltpu.VMEM(y.shape, y.dtype), dma((LAST_PARTS,)), dma((LAST_PARTS,)), dma, dma],
        input_output_aliases={3: 1, 4: 2},
        compiler_params=pltpu.CompilerParams(vmem_limit_bytes=60 << 20),
        name="last",
    )(seq_lens, y, new, k_copy, v_copy)


def solution(mesh):
    cache_spec = P("dp", "sp", "tp", None)

    def block_step(hidden, seq_lens, rope_cos, rope_sin, k_cache, v_cache, norm_gain, w_qkv, b_qkv, sink_logits, w_o, b_o):
        num_seqs, ctx_local, kv_local, head_dim = k_cache.shape
        rows = (num_seqs, ctx_local * kv_local, head_dim)
        k_rows, v_rows = k_cache.reshape(rows), v_cache.reshape(rows)
        half, k_copy, v_copy = project(hidden, rope_cos, rope_sin, norm_gain, w_qkv, b_qkv, k_rows, v_rows)
        sinks = sink_logits.reshape(1, sink_logits.shape[0])
        y, new = finish(seq_lens, half, sinks, hidden, b_o, w_o, k_rows, v_rows)
        return last(seq_lens, y, new, k_copy.reshape(k_cache.shape), v_copy.reshape(v_cache.shape))

    return jax.shard_map(block_step, mesh=mesh, in_specs=(P("dp", None), P("dp"), P("dp", None), P("dp", None), cache_spec, cache_spec, P(None), P(None, "tp", None), P("tp", None), P("tp"), P("tp", None), P(None)), out_specs=(P("dp", None), cache_spec, cache_spec), check_vma=False)
```

time: 96.7 us -> 94.2 us (0.974)
  local copies, waits for them, and re-layouts: 3.1 us -> 0 us
    unnamed x1 -> x0, local copies, waits for them, and re-layouts: 3.1 us -> none
where the time goes in v4:
time: 94.2 us; the launch traced here: 93.9 us
  Pallas kernels  93.3 us (99%)
    pallas_call x1, Pallas kernels, finish(): pl.pallas_call(finish_kernel, out_shape=[jax.ShapeDtypeStruct((num_seqs,...  60.1 us
    pallas_call x1, Pallas kernels, project(): pl.pallas_call(project_kernel, out_shape=[jax.ShapeDtypeStruct((rows, num...  29.3 us
    pallas_call x1, Pallas kernels, last(): pl.pallas_call(last_kernel, out_shape=[jax.ShapeDtypeStruct(a.shape, a.dt...  3.89 us

profile of v4, /device:TPU:0, one launch (start us, length us, event | category | flops | bytes accessed | tf_op | source)
XLA Modules:
  0.0 93.9 jit_solution(599986985648906752)
XLA Ops:
  0.6 29.3 %project.1 = (f32[20,128,128]{2,1,0:T(8,128)}, bf16[128,256,128]{2,1,0:T(8,128)(2,1)}, bf16[128,256,128]{2,1,0:T(8,128)(2,1)}) custom-call(bf16[128,8192]{1,0:T(8,128)(2,1)} %hid_ref.1, bf16[64,128]{1,0:T(8,128)(2,1)} %bitcast.18, f32[64,128]{1,0:T(8,128)} %bitcast.15, f32[64,128]{1,0:T(8,128)} %bitcast.16, bf16[4,1280]{1,0:T(4,128)(2,1)} %bias_ref.1, ...), custom_call_target="tpu_custom_call" | custom-call | tf_op jit(solution)/shard_map/project/pallas_call | solution.py:157
  29.9 60.1 %finish.1 = (bf16[128,8192]{1,0:T(8,128)(2,1)}, bf16[2,128,4,128]{3,2,1,0:T(4,128)(2,1)}) custom-call(s32[128]{0:T(128)} %lens_ref.3, f32[20,128,128]{2,1,0:T(8,128)} %get-tuple-element.8.half_hbm, f32[1,32]{1,0:T(1,128)} %bitcast.19, bf16[128,8192]{1,0:T(8,128)(2,1)} %hid_ref.1, bf16[64,128]{1,0:T(8,128)(2,1)} %bitcast.17, bf16[4096,8192]{1,0:T(8,128)(2,1)} %wo_ref.1, ...), custom_call_target="tpu_custom_call" | custom-call | tf_op jit(solution)/shard_map/finish/pallas_call | solution.py:511
  90.0 3.9 %last.1 = (bf16[128,8192]{1,0:T(8,128)(2,1)}, bf16[128,64,4,128]{3,2,1,0:T(4,128)(2,1)}, bf16[128,64,4,128]{3,2,1,0:T(4,128)(2,1)}) custom-call(s32[128]{0:T(128)} %lens_ref.3, bf16[128,8192]{1,0:T(8,128)(2,1)} %get-tuple-element.9.y_hbm, bf16[2,128,4,128]{3,2,1,0:T(4,128)(2,1)} %get-tuple-element.10.new_ref, ...), custom_call_target="tpu_custom_call", output_to_operand_aliasing={{1}: (3, {}), {2}: (4, {})} | custom-call | tf_op jit(solution)/shard_map/last/pallas_call | solution.py:599

commit v5 on v4

--- a/solution.py
+++ b/solution.py
@@ -182,10 +182,10 @@
 
 
 ATT_SEQS = 8
-ATT_SLOTS = 5
+ATT_SLOTS = 6
 OUT_COLS = 256
 SEQ_GROUPS = 2
-W_PARTS = 4
+W_PARTS = 8
 LAG_Y = 6
 LAG_X = 5
 
@@ -447,20 +447,20 @@
     carry = attend(0, 0, per_group, (zero, zero))
     to_partner(0, carry)
     x_copy_in.start()
-    for p in range(W_PARTS // 2):
-        w_copy(p).start()
     heads_wait(1)
     carry = attend(1, 0, half_group, (zero, zero))
     across(0)
     carry = attend(1, half_group, per_group, carry)
     to_partner(1, carry)
-    for p in range(W_PARTS // 2, W_PARTS):
-        w_copy(p).start()
+    w_copy(0).start()
     heads_wait(2)
     carry = attend(2, 0, half_group, (zero, zero))
     across(1)
+    w_copy(1).start()
     carry = attend(2, half_group, per_group, carry)
     to_partner(2, carry)
+    for p in range(2, W_PARTS):
+        w_copy(p).start()
     heads_wait(3)
     carry = attend(3, 0, per_group, (zero, zero))
     to_partner(3, carry)

time: 94.2 us -> 88.9 us (0.944)
  Pallas kernels: 93.3 us -> 88 us
    pallas_call x1, Pallas kernels: 60.1 us -> 54.7 us  [finish(): pl.pallas_call(finish_kernel, out_shape=[jax.ShapeDtypeStruct((num_seqs,...]
where the time goes in v5:
time: 88.9 us; the launch traced here: 88.7 us
  Pallas kernels  88 us (99%)
    pallas_call x1, Pallas kernels, finish(): pl.pallas_call(finish_kernel, out_shape=[jax.ShapeDtypeStruct((num_seqs,...  54.7 us
    pallas_call x1, Pallas kernels, project(): pl.pallas_call(project_kernel, out_shape=[jax.ShapeDtypeStruct((rows, num...  29.3 us
    pallas_call x1, Pallas kernels, last(): pl.pallas_call(last_kernel, out_shape=[jax.ShapeDtypeStruct(a.shape, a.dt...  3.98 us

profile of v5, /device:TPU:0, one launch (start us, length us, event | category | flops | bytes accessed | tf_op | source)
XLA Modules:
  0.0 88.7 jit_solution(1069680292766129017)
XLA Ops:
  0.6 29.3 %project.1 = (f32[20,128,128]{2,1,0:T(8,128)}, bf16[128,256,128]{2,1,0:T(8,128)(2,1)}, bf16[128,256,128]{2,1,0:T(8,128)(2,1)}) custom-call(bf16[128,8192]{1,0:T(8,128)(2,1)} %hid_ref.1, bf16[64,128]{1,0:T(8,128)(2,1)} %bitcast.18, f32[64,128]{1,0:T(8,128)} %bitcast.15, f32[64,128]{1,0:T(8,128)} %bitcast.16, bf16[4,1280]{1,0:T(4,128)(2,1)} %bias_ref.1, ...), custom_call_target="tpu_custom_call" | custom-call | tf_op jit(solution)/shard_map/project/pallas_call | solution.py:157
  29.9 54.7 %finish.1 = (bf16[128,8192]{1,0:T(8,128)(2,1)}, bf16[2,128,4,128]{3,2,1,0:T(4,128)(2,1)}) custom-call(s32[128]{0:T(128)} %lens_ref.3, f32[20,128,128]{2,1,0:T(8,128)} %get-tuple-element.8.half_hbm, f32[1,32]{1,0:T(1,128)} %bitcast.19, bf16[128,8192]{1,0:T(8,128)(2,1)} %hid_ref.1, bf16[64,128]{1,0:T(8,128)(2,1)} %bitcast.17, bf16[4096,8192]{1,0:T(8,128)(2,1)} %wo_ref.1, ...), custom_call_target="tpu_custom_call" | custom-call | tf_op jit(solution)/shard_map/finish/pallas_call | solution.py:511
  84.7 4.0 %last.1 = (bf16[128,8192]{1,0:T(8,128)(2,1)}, bf16[128,64,4,128]{3,2,1,0:T(4,128)(2,1)}, bf16[128,64,4,128]{3,2,1,0:T(4,128)(2,1)}) custom-call(s32[128]{0:T(128)} %lens_ref.3, bf16[128,8192]{1,0:T(8,128)(2,1)} %get-tuple-element.9.y_hbm, bf16[2,128,4,128]{3,2,1,0:T(4,128)(2,1)} %get-tuple-element.10.new_ref, ...), custom_call_target="tpu_custom_call", output_to_operand_aliasing={{1}: (3, {}), {2}: (4, {})} | custom-call | tf_op jit(solution)/shard_map/last/pallas_call | solution.py:599

commit v6 on v5

--- a/solution.py
+++ b/solution.py
@@ -32,13 +32,15 @@
 
 
 QKV_ROWS = 512
-QKV_SLOTS = 3
+QKV_SLOTS = 4
 CACHE_SEQS = 8
-CACHE_AHEAD = 4
-
-
-def project_kernel(x_ref, gain_ref, cos_ref, sin_ref, bias_ref, w_ref, k_ref, v_ref, out_ref, k_out, v_out,
-                   normed, gain, heads, acc_q, acc_e, wq_buf, we_buf, k_buf, v_buf, wq_sem, we_sem, out_sem, k_in, v_in, k_back, v_back):
+CACHE_AHEAD = 6
+CACHE_FIRST = 3
+X_PARTS = 4
+
+
+def project_kernel(x_hbm, gain_hbm, cos_hbm, sin_hbm, bias_hbm, w_ref, k_ref, v_ref, out_ref, k_out, v_out,
+                   x_ref, gain_ref, cos_ref, sin_ref, bias_ref, x_sem, small_sem, normed, gain, heads, acc_q, acc_e, wq_buf, we_buf, k_buf, v_buf, wq_sem, we_sem, out_sem, k_in, v_in, k_back, v_back):
     _, core = sp_place()
     num_seqs, depth = x_ref.shape
     head_dim = acc_e.shape[2]
@@ -47,6 +49,7 @@
     per_core = q_cols // head_dim
     group = 2 * per_core
     steps = depth // QKV_ROWS
+    x_rows = num_seqs // X_PARTS
     blocks = num_seqs // CACHE_SEQS
 
     def fetch(step, slot):
@@ -63,13 +66,28 @@
         at = pl.ds(i * CACHE_SEQS, CACHE_SEQS)
         return pltpu.make_async_copy(k_buf.at[at], k_out.at[at], k_back.at[i]), pltpu.make_async_copy(v_buf.at[at], v_out.at[at], v_back.at[i])
 
-    for s in range(QKV_SLOTS - 1):
+    small = [pltpu.make_async_copy(src, dst, small_sem.at[i]) for i, (src, dst) in enumerate(((gain_hbm, gain_ref), (cos_hbm, cos_ref), (sin_hbm, sin_ref), (bias_hbm, bias_ref)))]
+    small[0].start()
+    x_copies = []
+    for p in range(X_PARTS):
+        at = pl.ds(p * x_rows, x_rows)
+        x_copies.append(pltpu.make_async_copy(x_hbm.at[at], x_ref.at[at], x_sem.at[p]))
+        x_copies[-1].start()
+    for c in fetch(0, 0):
+        c.start()
+    for i in range(CACHE_FIRST):
+        for c in cache_in(i):
+            c.start()
+    for s in range(1, QKV_SLOTS - 1):
         for c in fetch(s, s):
             c.start()
-    for i in range(CACHE_AHEAD):
+    for i in range(CACHE_FIRST, CACHE_AHEAD):
         for c in cache_in(i):
             c.start()
-
+    for c in small[1:]:
+        c.start()
+
+    small[0].wait()
     gain[...] = gain_ref[...].astype(F32)
 
     def norm_rows(r, _):
@@ -81,7 +99,14 @@
             normed[rows, cols] = (xw[:, cols] * inv * gain[t : t + 1, :]).astype(BF16)
         return 0
 
-    lax.fori_loop(0, num_seqs // 16, norm_rows, 0)
+    for p in range(X_PARTS):
+        x_copies[p].wait()
+        lax.fori_loop(p * x_rows // 16, (p + 1) * x_rows // 16, norm_rows, 0)
+    for i in range(CACHE_FIRST):
+        for c in cache_in(i):
+            c.wait()
+        for c in cache_back(i):
+            c.start()
     acc_q[...] = jnp.zeros_like(acc_q)
     acc_e[...] = jnp.zeros_like(acc_e)
 
@@ -101,10 +126,12 @@
             for c in fetch(step + QKV_SLOTS - 1, lax.rem(step + QKV_SLOTS - 1, QKV_SLOTS)):
                 c.start()
 
-        for c in cache_in(step):
-            c.wait()
-        for c in cache_back(step):
-            c.start()
+        @pl.when(step + CACHE_FIRST < blocks)
+        def _():
+            for c in cache_in(step + CACHE_FIRST):
+                c.wait()
+            for c in cache_back(step + CACHE_FIRST):
+                c.start()
 
         h = normed[:, pl.ds(pl.multiple_of(step * QKV_ROWS, 128), QKV_ROWS)]
         wq = jnp.swapaxes(wq_buf[slot], 0, 1)
@@ -116,6 +143,8 @@
 
     lax.fori_loop(0, steps, step_fn, 0)
 
+    for c in small[1:]:
+        c.wait()
     cos_t = cos_ref[...].T
     sin_t = sin_ref[...].T
     cos2 = jnp.concatenate([cos_t, cos_t], axis=1)
@@ -150,8 +179,7 @@
     per_core = (w_qkv.shape[2] // head_dim - 2) // 2
     rows = kv_local * (per_core + 1)
     blocks = num_seqs // CACHE_SEQS
-    assert blocks == depth // QKV_ROWS
-    vmem = pl.BlockSpec(memory_space=pltpu.VMEM)
+    assert blocks <= depth // QKV_ROWS + CACHE_FIRST
     anyspace = pl.BlockSpec(memory_space=pl.ANY)
     dma = pltpu.SemaphoreType.DMA
     return pl.pallas_call(
@@ -161,9 +189,16 @@
             jax.ShapeDtypeStruct(k_rows.shape, BF16),
             jax.ShapeDtypeStruct(v_rows.shape, BF16),
         ],
-        in_specs=[vmem] * 5 + [anyspace] * 3,
+        in_specs=[anyspace] * 8,
         out_specs=[anyspace] * 3,
         scratch_shapes=[
+            pltpu.VMEM((num_seqs, depth), BF16),
+            pltpu.VMEM((depth // head_dim, head_dim), BF16),
+            pltpu.VMEM((head_dim // 2, num_seqs), F32),
+            pltpu.VMEM((head_dim // 2, num_seqs), F32),
+            pltpu.VMEM(b_qkv.shape, BF16),
+            dma((X_PARTS,)),
+            dma((4,)),
             pltpu.VMEM((num_seqs, depth), BF16),
             pltpu.VMEM((depth // head_dim, head_dim), F32),
             pltpu.VMEM((rows, num_seqs, head_dim), F32),
@@ -188,13 +223,15 @@
 W_PARTS = 8
 LAG_Y = 6
 LAG_X = 5
-
-
-def finish_kernel(lens_ref, half_hbm, sink_ref, hid_ref, bo_ref, wo_ref, k_hbm, v_hbm, y_ref, new_ref,
-                  w_buf, x_buf, h_buf, k_ring, v_ring, pos_ref, num, ml, sink_col, bo_f32, r1, r1ml, own, own_ml, away, away_ml, r2, r2ml, o_buf, r3, o_all,
+LAG_P = 2
+OUT_CHUNKS = 4
+
+
+def finish_kernel(lens_ref, half_hbm, sink_ref, hid_ref, bo_ref, wo_ref, k_hbm, v_hbm, y_out, new_ref,
+                  y_ref, w_buf, x_buf, h_buf, k_ring, v_ring, num, ml, sink_col, bo_f32, r1, r1ml, own, own_ml, away, away_ml, r2, r2ml, o_buf, r3, o_all,
                   y_send, y_recv, z_buf, x_recv, p1, p2,
                   w_sem, x_sem, k_sem, v_sem, h_in, h_send, h_recv, s1_send, s1_recv, s2_send, s2_recv, s3_send, s3_recv,
-                  y_ss, y_rs, x_ss, x_rs, p1_ss, p1_rs, p2_ss, p2_rs):
+                  y_ss, y_rs, x_ss, x_rs, p1_ss, p1_rs, p2_ss, p2_rs, o_sem):
     chip, core = sp_place()
     tp = lax.axis_index("tp")
     partner = {"sp": 2 * chip + (1 - core)}
@@ -257,7 +294,6 @@
     sink = sink_column(sink_ref, q_rows, 2, 2 * part_h)
     sink_col[...] = jnp.broadcast_to(sink, sink_col.shape)
     bo_f32[...] = bo_ref[...].astype(F32)
-    pos_ref[...] = lax.div(lax.broadcasted_iota(jnp.int32, pos_ref.shape, 0), kv_local).astype(F32).astype(BF16)
     pl.semaphore_wait(barrier, 3)
     for c in h_remote:
         c.start()
@@ -269,6 +305,8 @@
     col_pos = jnp.where(lax.rem(col, kv_local) == kv_row, lax.div(col, kv_local), ctx_local * 1024)
     lane = lax.broadcasted_iota(jnp.int32, (q_rows, ml.shape[2]), 1)
     batch = range(ATT_SEQS)
+    over_d = (((1,), (1,)), ((), ()))
+    new_code = jnp.where(lax.broadcasted_iota(jnp.int32, (q_rows, 16), 1) == lax.div(lax.rem(lax.broadcasted_iota(jnp.int32, (q_rows, 16), 0), half_h), part_h), 1, 2)
 
     def attend(i, first, last, carry):
         def step_fn(t, carry):
@@ -280,29 +318,28 @@
             start = block(p)
             heads = h_buf.at[:, pl.ds(pl.multiple_of(start, ATT_SEQS), ATT_SEQS)]
             rel = [lens_ref[start + s] - base for s in batch]
-            keys, values = [], []
-            for s in batch:
-                n = jnp.full((16, head_dim), rel[s].astype(F32)).astype(BF16)
-                hit = pos_ref[...].reshape(rows // 16, 16, head_dim) == n[None]
-                for j, (ring, out) in enumerate(((k_ring, keys), (v_ring, values))):
-                    new = heads[q_rows + j * kv_local : q_rows + (j + 1) * kv_local, s, :].astype(BF16)
-                    new_ref[j, start + s] = new
-                    new = jnp.concatenate([new] * (16 // kv_local), axis=0)
-                    old = ring[slot, s].reshape(rows // 16, 16, head_dim)
-                    out.append(jnp.where(hit, new[None], old).reshape(rows, head_dim))
+            inside = [jnp.where(jnp.logical_and(r >= 0, r < ctx_local), 1, 0) for r in rel]
             queries = [heads[0:q_rows, s, :].astype(BF16) for s in batch]
-            logits = [lax.dot_general(queries[s], keys[s], (((1,), (1,)), ((), ())), preferred_element_type=F32) for s in batch]
-            logits = [jnp.where(col_pos <= rel[s], logits[s] * scale, -jnp.inf) for s in batch]
-            tops = [jnp.maximum(jnp.max(logits[s], axis=1, keepdims=True), sink) for s in batch]
+            new_k, new_v = ([jnp.concatenate([heads[lo : lo + kv_local, s, :]] * (16 // kv_local), axis=0).astype(BF16) for s in batch] for lo in (q_rows, q_rows + kv_local))
+            logits = [lax.dot_general(queries[s], k_ring[slot, s], over_d, preferred_element_type=F32) for s in batch]
+            extra = [lax.dot_general(queries[s], new_k[s], over_d, preferred_element_type=F32) for s in batch]
+            logits = [jnp.where(col_pos < rel[s], logits[s] * scale, -jnp.inf) for s in batch]
+            extra = [jnp.where(new_code == inside[s], extra[s] * scale, -jnp.inf) for s in batch]
+            tops = [jnp.maximum(jnp.maximum(jnp.max(logits[s], axis=1, keepdims=True), jnp.max(extra[s], axis=1, keepdims=True)), sink) for s in batch]
             weights = [jnp.exp(logits[s] - tops[s]) for s in batch]
-            totals = [jnp.sum(weights[s], axis=1, keepdims=True) for s in batch]
-            sums = [jnp.dot(weights[s].astype(BF16), values[s], preferred_element_type=F32) for s in batch]
+            extra = [jnp.exp(extra[s] - tops[s]) for s in batch]
+            totals = [jnp.sum(weights[s], axis=1, keepdims=True) + jnp.sum(extra[s], axis=1, keepdims=True) for s in batch]
+            sums = [jnp.dot(weights[s].astype(BF16), v_ring[slot, s], preferred_element_type=F32) for s in batch]
+            sums = [sums[s] + jnp.dot(extra[s].astype(BF16), new_v[s], preferred_element_type=F32) for s in batch]
             out = num.at[i, :, pl.ds(pl.multiple_of(t * ATT_SEQS, ATT_SEQS), ATT_SEQS)]
             for s in batch:
                 here = lane == t * ATT_SEQS + s
                 m_all = jnp.where(here, tops[s], m_all)
                 l_all = jnp.where(here, totals[s], l_all)
                 out[:, s, :] = sums[s]
+            for s in batch:
+                for j in range(2):
+                    new_ref[j, start + s] = heads[q_rows + j * kv_local : q_rows + (j + 1) * kv_local, s, :].astype(BF16)
 
             @pl.when(p + ATT_SLOTS < steps)
             def _():
@@ -401,6 +438,19 @@
         g, j = lax.div(t, chunks), lax.rem(t, chunks)
         return seqs(which_seqs, g), pl.ds(pl.multiple_of(which_cols * cols + j * OUT_COLS, 128), OUT_COLS)
 
+    def out_copy(kind, q):
+        which_seqs, which_cols = ((chip, core), (1 - chip, core), (chip, 1 - core), (1 - chip, 1 - core))[kind]
+        rows_at, _ = place(which_seqs, which_cols, q * OUT_CHUNKS)
+        j = lax.rem(q * OUT_CHUNKS, chunks)
+        cols_at = pl.ds(pl.multiple_of(which_cols * cols + j * OUT_COLS, 128), OUT_CHUNKS * OUT_COLS)
+        return pltpu.make_async_copy(y_ref.at[rows_at, cols_at], y_out.at[rows_at, cols_at], o_sem.at[kind, q])
+
+    def put_out(u, kinds):
+        @pl.when(lax.rem(u, OUT_CHUNKS) == OUT_CHUNKS - 1)
+        def _():
+            for kind in kinds:
+                out_copy(kind, lax.div(u, OUT_CHUNKS)).start()
+
     def body(t, _):
         @pl.when(t < total)
         def _():
@@ -428,8 +478,9 @@
             p1_copy(u).start()
             rows_at, cols_at = place(chip, core, u)
             y_ref[rows_at, cols_at] = z
-
-        @pl.when(t >= LAG_Y + LAG_X)
+            put_out(u, (0,))
+
+        @pl.when(jnp.logical_and(t >= LAG_Y + LAG_X, t < total + LAG_Y + LAG_X))
         def _():
             u = t - (LAG_Y + LAG_X)
             x_copy(u).wait_recv()
@@ -439,6 +490,15 @@
             p1_copy(u).wait_recv()
             rows_at, cols_at = place(chip, 1 - core, u)
             y_ref[rows_at, cols_at] = p1[u].astype(BF16)
+            put_out(u, (1, 2))
+
+        @pl.when(t >= LAG_Y + LAG_X + LAG_P)
+        def _():
+            u = t - (LAG_Y + LAG_X + LAG_P)
+            p2_copy(u).wait_recv()
+            rows_at, cols_at = place(1 - chip, 1 - core, u)
+            y_ref[rows_at, cols_at] = p2[u].astype(BF16)
+            put_out(u, (3,))
 
         return 0
 
@@ -474,12 +534,9 @@
     c3.append(heads_start(1))
     lax.fori_loop(8, 12, body, 0)
     heads_end(1, c3[1])
-    lax.fori_loop(12, total + LAG_Y + LAG_X, body, 0)
+    lax.fori_loop(12, total + LAG_Y + LAG_X + LAG_P, body, 0)
 
     def tail(t, _):
-        p2_copy(t).wait_recv()
-        rows_at, cols_at = place(1 - chip, 1 - core, t)
-        y_ref[rows_at, cols_at] = p2[t].astype(BF16)
         y_copy(t).wait_send()
         x_copy(t).wait_send()
         p1_copy(t).wait_send()
@@ -487,6 +544,13 @@
         return 0
 
     lax.fori_loop(0, total, tail, 0)
+
+    def settle(q, _):
+        for kind in range(4):
+            out_copy(kind, q).wait()
+        return 0
+
+    lax.fori_loop(0, total // OUT_CHUNKS, settle, 0)
     for c in (*h_remote, *(c for pair in c1 + c2 for c in pair), *c3):
         c.wait_send()
 
@@ -515,13 +579,13 @@
             jax.ShapeDtypeStruct((2, num_seqs, kv_local, head_dim), BF16),
         ],
         in_specs=[pl.BlockSpec(memory_space=pltpu.SMEM), anyspace, vmem, anyspace, vmem, anyspace, anyspace, anyspace],
-        out_specs=[vmem, vmem],
+        out_specs=[anyspace, vmem],
         scratch_shapes=[
+            pltpu.VMEM((num_seqs, width), BF16),
             pltpu.VMEM((w_o.shape[0], cols), BF16),
             pltpu.VMEM((half_s, cols), BF16),
             pltpu.VMEM((q_rows + 2 * kv_local, num_seqs, head_dim), F32),
             ring, ring,
-            pltpu.VMEM((rows, head_dim), BF16),
             pltpu.VMEM((groups, q_rows, some, head_dim), F32),
             pltpu.VMEM((groups, 2 * q_rows, 128), F32),
             pltpu.VMEM((q_rows, 128), F32),
@@ -539,6 +603,7 @@
             dma((groups,)), dma((groups,)),
             dma((SEQ_GROUPS,)), dma((SEQ_GROUPS,)),
             *[dma((total,))] * 8,
+            dma((4, total // OUT_CHUNKS)),
         ],
         compiler_params=pltpu.CompilerParams(collective_id=1, has_side_effects=True, vmem_limit_bytes=62 << 20),
         name="finish",
@@ -546,12 +611,15 @@
 
 
 LAST_PARTS = 4
-
-
-def last_kernel(lens_ref, y_hbm, new_ref, k_in, v_in, y_out, k_out, v_out, y_buf, in_sem, out_sem, k_sem, v_sem):
+LAST_UNROLL = 8
+
+
+def last_kernel(lens_ref, y_hbm, new_hbm, k_in, v_in, y_out, k_out, v_out, y_buf, new_ref, in_sem, out_sem, new_sem, k_sem, v_sem):
     num_seqs, ctx_local = k_out.shape[:2]
     base = lax.axis_index("sp") * ctx_local
     rows = y_hbm.shape[0] // LAST_PARTS
+    new_copy = pltpu.make_async_copy(new_hbm, new_ref, new_sem)
+    new_copy.start()
     loads, stores = [], []
     for p in range(LAST_PARTS):
         at = pl.ds(p * rows, rows)
@@ -559,49 +627,39 @@
         stores.append(pltpu.make_async_copy(y_buf.at[at], y_out.at[at], out_sem.at[p]))
         loads[-1].start()
 
-    def copies(b, n):
-        return pltpu.make_async_copy(new_ref.at[0, b], k_out.at[b, n], k_sem), pltpu.make_async_copy(new_ref.at[1, b], v_out.at[b, n], v_sem)
-
-    def put(b, _):
-        n = lens_ref[b] - base
-
-        @pl.when(jnp.logical_and(n >= 0, n < ctx_local))
-        def _():
-            for c in copies(b, n):
-                c.start()
-
-        return 0
-
-    lax.fori_loop(0, num_seqs, put, 0)
+    def for_new_rows(act):
+        def step(i, _):
+            for b in (i * LAST_UNROLL + r for r in range(LAST_UNROLL)):
+                n = lens_ref[b] - base
+
+                @pl.when(jnp.logical_and(n >= 0, n < ctx_local))
+                def _():
+                    act(pltpu.make_async_copy(new_ref.at[0, b], k_out.at[b, n], k_sem))
+                    act(pltpu.make_async_copy(new_ref.at[1, b], v_out.at[b, n], v_sem))
+
+            return 0
+
+        lax.fori_loop(0, num_seqs // LAST_UNROLL, step, 0)
+
+    new_copy.wait()
+    for_new_rows(lambda c: c.start())
     for p in range(LAST_PARTS):
         loads[p].wait()
         stores[p].start()
-
-    def settle(b, _):
-        n = lens_ref[b] - base
-
-        @pl.when(jnp.logical_and(n >= 0, n < ctx_local))
-        def _():
-            for c in copies(b, n):
-                c.wait()
-
-        return 0
-
-    lax.fori_loop(0, num_seqs, settle, 0)
+    for_new_rows(lambda c: c.wait())
     for c in stores:
         c.wait()
 
 
 def last(seq_lens, y, new, k_copy, v_copy):
-    vmem = pl.BlockSpec(memory_space=pltpu.VMEM)
     anyspace = pl.BlockSpec(memory_space=pl.ANY)
     dma = pltpu.SemaphoreType.DMA
     return pl.pallas_call(
         last_kernel,
         out_shape=[jax.ShapeDtypeStruct(a.shape, a.dtype) for a in (y, k_copy, v_copy)],
-        in_specs=[pl.BlockSpec(memory_space=pltpu.SMEM), anyspace, vmem, anyspace, anyspace],
+        in_specs=[pl.BlockSpec(memory_space=pltpu.SMEM)] + [anyspace] * 4,
         out_specs=[anyspace] * 3,
-        scratch_shapes=[pltpu.VMEM(y.shape, y.dtype), dma((LAST_PARTS,)), dma((LAST_PARTS,)), dma, dma],
+        scratch_shapes=[pltpu.VMEM(y.shape, y.dtype), pltpu.VMEM(new.shape, new.dtype), dma((LAST_PARTS,)), dma((LAST_PARTS,)), dma, dma, dma],
         input_output_aliases={3: 1, 4: 2},
         compiler_params=pltpu.CompilerParams(vmem_limit_bytes=60 << 20),
         name="last",

time: 88.9 us -> 88.5 us (level)
    pallas_call x1, Pallas kernels: 54.7 us -> 53.6 us  [finish(): pl.pallas_call(finish_kernel, out_shape=[jax.ShapeDtypeStruct((num_seqs,...]
where the time goes in v6:
time: 88.5 us; the launch traced here: 88.3 us
  Pallas kernels  87.6 us (99%)
    pallas_call x1, Pallas kernels, finish(): pl.pallas_call(finish_kernel, out_shape=[jax.ShapeDtypeStruct((num_seqs,...  53.6 us
    pallas_call x1, Pallas kernels, project(): pl.pallas_call(project_kernel, out_shape=[jax.ShapeDtypeStruct((rows, num...  30.1 us
    pallas_call x1, Pallas kernels, last(): pl.pallas_call(last_kernel, out_shape=[jax.ShapeDtypeStruct(a.shape, a.dt...  3.96 us

profile of v6, /device:TPU:0, one launch (start us, length us, event | category | flops | bytes accessed | tf_op | source)
XLA Modules:
  0.0 88.3 jit_solution(470014195927795473)
XLA Ops:
  0.6 30.1 %project.1 = (f32[20,128,128]{2,1,0:T(8,128)}, bf16[128,256,128]{2,1,0:T(8,128)(2,1)}, bf16[128,256,128]{2,1,0:T(8,128)(2,1)}) custom-call(bf16[128,8192]{1,0:T(8,128)(2,1)} %hid_ref.1, bf16[64,128]{1,0:T(8,128)(2,1)} %bitcast.18, f32[64,128]{1,0:T(8,128)} %bitcast.15, f32[64,128]{1,0:T(8,128)} %bitcast.16, bf16[4,1280]{1,0:T(4,128)(2,1)} %bias_hbm.1, ...), custom_call_target="tpu_custom_call" | custom-call | tf_op jit(solution)/shard_map/project/pallas_call | solution.py:185
  30.7 53.6 %finish.1 = (bf16[128,8192]{1,0:T(8,128)(2,1)}, bf16[2,128,4,128]{3,2,1,0:T(4,128)(2,1)}) custom-call(s32[128]{0:T(128)} %lens_ref.3, f32[20,128,128]{2,1,0:T(8,128)} %get-tuple-element.8.half_hbm, f32[1,32]{1,0:T(1,128)} %bitcast.19, bf16[128,8192]{1,0:T(8,128)(2,1)} %hid_ref.1, bf16[64,128]{1,0:T(8,128)(2,1)} %bitcast.17, bf16[4096,8192]{1,0:T(8,128)(2,1)} %wo_ref.1, ...), custom_call_target="tpu_custom_call" | custom-call | tf_op jit(solution)/shard_map/finish/pallas_call | solution.py:575
  84.3 4.0 %last.1 = (bf16[128,8192]{1,0:T(8,128)(2,1)}, bf16[128,64,4,128]{3,2,1,0:T(4,128)(2,1)}, bf16[128,64,4,128]{3,2,1,0:T(4,128)(2,1)}) custom-call(s32[128]{0:T(128)} %lens_ref.3, bf16[128,8192]{1,0:T(8,128)(2,1)} %get-tuple-element.9.y_hbm, bf16[2,128,4,128]{3,2,1,0:T(4,128)(2,1)} %get-tuple-element.10.new_hbm, ...), custom_call_target="tpu_custom_call", output_to_operand_aliasing={{1}: (3, {}), {2}: (4, {})} | custom-call | tf_op jit(solution)/shard_map/last/pallas_call | solution.py:657

commit v7 on v6

--- a/solution.py
+++ b/solution.py
@@ -31,11 +31,11 @@
     return jnp.sum(jnp.where(same, jnp.broadcast_to(row_ref[...], (count, count)), 0.0), axis=1, keepdims=True)
 
 
-QKV_ROWS = 512
-QKV_SLOTS = 4
-CACHE_SEQS = 8
-CACHE_AHEAD = 6
-CACHE_FIRST = 3
+QKV_ROWS = 1024
+QKV_SLOTS = 3
+CACHE_SEQS = 16
+CACHE_AHEAD = 2
+CACHE_FIRST = 0
 X_PARTS = 4
 
 
@@ -218,13 +218,13 @@
 
 ATT_SEQS = 8
 ATT_SLOTS = 6
-OUT_COLS = 256
+OUT_COLS = 512
 SEQ_GROUPS = 2
 W_PARTS = 8
-LAG_Y = 6
-LAG_X = 5
-LAG_P = 2
-OUT_CHUNKS = 4
+LAG_Y = 3
+LAG_X = 3
+LAG_P = 1
+OUT_CHUNKS = 2
 
 
 def finish_kernel(lens_ref, half_hbm, sink_ref, hid_ref, bo_ref, wo_ref, k_hbm, v_hbm, y_out, new_ref,
@@ -530,11 +530,11 @@
     c3 = [heads_start(0)]
     heads_end(0, c3[0])
     x_copy_in.wait()
-    lax.fori_loop(0, 8, body, 0)
+    lax.fori_loop(0, chunks // 2, body, 0)
     c3.append(heads_start(1))
-    lax.fori_loop(8, 12, body, 0)
+    lax.fori_loop(chunks // 2, 3 * chunks // 4, body, 0)
     heads_end(1, c3[1])
-    lax.fori_loop(12, total + LAG_Y + LAG_X + LAG_P, body, 0)
+    lax.fori_loop(3 * chunks // 4, total + LAG_Y + LAG_X + LAG_P, body, 0)
 
     def tail(t, _):
         y_copy(t).wait_send()

time: 88.5 us -> 86.6 us (0.979)
  Pallas kernels: 87.6 us -> 85.5 us
    pallas_call x1, Pallas kernels: 30.1 us -> 28.5 us  [project(): pl.pallas_call(project_kernel, out_shape=[jax.ShapeDtypeStruct((rows, num...]
where the time goes in v7:
time: 86.6 us; the launch traced here: 86.2 us
  Pallas kernels  85.5 us (99%)
    pallas_call x1, Pallas kernels, finish(): pl.pallas_call(finish_kernel, out_shape=[jax.ShapeDtypeStruct((num_seqs,...  53.1 us
    pallas_call x1, Pallas kernels, project(): pl.pallas_call(project_kernel, out_shape=[jax.ShapeDtypeStruct((rows, num...  28.5 us
    pallas_call x1, Pallas kernels, last(): pl.pallas_call(last_kernel, out_shape=[jax.ShapeDtypeStruct(a.shape, a.dt...  3.95 us

profile of v7, /device:TPU:0, one launch (start us, length us, event | category | flops | bytes accessed | tf_op | source)
XLA Modules:
  0.0 86.2 jit_solution(15793188588115388932)
XLA Ops:
  0.6 28.5 %project.1 = (f32[20,128,128]{2,1,0:T(8,128)}, bf16[128,256,128]{2,1,0:T(8,128)(2,1)}, bf16[128,256,128]{2,1,0:T(8,128)(2,1)}) custom-call(bf16[128,8192]{1,0:T(8,128)(2,1)} %hid_ref.1, bf16[64,128]{1,0:T(8,128)(2,1)} %bitcast.18, f32[64,128]{1,0:T(8,128)} %bitcast.15, f32[64,128]{1,0:T(8,128)} %bitcast.16, bf16[4,1280]{1,0:T(4,128)(2,1)} %bias_hbm.1, ...), custom_call_target="tpu_custom_call" | custom-call | tf_op jit(solution)/shard_map/project/pallas_call | solution.py:185
  29.2 53.1 %finish.1 = (bf16[128,8192]{1,0:T(8,128)(2,1)}, bf16[2,128,4,128]{3,2,1,0:T(4,128)(2,1)}) custom-call(s32[128]{0:T(128)} %lens_ref.3, f32[20,128,128]{2,1,0:T(8,128)} %get-tuple-element.8.half_hbm, f32[1,32]{1,0:T(1,128)} %bitcast.19, bf16[128,8192]{1,0:T(8,128)(2,1)} %hid_ref.1, bf16[64,128]{1,0:T(8,128)(2,1)} %bitcast.17, bf16[4096,8192]{1,0:T(8,128)(2,1)} %wo_ref.1, ...), custom_call_target="tpu_custom_call" | custom-call | tf_op jit(solution)/shard_map/finish/pallas_call | solution.py:575
  82.2 3.9 %last.1 = (bf16[128,8192]{1,0:T(8,128)(2,1)}, bf16[128,64,4,128]{3,2,1,0:T(4,128)(2,1)}, bf16[128,64,4,128]{3,2,1,0:T(4,128)(2,1)}) custom-call(s32[128]{0:T(128)} %lens_ref.3, bf16[128,8192]{1,0:T(8,128)(2,1)} %get-tuple-element.9.y_hbm, bf16[2,128,4,128]{3,2,1,0:T(4,128)(2,1)} %get-tuple-element.10.new_hbm, ...), custom_call_target="tpu_custom_call", output_to_operand_aliasing={{1}: (3, {}), {2}: (4, {})} | custom-call | tf_op jit(solution)/shard_map/last/pallas_call | solution.py:657

commit v8 on v7

--- a/solution.py
+++ b/solution.py
@@ -34,7 +34,7 @@
 QKV_ROWS = 1024
 QKV_SLOTS = 3
 CACHE_SEQS = 16
-CACHE_AHEAD = 2
+CACHE_AHEAD = 1
 CACHE_FIRST = 0
 X_PARTS = 4
 
@@ -164,12 +164,16 @@
             heads[k * per_core + g] = rotate(acc_q[k, :, cols] + bias_q[:, cols], cos2, sin2)
         bias_e = bias_ref[k : k + 1, pl.ds(pl.multiple_of((group + core) * head_dim, 128), head_dim)].astype(F32)
         heads[kv_local * per_core + k] = rotate(acc_e[k] + bias_e, cos_e, sin_e)
-    done = pltpu.make_async_copy(heads, out_ref, out_sem)
-    done.start()
+    done = []
+    for k in range(kv_local + 1):
+        part = pl.ds(k * per_core, per_core)
+        done.append(pltpu.make_async_copy(heads.at[part], out_ref.at[part], out_sem.at[k]))
+        done[-1].start()
     for i in range(blocks):
         for c in cache_back(i):
             c.wait()
-    done.wait()
+    for c in done:
+        c.wait()
 
 
 def project(hidden, rope_cos, rope_sin, norm_gain, w_qkv, b_qkv, k_rows, v_rows):
@@ -208,7 +212,7 @@
             pltpu.VMEM((QKV_SLOTS, QKV_ROWS, kv_local, head_dim), BF16),
             pltpu.VMEM(k_rows.shape, BF16),
             pltpu.VMEM(v_rows.shape, BF16),
-            dma((QKV_SLOTS,)), dma((QKV_SLOTS,)), dma,
+            dma((QKV_SLOTS,)), dma((QKV_SLOTS,)), dma((kv_local + 1,)),
             dma((blocks,)), dma((blocks,)), dma((blocks,)), dma((blocks,)),
         ],
         compiler_params=pltpu.CompilerParams(vmem_limit_bytes=60 << 20),
@@ -219,16 +223,15 @@
 ATT_SEQS = 8
 ATT_SLOTS = 6
 OUT_COLS = 512
-SEQ_GROUPS = 2
+SEQ_GROUPS = (24, 40)
 W_PARTS = 8
 LAG_Y = 3
 LAG_X = 3
 LAG_P = 1
-OUT_CHUNKS = 2
-
-
-def finish_kernel(lens_ref, half_hbm, sink_ref, hid_ref, bo_ref, wo_ref, k_hbm, v_hbm, y_out, new_ref,
-                  y_ref, w_buf, x_buf, h_buf, k_ring, v_ring, num, ml, sink_col, bo_f32, r1, r1ml, own, own_ml, away, away_ml, r2, r2ml, o_buf, r3, o_all,
+
+
+def finish_kernel(lens_hbm, half_hbm, sink_hbm, hid_ref, bo_hbm, wo_ref, k_hbm, v_hbm, y_out, new_ref,
+                  lens_ref, sink_ref, bo_ref, small_sem, y_parts, w_buf, x_buf, h_buf, k_ring, v_ring, num, ml, sink_col, bo_f32, r1, r1ml, own, own_ml, away, away_ml, r2, r2ml, o_buf, r3, o_all,
                   y_send, y_recv, z_buf, x_recv, p1, p2,
                   w_sem, x_sem, k_sem, v_sem, h_in, h_send, h_recv, s1_send, s1_recv, s2_send, s2_recv, s3_send, s3_recv,
                   y_ss, y_rs, x_ss, x_rs, p1_ss, p1_rs, p2_ss, p2_rs, o_sem):
@@ -237,7 +240,9 @@
     partner = {"sp": 2 * chip + (1 - core)}
     across_x = {"sp": 2 * (1 - chip) + core}
     across_y = {"tp": 1 - tp}
-    groups, q_rows, some, head_dim = num.shape
+    q_rows, _, head_dim = num[0].shape
+    chip_groups = len(SEQ_GROUPS)
+    offsets = [sum(SEQ_GROUPS[:g]) for g in range(chip_groups)]
     num_seqs = h_buf.shape[1]
     kv_local = (h_buf.shape[0] - q_rows) // 2
     rows = k_ring.shape[2]
@@ -247,18 +252,21 @@
     part_h = half_h // kv_local
     cols = w_buf.shape[1]
     chunks = cols // OUT_COLS
-    total = SEQ_GROUPS * chunks
+    total = chip_groups * chunks
     mine = pl.multiple_of(core * half_h, half_h)
     theirs = pl.multiple_of((1 - core) * half_h, half_h)
 
     def seqs(which, g):
-        return pl.ds(pl.multiple_of(which * half_s + g * some, some), some)
-
+        return pl.ds(pl.multiple_of(which * half_s + offsets[g], 8), SEQ_GROUPS[g])
+
+    small = [pltpu.make_async_copy(src, dst, small_sem.at[i]) for i, (src, dst) in enumerate(((lens_hbm, lens_ref), (sink_hbm, sink_ref), (bo_hbm, bo_ref)))]
+    for c in small:
+        c.start()
     barrier = pltpu.get_barrier_semaphore()
     for peer in (partner, across_x, across_y):
         pl.semaphore_signal(barrier, inc=1, device_id=peer, device_id_type=MESH)
 
-    order = [(1 - chip, g) for g in range(SEQ_GROUPS)] + [(chip, g) for g in range(SEQ_GROUPS)]
+    order = [(1 - chip, g) for g in range(chip_groups)] + [(chip, g) for g in range(chip_groups)]
     own_rows = (pl.ds(mine, half_h), pl.ds(pl.multiple_of(q_rows + kv_local * core, kv_local), kv_local))
     src_rows = (pl.ds(0, half_h), pl.ds(half_h, kv_local))
     h_local, h_remote = [], []
@@ -270,7 +278,8 @@
             h_remote.append(remote(half_hbm.at[src_rows[j], at], h_buf.at[own_rows[j], at], h_send.at[2 * i + j], h_recv.at[2 * i + j], partner))
 
     steps = num_seqs // ATT_SEQS
-    per_group = some // ATT_SEQS
+    counts = [n // ATT_SEQS for n in SEQ_GROUPS] * 2
+    starts = [sum(counts[:i]) for i in range(len(counts))]
 
     def block(p):
         return lax.rem(p + (1 - chip) * (steps // 2), steps) * ATT_SEQS
@@ -284,13 +293,15 @@
         for c in kv_load(p):
             c.start()
     my_cols = pl.ds(pl.multiple_of(core * cols, 128), cols)
-    x_copy_in = pltpu.make_async_copy(hid_ref.at[pl.ds(pl.multiple_of(chip * half_s, half_s), half_s), my_cols], x_buf, x_sem)
+    x_in = [pltpu.make_async_copy(hid_ref.at[seqs(chip, g), my_cols], x_buf[g], x_sem.at[g]) for g in range(chip_groups)]
     w_cols = cols // W_PARTS
     w_chunks = w_cols // OUT_COLS
 
     def w_copy(p):
         return pltpu.make_async_copy(wo_ref.at[:, pl.ds(pl.multiple_of(core * cols + p * w_cols, 128), w_cols)], w_buf.at[:, pl.ds(pl.multiple_of(p * w_cols, 128), w_cols)], w_sem.at[p])
 
+    for c in small:
+        c.wait()
     sink = sink_column(sink_ref, q_rows, 2, 2 * part_h)
     sink_col[...] = jnp.broadcast_to(sink, sink_col.shape)
     bo_f32[...] = bo_ref[...].astype(F32)
@@ -311,7 +322,7 @@
     def attend(i, first, last, carry):
         def step_fn(t, carry):
             m_all, l_all = carry
-            p = i * per_group + t
+            p = starts[i] + t
             slot = lax.rem(p, ATT_SLOTS)
             for c in kv_load(p):
                 c.wait()
@@ -331,7 +342,7 @@
             totals = [jnp.sum(weights[s], axis=1, keepdims=True) + jnp.sum(extra[s], axis=1, keepdims=True) for s in batch]
             sums = [jnp.dot(weights[s].astype(BF16), v_ring[slot, s], preferred_element_type=F32) for s in batch]
             sums = [sums[s] + jnp.dot(extra[s].astype(BF16), new_v[s], preferred_element_type=F32) for s in batch]
-            out = num.at[i, :, pl.ds(pl.multiple_of(t * ATT_SEQS, ATT_SEQS), ATT_SEQS)]
+            out = num[i].at[:, pl.ds(pl.multiple_of(t * ATT_SEQS, ATT_SEQS), ATT_SEQS)]
             for s in batch:
                 here = lane == t * ATT_SEQS + s
                 m_all = jnp.where(here, tops[s], m_all)
@@ -363,7 +374,7 @@
         ml[i, q_rows : 2 * q_rows] = carry[1]
         c1.append((
             remote(ml.at[i], r1ml.at[i], s1_send.at[2 * i], s1_recv.at[2 * i], partner),
-            remote(num.at[i, pl.ds(theirs, half_h)], r1.at[i], s1_send.at[2 * i + 1], s1_recv.at[2 * i + 1], partner),
+            remote(num[i].at[pl.ds(theirs, half_h)], r1[i], s1_send.at[2 * i + 1], s1_recv.at[2 * i + 1], partner),
         ))
         for c in c1[-1]:
             c.start()
@@ -380,15 +391,15 @@
         dst_ml[half_h : 2 * half_h] = l_a * f_a + l_b * f_b
         f_a, f_b = f_a.T, f_b.T
         for h in range(half_h):
-            dst[h] = num[i, mine + h] * f_a[0:some, h : h + 1] + r1[i, h] * f_b[0:some, h : h + 1]
+            dst[h] = num[i][mine + h] * f_a[0 : dst.shape[1], h : h + 1] + r1[i][h] * f_b[0 : dst.shape[1], h : h + 1]
 
     c2 = []
 
     def across(g):
-        combine(g, away.at[g], away_ml.at[g])
+        combine(g, away[g], away_ml.at[g])
         c2.append((
             remote(away_ml.at[g], r2ml.at[g], s2_send.at[2 * g], s2_recv.at[2 * g], across_x),
-            remote(away.at[g], r2.at[g], s2_send.at[2 * g + 1], s2_recv.at[2 * g + 1], across_x),
+            remote(away[g], r2[g], s2_send.at[2 * g + 1], s2_recv.at[2 * g + 1], across_x),
         ))
         for c in c2[-1]:
             c.start()
@@ -410,147 +421,130 @@
         den = l_a * f_a + l_b * f_b + jnp.exp(sink_col[pl.ds(mine, half_h)] - m_top)
         f_a, f_b = (f_a / den).T, (f_b / den).T
         for h in range(half_h):
-            o_buf[g, :, h * head_dim : (h + 1) * head_dim] = own[g, h] * f_a[0:some, h : h + 1] + r2[g, h] * f_b[0:some, h : h + 1]
-        c = remote(o_buf.at[g], r3.at[g], s3_send.at[g], s3_recv.at[g], partner)
+            o_buf[g][:, h * head_dim : (h + 1) * head_dim] = own[g][h] * f_a[0 : SEQ_GROUPS[g], h : h + 1] + r2[g][h] * f_b[0 : SEQ_GROUPS[g], h : h + 1]
+        c = remote(o_buf[g], r3[g], s3_send.at[g], s3_recv.at[g], partner)
         c.start()
         for k in range(kv_local):
-            o_all[g, :, o_place(core, k)] = o_buf[g, :, k * part_w : (k + 1) * part_w].astype(BF16)
+            o_all[g][:, o_place(core, k)] = o_buf[g][:, k * part_w : (k + 1) * part_w].astype(BF16)
         return c
 
     def heads_end(g, c):
         c.wait_recv()
         for k in range(kv_local):
-            o_all[g, :, o_place(1 - core, k)] = r3[g, :, k * part_w : (k + 1) * part_w].astype(BF16)
-
-    def y_copy(t):
-        return remote(y_send.at[t], y_recv.at[t], y_ss.at[t], y_rs.at[t], across_y)
-
-    def x_copy(t):
-        return remote(z_buf.at[t], x_recv.at[t], x_ss.at[t], x_rs.at[t], across_x)
-
-    def p1_copy(t):
-        return remote(z_buf.at[t], p1.at[t], p1_ss.at[t], p1_rs.at[t], partner)
-
-    def p2_copy(t):
-        return remote(x_recv.at[t], p2.at[t], p2_ss.at[t], p2_rs.at[t], partner)
-
-    def place(which_seqs, which_cols, t):
-        g, j = lax.div(t, chunks), lax.rem(t, chunks)
-        return seqs(which_seqs, g), pl.ds(pl.multiple_of(which_cols * cols + j * OUT_COLS, 128), OUT_COLS)
-
-    def out_copy(kind, q):
+            o_all[g][:, o_place(1 - core, k)] = r3[g][:, k * part_w : (k + 1) * part_w].astype(BF16)
+
+    def y_copy(g, j):
+        t = g * chunks + j
+        return remote(y_send[g].at[j], y_recv[g].at[j], y_ss.at[t], y_rs.at[t], across_y)
+
+    def x_copy(g, j):
+        t = g * chunks + j
+        return remote(z_buf[g].at[j], x_recv[g].at[j], x_ss.at[t], x_rs.at[t], across_x)
+
+    def p1_copy(g, j):
+        t = g * chunks + j
+        return remote(z_buf[g].at[j], p1[g].at[j], p1_ss.at[t], p1_rs.at[t], partner)
+
+    def p2_copy(g, j):
+        t = g * chunks + j
+        return remote(x_recv[g].at[j], p2[g].at[j], p2_ss.at[t], p2_rs.at[t], partner)
+
+    def out_copy(kind, g, j):
         which_seqs, which_cols = ((chip, core), (1 - chip, core), (chip, 1 - core), (1 - chip, 1 - core))[kind]
-        rows_at, _ = place(which_seqs, which_cols, q * OUT_CHUNKS)
-        j = lax.rem(q * OUT_CHUNKS, chunks)
-        cols_at = pl.ds(pl.multiple_of(which_cols * cols + j * OUT_COLS, 128), OUT_CHUNKS * OUT_COLS)
-        return pltpu.make_async_copy(y_ref.at[rows_at, cols_at], y_out.at[rows_at, cols_at], o_sem.at[kind, q])
-
-    def put_out(u, kinds):
-        @pl.when(lax.rem(u, OUT_CHUNKS) == OUT_CHUNKS - 1)
-        def _():
-            for kind in kinds:
-                out_copy(kind, lax.div(u, OUT_CHUNKS)).start()
-
-    def body(t, _):
-        @pl.when(t < total)
-        def _():
-            g, j = lax.div(t, chunks), lax.rem(t, chunks)
-
-            @pl.when(jnp.logical_and(g == 0, lax.rem(j, w_chunks) == 0))
+        cols_at = pl.ds(pl.multiple_of(which_cols * cols + j * OUT_COLS, 128), OUT_COLS)
+        return pltpu.make_async_copy(y_parts[g].at[kind, j], y_out.at[seqs(which_seqs, g), cols_at], o_sem.at[kind, g * chunks + j])
+
+    def put_out(kind, g, j, value):
+        y_parts[g][kind, j] = value
+        out_copy(kind, g, j).start()
+
+    def multiply(g, j):
+        if g == 0:
+            @pl.when(lax.rem(j, w_chunks) == 0)
             def _():
                 w_copy(lax.div(j, w_chunks)).wait()
 
-            w = w_buf[:, pl.ds(pl.multiple_of(j * OUT_COLS, 128), OUT_COLS)]
-            y_send[t] = jnp.dot(o_all[g], w, preferred_element_type=F32)
-            y_copy(t).start()
-
-        @pl.when(jnp.logical_and(t >= LAG_Y, t < total + LAG_Y))
-        def _():
-            u = t - LAG_Y
-            g, j = lax.div(u, chunks), lax.rem(u, chunks)
-            y_copy(u).wait_recv()
-            x_part = x_buf[pl.ds(pl.multiple_of(g * some, some), some), pl.ds(pl.multiple_of(j * OUT_COLS, 128), OUT_COLS)].astype(F32)
-            row = (core * cols + j * OUT_COLS) // head_dim
-            bias = jnp.concatenate([bo_f32[pl.ds(row + i, 1), :] for i in range(OUT_COLS // head_dim)], axis=1)
-            z = (x_part + (y_send[u] + y_recv[u]) + bias).astype(BF16)
-            z_buf[u] = z.astype(F32)
-            x_copy(u).start()
-            p1_copy(u).start()
-            rows_at, cols_at = place(chip, core, u)
-            y_ref[rows_at, cols_at] = z
-            put_out(u, (0,))
-
-        @pl.when(jnp.logical_and(t >= LAG_Y + LAG_X, t < total + LAG_Y + LAG_X))
-        def _():
-            u = t - (LAG_Y + LAG_X)
-            x_copy(u).wait_recv()
-            p2_copy(u).start()
-            rows_at, cols_at = place(1 - chip, core, u)
-            y_ref[rows_at, cols_at] = x_recv[u].astype(BF16)
-            p1_copy(u).wait_recv()
-            rows_at, cols_at = place(chip, 1 - core, u)
-            y_ref[rows_at, cols_at] = p1[u].astype(BF16)
-            put_out(u, (1, 2))
-
-        @pl.when(t >= LAG_Y + LAG_X + LAG_P)
-        def _():
-            u = t - (LAG_Y + LAG_X + LAG_P)
-            p2_copy(u).wait_recv()
-            rows_at, cols_at = place(1 - chip, 1 - core, u)
-            y_ref[rows_at, cols_at] = p2[u].astype(BF16)
-            put_out(u, (3,))
+        w = w_buf[:, pl.ds(pl.multiple_of(j * OUT_COLS, 128), OUT_COLS)]
+        y_send[g][j] = jnp.dot(o_all[g][...], w, preferred_element_type=F32)
+        y_copy(g, j).start()
+
+    def add(g, j):
+        y_copy(g, j).wait_recv()
+        x_part = x_buf[g][:, pl.ds(pl.multiple_of(j * OUT_COLS, 128), OUT_COLS)].astype(F32)
+        row = (core * cols + j * OUT_COLS) // head_dim
+        bias = jnp.concatenate([bo_f32[pl.ds(row + i, 1), :] for i in range(OUT_COLS // head_dim)], axis=1)
+        z = (x_part + (y_send[g][j] + y_recv[g][j]) + bias).astype(BF16)
+        z_buf[g][j] = z.astype(F32)
+        x_copy(g, j).start()
+        p1_copy(g, j).start()
+        put_out(0, g, j, z)
+
+    def spread(g, j):
+        x_copy(g, j).wait_recv()
+        p2_copy(g, j).start()
+        put_out(1, g, j, x_recv[g][j].astype(BF16))
+        p1_copy(g, j).wait_recv()
+        put_out(2, g, j, p1[g][j].astype(BF16))
+
+    def receive(g, j):
+        p2_copy(g, j).wait_recv()
+        put_out(3, g, j, p2[g][j].astype(BF16))
+
+    def body(t, _):
+        for stage, lag in ((multiply, 0), (add, LAG_Y), (spread, LAG_Y + LAG_X), (receive, LAG_Y + LAG_X + LAG_P)):
+            for g in range(chip_groups):
+                j = t - lag - g * chunks
+
+                @pl.when(jnp.logical_and(j >= 0, j < chunks))
+                def _():
+                    stage(g, j)
 
         return 0
 
-    half_group = per_group // 2
     heads_wait(0)
-    carry = attend(0, 0, per_group, (zero, zero))
+    carry = attend(0, 0, counts[0], (zero, zero))
     to_partner(0, carry)
-    x_copy_in.start()
+    for c in x_in:
+        c.start()
     heads_wait(1)
-    carry = attend(1, 0, half_group, (zero, zero))
+    carry = attend(1, 0, 2, (zero, zero))
     across(0)
-    carry = attend(1, half_group, per_group, carry)
+    carry = attend(1, 2, counts[1], carry)
     to_partner(1, carry)
     w_copy(0).start()
     heads_wait(2)
-    carry = attend(2, 0, half_group, (zero, zero))
+    carry = attend(2, 0, 2, (zero, zero))
     across(1)
     w_copy(1).start()
-    carry = attend(2, half_group, per_group, carry)
+    carry = attend(2, 2, counts[2], carry)
     to_partner(2, carry)
     for p in range(2, W_PARTS):
         w_copy(p).start()
     heads_wait(3)
-    carry = attend(3, 0, per_group, (zero, zero))
+    carry = attend(3, 0, counts[3], (zero, zero))
     to_partner(3, carry)
-    combine(2, own.at[0], own_ml.at[0])
-    combine(3, own.at[1], own_ml.at[1])
+    combine(2, own[0], own_ml.at[0])
+    combine(3, own[1], own_ml.at[1])
 
     c3 = [heads_start(0)]
     heads_end(0, c3[0])
-    x_copy_in.wait()
-    lax.fori_loop(0, chunks // 2, body, 0)
+    for c in x_in:
+        c.wait()
+    lax.fori_loop(0, chunks - 3, body, 0)
     c3.append(heads_start(1))
-    lax.fori_loop(chunks // 2, 3 * chunks // 4, body, 0)
+    lax.fori_loop(chunks - 3, chunks - 1, body, 0)
     heads_end(1, c3[1])
-    lax.fori_loop(3 * chunks // 4, total + LAG_Y + LAG_X + LAG_P, body, 0)
-
-    def tail(t, _):
-        y_copy(t).wait_send()
-        x_copy(t).wait_send()
-        p1_copy(t).wait_send()
-        p2_copy(t).wait_send()
-        return 0
-
-    lax.fori_loop(0, total, tail, 0)
-
-    def settle(q, _):
-        for kind in range(4):
-            out_copy(kind, q).wait()
-        return 0
-
-    lax.fori_loop(0, total // OUT_CHUNKS, settle, 0)
+    lax.fori_loop(chunks - 1, total + LAG_Y + LAG_X + LAG_P, body, 0)
+
+    for g in range(chip_groups):
+        def tail(j, _):
+            for copy in (y_copy, x_copy, p1_copy, p2_copy):
+                copy(g, j).wait_send()
+            for kind in range(4):
+                out_copy(kind, g, j).wait()
+            return 0
+
+        lax.fori_loop(0, chunks, tail, 0)
     for c in (*h_remote, *(c for pair in c1 + c2 for c in pair), *c3):
         c.wait_send()
 
@@ -560,16 +554,19 @@
     q_rows = sinks.shape[1]
     half_h, half_s = q_rows // 2, num_seqs // 2
     kv_local = half.shape[0] - half_h
-    some = half_s // SEQ_GROUPS
-    groups = 2 * SEQ_GROUPS
+    assert sum(SEQ_GROUPS) == half_s
+    order = SEQ_GROUPS * 2
+    chip_groups, groups = len(SEQ_GROUPS), len(order)
     width = w_o.shape[1]
     cols = width // 2
-    total = SEQ_GROUPS * (cols // OUT_COLS)
+    chunks = cols // OUT_COLS
+    total = chip_groups * chunks
     vmem = pl.BlockSpec(memory_space=pltpu.VMEM)
     anyspace = pl.BlockSpec(memory_space=pl.ANY)
-    chunked = pltpu.VMEM((total, some, OUT_COLS), F32)
-    parts = pltpu.VMEM((SEQ_GROUPS, half_h, some, head_dim), F32)
-    parts_ml = pltpu.VMEM((SEQ_GROUPS, 2 * half_h, 128), F32)
+    chunked = tuple(pltpu.VMEM((chunks, n, OUT_COLS), F32) for n in SEQ_GROUPS)
+    parts = tuple(pltpu.VMEM((half_h, n, head_dim), F32) for n in SEQ_GROUPS)
+    parts_ml = pltpu.VMEM((chip_groups, 2 * half_h, 128), F32)
+    o_parts = tuple(pltpu.VMEM((n, half_h * head_dim), F32) for n in SEQ_GROUPS)
     ring = pltpu.VMEM((ATT_SLOTS, ATT_SEQS, rows, head_dim), BF16)
     dma = pltpu.SemaphoreType.DMA
     return pl.pallas_call(
@@ -578,48 +575,53 @@
             jax.ShapeDtypeStruct((num_seqs, width), BF16),
             jax.ShapeDtypeStruct((2, num_seqs, kv_local, head_dim), BF16),
         ],
-        in_specs=[pl.BlockSpec(memory_space=pltpu.SMEM), anyspace, vmem, anyspace, vmem, anyspace, anyspace, anyspace],
+        in_specs=[anyspace] * 8,
         out_specs=[anyspace, vmem],
         scratch_shapes=[
-            pltpu.VMEM((num_seqs, width), BF16),
+            pltpu.SMEM((num_seqs,), jnp.int32),
+            pltpu.VMEM((1, q_rows), F32),
+            pltpu.VMEM((width // head_dim, head_dim), BF16),
+            dma((3,)),
+            tuple(pltpu.VMEM((4, chunks, n, OUT_COLS), BF16) for n in SEQ_GROUPS),
             pltpu.VMEM((w_o.shape[0], cols), BF16),
-            pltpu.VMEM((half_s, cols), BF16),
+            tuple(pltpu.VMEM((n, cols), BF16) for n in SEQ_GROUPS),
             pltpu.VMEM((q_rows + 2 * kv_local, num_seqs, head_dim), F32),
             ring, ring,
-            pltpu.VMEM((groups, q_rows, some, head_dim), F32),
+            tuple(pltpu.VMEM((q_rows, n, head_dim), F32) for n in order),
             pltpu.VMEM((groups, 2 * q_rows, 128), F32),
             pltpu.VMEM((q_rows, 128), F32),
             pltpu.VMEM((width // head_dim, head_dim), F32),
-            pltpu.VMEM((groups, half_h, some, head_dim), F32),
+            tuple(pltpu.VMEM((half_h, n, head_dim), F32) for n in order),
             pltpu.VMEM((groups, 2 * q_rows, 128), F32),
             parts, parts_ml, parts, parts_ml, parts, parts_ml,
-            pltpu.VMEM((SEQ_GROUPS, some, half_h * head_dim), F32),
-            pltpu.VMEM((SEQ_GROUPS, some, half_h * head_dim), F32),
-            pltpu.VMEM((SEQ_GROUPS, some, q_rows * head_dim), BF16),
+            o_parts, o_parts,
+            tuple(pltpu.VMEM((n, q_rows * head_dim), BF16) for n in SEQ_GROUPS),
             chunked, chunked, chunked, chunked, chunked, chunked,
-            dma((W_PARTS,)), dma, dma((ATT_SLOTS,)), dma((ATT_SLOTS,)),
+            dma((W_PARTS,)), dma((chip_groups,)), dma((ATT_SLOTS,)), dma((ATT_SLOTS,)),
             dma((2 * groups,)), dma((2 * groups,)), dma((2 * groups,)),
             dma((2 * groups,)), dma((2 * groups,)),
             dma((groups,)), dma((groups,)),
-            dma((SEQ_GROUPS,)), dma((SEQ_GROUPS,)),
+            dma((chip_groups,)), dma((chip_groups,)),
             *[dma((total,))] * 8,
-            dma((4, total // OUT_CHUNKS)),
+            dma((4, total)),
         ],
         compiler_params=pltpu.CompilerParams(collective_id=1, has_side_effects=True, vmem_limit_bytes=62 << 20),
         name="finish",
     )(seq_lens, half, sinks, hidden, b_o.reshape(width // head_dim, head_dim), w_o, k_rows, v_rows)
 
 
-LAST_PARTS = 4
+LAST_PARTS = 8
 LAST_UNROLL = 8
 
 
-def last_kernel(lens_ref, y_hbm, new_hbm, k_in, v_in, y_out, k_out, v_out, y_buf, new_ref, in_sem, out_sem, new_sem, k_sem, v_sem):
+def last_kernel(lens_hbm, y_hbm, new_hbm, k_in, v_in, y_out, k_out, v_out, lens_ref, lens_sem, y_buf, new_ref, in_sem, out_sem, new_sem, k_sem, v_sem):
     num_seqs, ctx_local = k_out.shape[:2]
     base = lax.axis_index("sp") * ctx_local
     rows = y_hbm.shape[0] // LAST_PARTS
     new_copy = pltpu.make_async_copy(new_hbm, new_ref, new_sem)
     new_copy.start()
+    lens_copy = pltpu.make_async_copy(lens_hbm, lens_ref, lens_sem)
+    lens_copy.start()
     loads, stores = [], []
     for p in range(LAST_PARTS):
         at = pl.ds(p * rows, rows)
@@ -641,6 +643,7 @@
 
         lax.fori_loop(0, num_seqs // LAST_UNROLL, step, 0)
 
+    lens_copy.wait()
     new_copy.wait()
     for_new_rows(lambda c: c.start())
     for p in range(LAST_PARTS):
@@ -657,9 +660,9 @@
     return pl.pallas_call(
         last_kernel,
         out_shape=[jax.ShapeDtypeStruct(a.shape, a.dtype) for a in (y, k_copy, v_copy)],
-        in_specs=[pl.BlockSpec(memory_space=pltpu.SMEM)] + [anyspace] * 4,
+        in_specs=[anyspace] * 5,
         out_specs=[anyspace] * 3,
-        scratch_shapes=[pltpu.VMEM(y.shape, y.dtype), pltpu.VMEM(new.shape, new.dtype), dma((LAST_PARTS,)), dma((LAST_PARTS,)), dma, dma, dma],
+        scratch_shapes=[pltpu.SMEM(seq_lens.shape, jnp.int32), dma, pltpu.VMEM(y.shape, y.dtype), pltpu.VMEM(new.shape, new.dtype), dma((LAST_PARTS,)), dma((LAST_PARTS,)), dma, dma, dma],
         input_output_aliases={3: 1, 4: 2},
         compiler_params=pltpu.CompilerParams(vmem_limit_bytes=60 << 20),
         name="last",

time: 86.6 us -> 86.5 us (level)
  no operation moved by 1% of the time
where the time goes in v8:
time: 86.5 us; the launch traced here: 86.3 us
  Pallas kernels  85.6 us (99%)
    pallas_call x1, Pallas kernels, finish(): pl.pallas_call(finish_kernel, out_shape=[jax.ShapeDtypeStruct((num_seqs,...  53 us
    pallas_call x1, Pallas kernels, project(): pl.pallas_call(project_kernel, out_shape=[jax.ShapeDtypeStruct((rows, num...  29.1 us
    pallas_call x1, Pallas kernels, last(): pl.pallas_call(last_kernel, out_shape=[jax.ShapeDtypeStruct(a.shape, a.dt...  3.55 us

profile of v8, /device:TPU:0, one launch (start us, length us, event | category | flops | bytes accessed | tf_op | source)
XLA Modules:
  0.0 86.3 jit_solution(2513990027907605526)
XLA Ops:
  0.6 29.1 %project.1 = (f32[20,128,128]{2,1,0:T(8,128)}, bf16[128,256,128]{2,1,0:T(8,128)(2,1)}, bf16[128,256,128]{2,1,0:T(8,128)(2,1)}) custom-call(bf16[128,8192]{1,0:T(8,128)(2,1)} %hid_ref.1, bf16[64,128]{1,0:T(8,128)(2,1)} %bitcast.18, f32[64,128]{1,0:T(8,128)} %bitcast.15, f32[64,128]{1,0:T(8,128)} %bitcast.16, bf16[4,1280]{1,0:T(4,128)(2,1)} %bias_hbm.1, ...), custom_call_target="tpu_custom_call" | custom-call | tf_op jit(solution)/shard_map/project/pallas_call | solution.py:189
  29.8 53.0 %finish.1 = (bf16[128,8192]{1,0:T(8,128)(2,1)}, bf16[2,128,4,128]{3,2,1,0:T(4,128)(2,1)}) custom-call(s32[128]{0:T(128)} %lens_hbm.3, f32[20,128,128]{2,1,0:T(8,128)} %get-tuple-element.8.half_hbm, f32[1,32]{1,0:T(1,128)} %bitcast.19, bf16[128,8192]{1,0:T(8,128)(2,1)} %hid_ref.1, bf16[64,128]{1,0:T(8,128)(2,1)} %bitcast.17, bf16[4096,8192]{1,0:T(8,128)(2,1)} %wo_ref.1, ...), custom_call_target="tpu_custom_call" | custom-call | tf_op jit(solution)/shard_map/finish/pallas_call | solution.py:572
  82.7 3.6 %last.1 = (bf16[128,8192]{1,0:T(8,128)(2,1)}, bf16[128,64,4,128]{3,2,1,0:T(4,128)(2,1)}, bf16[128,64,4,128]{3,2,1,0:T(4,128)(2,1)}) custom-call(s32[128]{0:T(128)} %lens_hbm.3, bf16[128,8192]{1,0:T(8,128)(2,1)} %get-tuple-element.9.y_hbm, bf16[2,128,4,128]{3,2,1,0:T(4,128)(2,1)} %get-tuple-element.10.new_hbm, ...), custom_call_target="tpu_custom_call", output_to_operand_aliasing={{1}: (3, {}), {2}: (4, {})} | custom-call | tf_op jit(solution)/shard_map/last/pallas_call | solution.py:660

commit v9 on v8

--- a/solution.py
+++ b/solution.py
@@ -34,8 +34,8 @@
 QKV_ROWS = 1024
 QKV_SLOTS = 3
 CACHE_SEQS = 16
-CACHE_AHEAD = 1
-CACHE_FIRST = 0
+CACHE_AHEAD = 4
+CACHE_FIRST = 1
 X_PARTS = 4
 
 
@@ -224,6 +224,7 @@
 ATT_SLOTS = 6
 OUT_COLS = 512
 SEQ_GROUPS = (24, 40)
+PIECES = ((0, 0, 8), (0, 8, 16), (1, 0, 40))
 W_PARTS = 8
 LAG_Y = 3
 LAG_X = 3
@@ -256,8 +257,8 @@
     mine = pl.multiple_of(core * half_h, half_h)
     theirs = pl.multiple_of((1 - core) * half_h, half_h)
 
-    def seqs(which, g):
-        return pl.ds(pl.multiple_of(which * half_s + offsets[g], 8), SEQ_GROUPS[g])
+    def seqs(which, g, first=0, count=None):
+        return pl.ds(pl.multiple_of(which * half_s + offsets[g] + first, 8), SEQ_GROUPS[g] if count is None else count)
 
     small = [pltpu.make_async_copy(src, dst, small_sem.at[i]) for i, (src, dst) in enumerate(((lens_hbm, lens_ref), (sink_hbm, sink_ref), (bo_hbm, bo_ref)))]
     for c in small:
@@ -266,19 +267,19 @@
     for peer in (partner, across_x, across_y):
         pl.semaphore_signal(barrier, inc=1, device_id=peer, device_id_type=MESH)
 
-    order = [(1 - chip, g) for g in range(chip_groups)] + [(chip, g) for g in range(chip_groups)]
+    order = [(1 - chip, *piece) for piece in PIECES] + [(chip, g, 0, n) for g, n in enumerate(SEQ_GROUPS)]
     own_rows = (pl.ds(mine, half_h), pl.ds(pl.multiple_of(q_rows + kv_local * core, kv_local), kv_local))
     src_rows = (pl.ds(0, half_h), pl.ds(half_h, kv_local))
     h_local, h_remote = [], []
-    for i, (which, g) in enumerate(order):
-        at = seqs(which, g)
+    for i, piece in enumerate(order):
+        at = seqs(*piece)
         for j in range(2):
             h_local.append(pltpu.make_async_copy(half_hbm.at[src_rows[j], at], h_buf.at[own_rows[j], at], h_in.at[2 * i + j]))
             h_local[-1].start()
             h_remote.append(remote(half_hbm.at[src_rows[j], at], h_buf.at[own_rows[j], at], h_send.at[2 * i + j], h_recv.at[2 * i + j], partner))
 
     steps = num_seqs // ATT_SEQS
-    counts = [n // ATT_SEQS for n in SEQ_GROUPS] * 2
+    counts = [n // ATT_SEQS for _, _, _, n in order]
     starts = [sum(counts[:i]) for i in range(len(counts))]
 
     def block(p):
@@ -344,7 +345,7 @@
             sums = [sums[s] + jnp.dot(extra[s].astype(BF16), new_v[s], preferred_element_type=F32) for s in batch]
             out = num[i].at[:, pl.ds(pl.multiple_of(t * ATT_SEQS, ATT_SEQS), ATT_SEQS)]
             for s in batch:
-                here = lane == t * ATT_SEQS + s
+                here = lane == order[i][2] + t * ATT_SEQS + s
                 m_all = jnp.where(here, tops[s], m_all)
                 l_all = jnp.where(here, totals[s], l_all)
                 out[:, s, :] = sums[s]
@@ -390,16 +391,19 @@
         dst_ml[0:half_h] = m_chip
         dst_ml[half_h : 2 * half_h] = l_a * f_a + l_b * f_b
         f_a, f_b = f_a.T, f_b.T
+        some = slice(order[i][2], order[i][2] + order[i][3])
         for h in range(half_h):
-            dst[h] = num[i][mine + h] * f_a[0 : dst.shape[1], h : h + 1] + r1[i][h] * f_b[0 : dst.shape[1], h : h + 1]
+            dst[h, some] = num[i][mine + h] * f_a[some, h : h + 1] + r1[i][h] * f_b[some, h : h + 1]
 
     c2 = []
 
-    def across(g):
-        combine(g, away[g], away_ml.at[g])
+    def across(i):
+        _, g, first, count = order[i]
+        combine(i, away[g], away_ml.at[i])
+        at = pl.ds(first, count)
         c2.append((
-            remote(away_ml.at[g], r2ml.at[g], s2_send.at[2 * g], s2_recv.at[2 * g], across_x),
-            remote(away[g], r2[g], s2_send.at[2 * g + 1], s2_recv.at[2 * g + 1], across_x),
+            remote(away_ml.at[i], r2ml.at[i], s2_send.at[2 * i], s2_recv.at[2 * i], across_x),
+            remote(away[g].at[:, at], r2[g].at[:, at], s2_send.at[2 * i + 1], s2_recv.at[2 * i + 1], across_x),
         ))
         for c in c2[-1]:
             c.start()
@@ -411,10 +415,18 @@
         return pl.ds(pl.multiple_of(2 * k * part_w + which_half * part_w, 128), part_w)
 
     def heads_start(g):
-        for c in c2[g]:
-            c.wait_recv()
         m_a, l_a = own_ml[g, 0:half_h], own_ml[g, half_h : 2 * half_h]
-        m_b, l_b = r2ml[g, 0:half_h], r2ml[g, half_h : 2 * half_h]
+        m_b, l_b = None, None
+        for i, (group, first, _) in enumerate(PIECES):
+            if group == g:
+                for c in c2[i]:
+                    c.wait_recv()
+                m_i, l_i = r2ml[i, 0:half_h], r2ml[i, half_h : 2 * half_h]
+                if m_b is None:
+                    m_b, l_b = m_i, l_i
+                else:
+                    m_b = jnp.where(lane[0:half_h] < first, m_b, m_i)
+                    l_b = jnp.where(lane[0:half_h] < first, l_b, l_i)
         m_top = jnp.maximum(m_a, m_b)
         f_a = jnp.exp(m_a - m_top)
         f_b = jnp.exp(m_b - m_top)
@@ -502,29 +514,28 @@
         return 0
 
     heads_wait(0)
-    carry = attend(0, 0, counts[0], (zero, zero))
-    to_partner(0, carry)
-    for c in x_in:
-        c.start()
+    to_partner(0, attend(0, 0, counts[0], (zero, zero)))
     heads_wait(1)
-    carry = attend(1, 0, 2, (zero, zero))
+    to_partner(1, attend(1, 0, counts[1], (zero, zero)))
     across(0)
-    carry = attend(1, 2, counts[1], carry)
-    to_partner(1, carry)
-    w_copy(0).start()
     heads_wait(2)
     carry = attend(2, 0, 2, (zero, zero))
     across(1)
+    for c in x_in:
+        c.start()
+    to_partner(2, attend(2, 2, counts[2], carry))
+    w_copy(0).start()
+    heads_wait(3)
+    carry = attend(3, 0, counts[3], (zero, zero))
+    across(2)
     w_copy(1).start()
-    carry = attend(2, 2, counts[2], carry)
-    to_partner(2, carry)
+    to_partner(3, carry)
     for p in range(2, W_PARTS):
         w_copy(p).start()
-    heads_wait(3)
-    carry = attend(3, 0, counts[3], (zero, zero))
-    to_partner(3, carry)
-    combine(2, own[0], own_ml.at[0])
-    combine(3, own[1], own_ml.at[1])
+    heads_wait(4)
+    to_partner(4, attend(4, 0, counts[4], (zero, zero)))
+    combine(3, own[0], own_ml.at[0])
+    combine(4, own[1], own_ml.at[1])
 
     c3 = [heads_start(0)]
     heads_end(0, c3[0])
@@ -555,7 +566,7 @@
     half_h, half_s = q_rows // 2, num_seqs // 2
     kv_local = half.shape[0] - half_h
     assert sum(SEQ_GROUPS) == half_s
-    order = SEQ_GROUPS * 2
+    order = tuple(n for _, _, n in PIECES) + SEQ_GROUPS
     chip_groups, groups = len(SEQ_GROUPS), len(order)
     width = w_o.shape[1]
     cols = width // 2
@@ -565,7 +576,8 @@
     anyspace = pl.BlockSpec(memory_space=pl.ANY)
     chunked = tuple(pltpu.VMEM((chunks, n, OUT_COLS), F32) for n in SEQ_GROUPS)
     parts = tuple(pltpu.VMEM((half_h, n, head_dim), F32) for n in SEQ_GROUPS)
-    parts_ml = pltpu.VMEM((chip_groups, 2 * half_h, 128), F32)
+    own_ml = pltpu.VMEM((chip_groups, 2 * half_h, 128), F32)
+    piece_ml = pltpu.VMEM((len(PIECES), 2 * half_h, 128), F32)
     o_parts = tuple(pltpu.VMEM((n, half_h * head_dim), F32) for n in SEQ_GROUPS)
     ring = pltpu.VMEM((ATT_SLOTS, ATT_SEQS, rows, head_dim), BF16)
     dma = pltpu.SemaphoreType.DMA
@@ -593,14 +605,14 @@
             pltpu.VMEM((width // head_dim, head_dim), F32),
             tuple(pltpu.VMEM((half_h, n, head_dim), F32) for n in order),
             pltpu.VMEM((groups, 2 * q_rows, 128), F32),
-            parts, parts_ml, parts, parts_ml, parts, parts_ml,
+            parts, own_ml, parts, piece_ml, parts, piece_ml,
             o_parts, o_parts,
             tuple(pltpu.VMEM((n, q_rows * head_dim), BF16) for n in SEQ_GROUPS),
             chunked, chunked, chunked, chunked, chunked, chunked,
             dma((W_PARTS,)), dma((chip_groups,)), dma((ATT_SLOTS,)), dma((ATT_SLOTS,)),
             dma((2 * groups,)), dma((2 * groups,)), dma((2 * groups,)),
             dma((2 * groups,)), dma((2 * groups,)),
-            dma((groups,)), dma((groups,)),
+            dma((2 * len(PIECES),)), dma((2 * len(PIECES),)),
             dma((chip_groups,)), dma((chip_groups,)),
             *[dma((total,))] * 8,
             dma((4, total)),

time: 86.5 us -> 87 us (level)
  no operation moved by 1% of the time
where the time goes in v9:
time: 87 us; the launch traced here: 86.8 us
  Pallas kernels  86.1 us (99%)
    pallas_call x1, Pallas kernels, finish(): pl.pallas_call(finish_kernel, out_shape=[jax.ShapeDtypeStruct((num_seqs,...  52.9 us
    pallas_call x1, Pallas kernels, project(): pl.pallas_call(project_kernel, out_shape=[jax.ShapeDtypeStruct((rows, num...  29.7 us
    pallas_call x1, Pallas kernels, last(): pl.pallas_call(last_kernel, out_shape=[jax.ShapeDtypeStruct(a.shape, a.dt...  3.58 us

profile of v9, /device:TPU:0, one launch (start us, length us, event | category | flops | bytes accessed | tf_op | source)
XLA Modules:
  0.0 86.8 jit_solution(11007791133958251576)
XLA Ops:
  0.6 29.7 %project.1 = (f32[20,128,128]{2,1,0:T(8,128)}, bf16[128,256,128]{2,1,0:T(8,128)(2,1)}, bf16[128,256,128]{2,1,0:T(8,128)(2,1)}) custom-call(bf16[128,8192]{1,0:T(8,128)(2,1)} %hid_ref.1, bf16[64,128]{1,0:T(8,128)(2,1)} %bitcast.18, f32[64,128]{1,0:T(8,128)} %bitcast.15, f32[64,128]{1,0:T(8,128)} %bitcast.16, bf16[4,1280]{1,0:T(4,128)(2,1)} %bias_hbm.1, ...), custom_call_target="tpu_custom_call" | custom-call | tf_op jit(solution)/shard_map/project/pallas_call | solution.py:189
  30.3 52.9 %finish.1 = (bf16[128,8192]{1,0:T(8,128)(2,1)}, bf16[2,128,4,128]{3,2,1,0:T(4,128)(2,1)}) custom-call(s32[128]{0:T(128)} %lens_hbm.3, f32[20,128,128]{2,1,0:T(8,128)} %get-tuple-element.8.half_hbm, f32[1,32]{1,0:T(1,128)} %bitcast.19, bf16[128,8192]{1,0:T(8,128)(2,1)} %hid_ref.1, bf16[64,128]{1,0:T(8,128)(2,1)} %bitcast.17, bf16[4096,8192]{1,0:T(8,128)(2,1)} %wo_ref.1, ...), custom_call_target="tpu_custom_call" | custom-call | tf_op jit(solution)/shard_map/finish/pallas_call | solution.py:584
  83.2 3.6 %last.1 = (bf16[128,8192]{1,0:T(8,128)(2,1)}, bf16[128,64,4,128]{3,2,1,0:T(4,128)(2,1)}, bf16[128,64,4,128]{3,2,1,0:T(4,128)(2,1)}) custom-call(s32[128]{0:T(128)} %lens_hbm.3, bf16[128,8192]{1,0:T(8,128)(2,1)} %get-tuple-element.9.y_hbm, bf16[2,128,4,128]{3,2,1,0:T(4,128)(2,1)} %get-tuple-element.10.new_hbm, ...), custom_call_target="tpu_custom_call", output_to_operand_aliasing={{1}: (3, {}), {2}: (4, {})} | custom-call | tf_op jit(solution)/shard_map/last/pallas_call | solution.py:672

commit v10 on v9

--- a/solution.py
+++ b/solution.py
@@ -34,8 +34,8 @@
 QKV_ROWS = 1024
 QKV_SLOTS = 3
 CACHE_SEQS = 16
-CACHE_AHEAD = 4
-CACHE_FIRST = 1
+CACHE_AHEAD = 2
+CACHE_FIRST = 0
 X_PARTS = 4
 
 
@@ -301,6 +301,8 @@
     def w_copy(p):
         return pltpu.make_async_copy(wo_ref.at[:, pl.ds(pl.multiple_of(core * cols + p * w_cols, 128), w_cols)], w_buf.at[:, pl.ds(pl.multiple_of(p * w_cols, 128), w_cols)], w_sem.at[p])
 
+    w_copy(0).start()
+    w_copy(1).start()
     for c in small:
         c.wait()
     sink = sink_column(sink_ref, q_rows, 2, 2 * part_h)
@@ -518,20 +520,21 @@
     heads_wait(1)
     to_partner(1, attend(1, 0, counts[1], (zero, zero)))
     across(0)
+    w_copy(2).start()
     heads_wait(2)
     carry = attend(2, 0, 2, (zero, zero))
     across(1)
     for c in x_in:
         c.start()
+    w_copy(3).start()
     to_partner(2, attend(2, 2, counts[2], carry))
-    w_copy(0).start()
+    w_copy(4).start()
     heads_wait(3)
     carry = attend(3, 0, counts[3], (zero, zero))
     across(2)
-    w_copy(1).start()
+    for p in range(5, W_PARTS):
+        w_copy(p).start()
     to_partner(3, carry)
-    for p in range(2, W_PARTS):
-        w_copy(p).start()
     heads_wait(4)
     to_partner(4, attend(4, 0, counts[4], (zero, zero)))
     combine(3, own[0], own_ml.at[0])

time: 87 us -> 86.2 us (level)
  Pallas kernels: 86.1 us -> 85.2 us
    pallas_call x1, Pallas kernels: 29.7 us -> 28.5 us  [project(): pl.pallas_call(project_kernel, out_shape=[jax.ShapeDtypeStruct((rows, num...]
where the time goes in v10:
time: 86.2 us; the launch traced here: 85.9 us
  Pallas kernels  85.2 us (99%)
    pallas_call x1, Pallas kernels, finish(): pl.pallas_call(finish_kernel, out_shape=[jax.ShapeDtypeStruct((num_seqs,...  53.2 us
    pallas_call x1, Pallas kernels, project(): pl.pallas_call(project_kernel, out_shape=[jax.ShapeDtypeStruct((rows, num...  28.5 us
    pallas_call x1, Pallas kernels, last(): pl.pallas_call(last_kernel, out_shape=[jax.ShapeDtypeStruct(a.shape, a.dt...  3.48 us

profile of v10, /device:TPU:0, one launch (start us, length us, event | category | flops | bytes accessed | tf_op | source)
XLA Modules:
  0.0 85.9 jit_solution(12133594999216051745)
XLA Ops:
  0.6 28.5 %project.1 = (f32[20,128,128]{2,1,0:T(8,128)}, bf16[128,256,128]{2,1,0:T(8,128)(2,1)}, bf16[128,256,128]{2,1,0:T(8,128)(2,1)}) custom-call(bf16[128,8192]{1,0:T(8,128)(2,1)} %hid_ref.1, bf16[64,128]{1,0:T(8,128)(2,1)} %bitcast.18, f32[64,128]{1,0:T(8,128)} %bitcast.15, f32[64,128]{1,0:T(8,128)} %bitcast.16, bf16[4,1280]{1,0:T(4,128)(2,1)} %bias_hbm.1, ...), custom_call_target="tpu_custom_call" | custom-call | tf_op jit(solution)/shard_map/project/pallas_call | solution.py:189
  29.2 53.2 %finish.1 = (bf16[128,8192]{1,0:T(8,128)(2,1)}, bf16[2,128,4,128]{3,2,1,0:T(4,128)(2,1)}) custom-call(s32[128]{0:T(128)} %lens_hbm.3, f32[20,128,128]{2,1,0:T(8,128)} %get-tuple-element.8.half_hbm, f32[1,32]{1,0:T(1,128)} %bitcast.19, bf16[128,8192]{1,0:T(8,128)(2,1)} %hid_ref.1, bf16[64,128]{1,0:T(8,128)(2,1)} %bitcast.17, bf16[4096,8192]{1,0:T(8,128)(2,1)} %wo_ref.1, ...), custom_call_target="tpu_custom_call" | custom-call | tf_op jit(solution)/shard_map/finish/pallas_call | solution.py:587
  82.4 3.5 %last.1 = (bf16[128,8192]{1,0:T(8,128)(2,1)}, bf16[128,64,4,128]{3,2,1,0:T(4,128)(2,1)}, bf16[128,64,4,128]{3,2,1,0:T(4,128)(2,1)}) custom-call(s32[128]{0:T(128)} %lens_hbm.3, bf16[128,8192]{1,0:T(8,128)(2,1)} %get-tuple-element.9.y_hbm, bf16[2,128,4,128]{3,2,1,0:T(4,128)(2,1)} %get-tuple-element.10.new_hbm, ...), custom_call_target="tpu_custom_call", output_to_operand_aliasing={{1}: (3, {}), {2}: (4, {})} | custom-call | tf_op jit(solution)/shard_map/last/pallas_call | solution.py:675

commit v11 on v10

--- a/solution.py
+++ b/solution.py
@@ -222,13 +222,13 @@
 
 ATT_SEQS = 8
 ATT_SLOTS = 6
-OUT_COLS = 512
+OUT_COLS = 256
 SEQ_GROUPS = (24, 40)
 PIECES = ((0, 0, 8), (0, 8, 16), (1, 0, 40))
 W_PARTS = 8
-LAG_Y = 3
-LAG_X = 3
-LAG_P = 1
+LAG_Y = 6
+LAG_X = 8
+LAG_P = 2
 
 
 def finish_kernel(lens_hbm, half_hbm, sink_hbm, hid_ref, bo_hbm, wo_ref, k_hbm, v_hbm, y_out, new_ref,
@@ -544,11 +544,11 @@
     heads_end(0, c3[0])
     for c in x_in:
         c.wait()
-    lax.fori_loop(0, chunks - 3, body, 0)
+    lax.fori_loop(0, chunks - 6, body, 0)
     c3.append(heads_start(1))
-    lax.fori_loop(chunks - 3, chunks - 1, body, 0)
+    lax.fori_loop(chunks - 6, chunks - 2, body, 0)
     heads_end(1, c3[1])
-    lax.fori_loop(chunks - 1, total + LAG_Y + LAG_X + LAG_P, body, 0)
+    lax.fori_loop(chunks - 2, total + LAG_Y + LAG_X + LAG_P, body, 0)
 
     for g in range(chip_groups):
         def tail(j, _):

time: 86.2 us -> 87.8 us (1.019)
  Pallas kernels: 85.2 us -> 87 us
    pallas_call x1, Pallas kernels: 53.2 us -> 54.9 us  [finish(): pl.pallas_call(finish_kernel, out_shape=[jax.ShapeDtypeStruct((num_seqs,...]
where the time goes in v11:
time: 87.8 us; the launch traced here: 87.6 us
  Pallas kernels  87 us (99%)
    pallas_call x1, Pallas kernels, finish(): pl.pallas_call(finish_kernel, out_shape=[jax.ShapeDtypeStruct((num_seqs,...  54.9 us
    pallas_call x1, Pallas kernels, project(): pl.pallas_call(project_kernel, out_shape=[jax.ShapeDtypeStruct((rows, num...  28.5 us
    pallas_call x1, Pallas kernels, last(): pl.pallas_call(last_kernel, out_shape=[jax.ShapeDtypeStruct(a.shape, a.dt...  3.57 us

profile of v11, /device:TPU:0, one launch (start us, length us, event | category | flops | bytes accessed | tf_op | source)
XLA Modules:
  0.0 87.6 jit_solution(613169137415261137)
XLA Ops:
  0.6 28.5 %project.1 = (f32[20,128,128]{2,1,0:T(8,128)}, bf16[128,256,128]{2,1,0:T(8,128)(2,1)}, bf16[128,256,128]{2,1,0:T(8,128)(2,1)}) custom-call(bf16[128,8192]{1,0:T(8,128)(2,1)} %hid_ref.1, bf16[64,128]{1,0:T(8,128)(2,1)} %bitcast.18, f32[64,128]{1,0:T(8,128)} %bitcast.15, f32[64,128]{1,0:T(8,128)} %bitcast.16, bf16[4,1280]{1,0:T(4,128)(2,1)} %bias_hbm.1, ...), custom_call_target="tpu_custom_call" | custom-call | tf_op jit(solution)/shard_map/project/pallas_call | solution.py:189
  29.2 54.9 %finish.1 = (bf16[128,8192]{1,0:T(8,128)(2,1)}, bf16[2,128,4,128]{3,2,1,0:T(4,128)(2,1)}) custom-call(s32[128]{0:T(128)} %lens_hbm.3, f32[20,128,128]{2,1,0:T(8,128)} %get-tuple-element.8.half_hbm, f32[1,32]{1,0:T(1,128)} %bitcast.19, bf16[128,8192]{1,0:T(8,128)(2,1)} %hid_ref.1, bf16[64,128]{1,0:T(8,128)(2,1)} %bitcast.17, bf16[4096,8192]{1,0:T(8,128)(2,1)} %wo_ref.1, ...), custom_call_target="tpu_custom_call" | custom-call | tf_op jit(solution)/shard_map/finish/pallas_call | solution.py:587
  84.1 3.6 %last.1 = (bf16[128,8192]{1,0:T(8,128)(2,1)}, bf16[128,64,4,128]{3,2,1,0:T(4,128)(2,1)}, bf16[128,64,4,128]{3,2,1,0:T(4,128)(2,1)}) custom-call(s32[128]{0:T(128)} %lens_hbm.3, bf16[128,8192]{1,0:T(8,128)(2,1)} %get-tuple-element.9.y_hbm, bf16[2,128,4,128]{3,2,1,0:T(4,128)(2,1)} %get-tuple-element.10.new_hbm, ...), custom_call_target="tpu_custom_call", output_to_operand_aliasing={{1}: (3, {}), {2}: (4, {})} | custom-call | tf_op jit(solution)/shard_map/last/pallas_call | solution.py:675

commit v12 on v10

--- a/solution.py
+++ b/solution.py
@@ -223,11 +223,11 @@
 ATT_SEQS = 8
 ATT_SLOTS = 6
 OUT_COLS = 512
-SEQ_GROUPS = (24, 40)
-PIECES = ((0, 0, 8), (0, 8, 16), (1, 0, 40))
+SEQ_GROUPS = (24, 24, 16)
+PIECES = ((0, 0, 8), (0, 8, 16), (1, 0, 24), (2, 0, 16))
 W_PARTS = 8
-LAG_Y = 3
-LAG_X = 3
+LAG_Y = 4
+LAG_X = 4
 LAG_P = 1
 
 
@@ -532,23 +532,31 @@
     heads_wait(3)
     carry = attend(3, 0, counts[3], (zero, zero))
     across(2)
+    to_partner(3, carry)
     for p in range(5, W_PARTS):
         w_copy(p).start()
-    to_partner(3, carry)
     heads_wait(4)
-    to_partner(4, attend(4, 0, counts[4], (zero, zero)))
-    combine(3, own[0], own_ml.at[0])
-    combine(4, own[1], own_ml.at[1])
+    carry = attend(4, 0, counts[4], (zero, zero))
+    across(3)
+    to_partner(4, carry)
+    for i in (5, 6):
+        heads_wait(i)
+        to_partner(i, attend(i, 0, counts[i], (zero, zero)))
+    for g in range(chip_groups):
+        combine(len(PIECES) + g, own[g], own_ml.at[g])
 
     c3 = [heads_start(0)]
     heads_end(0, c3[0])
     for c in x_in:
         c.wait()
-    lax.fori_loop(0, chunks - 3, body, 0)
-    c3.append(heads_start(1))
-    lax.fori_loop(chunks - 3, chunks - 1, body, 0)
-    heads_end(1, c3[1])
-    lax.fori_loop(chunks - 1, total + LAG_Y + LAG_X + LAG_P, body, 0)
+    done = 0
+    for g in range(1, chip_groups):
+        lax.fori_loop(done, g * chunks - 4, body, 0)
+        c3.append(heads_start(g))
+        lax.fori_loop(g * chunks - 4, g * chunks - 2, body, 0)
+        heads_end(g, c3[g])
+        done = g * chunks - 2
+    lax.fori_loop(done, total + LAG_Y + LAG_X + LAG_P, body, 0)
 
     for g in range(chip_groups):
         def tail(j, _):

time: 86.2 us -> 90.9 us (1.055)
  Pallas kernels: 85.2 us -> 89.9 us
    pallas_call x1, Pallas kernels: 53.2 us -> 57.8 us  [finish(): pl.pallas_call(finish_kernel, out_shape=[jax.ShapeDtypeStruct((num_seqs,...]
where the time goes in v12:
time: 90.9 us; the launch traced here: 90.7 us
  Pallas kernels  89.9 us (99%)
    pallas_call x1, Pallas kernels, finish(): pl.pallas_call(finish_kernel, out_shape=[jax.ShapeDtypeStruct((num_seqs,...  57.8 us
    pallas_call x1, Pallas kernels, project(): pl.pallas_call(project_kernel, out_shape=[jax.ShapeDtypeStruct((rows, num...  28.6 us
    pallas_call x1, Pallas kernels, last(): pl.pallas_call(last_kernel, out_shape=[jax.ShapeDtypeStruct(a.shape, a.dt...  3.5 us

profile of v12, /device:TPU:0, one launch (start us, length us, event | category | flops | bytes accessed | tf_op | source)
XLA Modules:
  0.0 90.7 jit_solution(3716776770968943856)
XLA Ops:
  0.6 28.6 %project.1 = (f32[20,128,128]{2,1,0:T(8,128)}, bf16[128,256,128]{2,1,0:T(8,128)(2,1)}, bf16[128,256,128]{2,1,0:T(8,128)(2,1)}) custom-call(bf16[128,8192]{1,0:T(8,128)(2,1)} %hid_ref.1, bf16[64,128]{1,0:T(8,128)(2,1)} %bitcast.18, f32[64,128]{1,0:T(8,128)} %bitcast.15, f32[64,128]{1,0:T(8,128)} %bitcast.16, bf16[4,1280]{1,0:T(4,128)(2,1)} %bias_hbm.1, ...), custom_call_target="tpu_custom_call" | custom-call | tf_op jit(solution)/shard_map/project/pallas_call | solution.py:189
  29.2 57.8 %finish.1 = (bf16[128,8192]{1,0:T(8,128)(2,1)}, bf16[2,128,4,128]{3,2,1,0:T(4,128)(2,1)}) custom-call(s32[128]{0:T(128)} %lens_hbm.3, f32[20,128,128]{2,1,0:T(8,128)} %get-tuple-element.8.half_hbm, f32[1,32]{1,0:T(1,128)} %bitcast.19, bf16[128,8192]{1,0:T(8,128)(2,1)} %hid_ref.1, bf16[64,128]{1,0:T(8,128)(2,1)} %bitcast.17, bf16[4096,8192]{1,0:T(8,128)(2,1)} %wo_ref.1, ...), custom_call_target="tpu_custom_call" | custom-call | tf_op jit(solution)/shard_map/finish/pallas_call | solution.py:595
  87.0 3.5 %last.1 = (bf16[128,8192]{1,0:T(8,128)(2,1)}, bf16[128,64,4,128]{3,2,1,0:T(4,128)(2,1)}, bf16[128,64,4,128]{3,2,1,0:T(4,128)(2,1)}) custom-call(s32[128]{0:T(128)} %lens_hbm.3, bf16[128,8192]{1,0:T(8,128)(2,1)} %get-tuple-element.9.y_hbm, bf16[2,128,4,128]{3,2,1,0:T(4,128)(2,1)} %get-tuple-element.10.new_hbm, ...), custom_call_target="tpu_custom_call", output_to_operand_aliasing={{1}: (3, {}), {2}: (4, {})} | custom-call | tf_op jit(solution)/shard_map/last/pallas_call | solution.py:683

commit v13 on v9

--- a/solution.py
+++ b/solution.py
@@ -34,8 +34,8 @@
 QKV_ROWS = 1024
 QKV_SLOTS = 3
 CACHE_SEQS = 16
-CACHE_AHEAD = 4
-CACHE_FIRST = 1
+CACHE_AHEAD = 2
+CACHE_FIRST = 0
 X_PARTS = 4
 
 

time: 87 us -> 85.9 us (0.987)
  Pallas kernels: 86.1 us -> 84.9 us
    pallas_call x1, Pallas kernels: 29.7 us -> 28.5 us  [project(): pl.pallas_call(project_kernel, out_shape=[jax.ShapeDtypeStruct((rows, num...]
where the time goes in v13:
time: 85.9 us; the launch traced here: 85.5 us
  Pallas kernels  84.9 us (99%)
    pallas_call x1, Pallas kernels, finish(): pl.pallas_call(finish_kernel, out_shape=[jax.ShapeDtypeStruct((num_seqs,...  52.9 us
    pallas_call x1, Pallas kernels, project(): pl.pallas_call(project_kernel, out_shape=[jax.ShapeDtypeStruct((rows, num...  28.5 us
    pallas_call x1, Pallas kernels, last(): pl.pallas_call(last_kernel, out_shape=[jax.ShapeDtypeStruct(a.shape, a.dt...  3.46 us

profile of v13, /device:TPU:0, one launch (start us, length us, event | category | flops | bytes accessed | tf_op | source)
XLA Modules:
  0.0 85.5 jit_solution(18325157842943948937)
XLA Ops:
  0.6 28.5 %project.1 = (f32[20,128,128]{2,1,0:T(8,128)}, bf16[128,256,128]{2,1,0:T(8,128)(2,1)}, bf16[128,256,128]{2,1,0:T(8,128)(2,1)}) custom-call(bf16[128,8192]{1,0:T(8,128)(2,1)} %hid_ref.1, bf16[64,128]{1,0:T(8,128)(2,1)} %bitcast.18, f32[64,128]{1,0:T(8,128)} %bitcast.15, f32[64,128]{1,0:T(8,128)} %bitcast.16, bf16[4,1280]{1,0:T(4,128)(2,1)} %bias_hbm.1, ...), custom_call_target="tpu_custom_call" | custom-call | tf_op jit(solution)/shard_map/project/pallas_call | solution.py:189
  29.2 52.9 %finish.1 = (bf16[128,8192]{1,0:T(8,128)(2,1)}, bf16[2,128,4,128]{3,2,1,0:T(4,128)(2,1)}) custom-call(s32[128]{0:T(128)} %lens_hbm.3, f32[20,128,128]{2,1,0:T(8,128)} %get-tuple-element.8.half_hbm, f32[1,32]{1,0:T(1,128)} %bitcast.19, bf16[128,8192]{1,0:T(8,128)(2,1)} %hid_ref.1, bf16[64,128]{1,0:T(8,128)(2,1)} %bitcast.17, bf16[4096,8192]{1,0:T(8,128)(2,1)} %wo_ref.1, ...), custom_call_target="tpu_custom_call" | custom-call | tf_op jit(solution)/shard_map/finish/pallas_call | solution.py:584
  82.1 3.5 %last.1 = (bf16[128,8192]{1,0:T(8,128)(2,1)}, bf16[128,64,4,128]{3,2,1,0:T(4,128)(2,1)}, bf16[128,64,4,128]{3,2,1,0:T(4,128)(2,1)}) custom-call(s32[128]{0:T(128)} %lens_hbm.3, bf16[128,8192]{1,0:T(8,128)(2,1)} %get-tuple-element.9.y_hbm, bf16[2,128,4,128]{3,2,1,0:T(4,128)(2,1)} %get-tuple-element.10.new_hbm, ...), custom_call_target="tpu_custom_call", output_to_operand_aliasing={{1}: (3, {}), {2}: (4, {})} | custom-call | tf_op jit(solution)/shard_map/last/pallas_call | solution.py:672
